TPU v7x, 256 devices: a whole 4x4x8 slice. The times are simulated.
256 devices in a mesh: row: 32 (over y_hi, z, core), col: 8 (over x, y_lo).
Axes of the slice: x: 4, y: 4 (y_hi: 2, y_lo: 2; y = y_hi * 2 + y_lo), z: 8, core: 2. Of those that a mesh axis runs over, the one named last changes fastest.
Arguments:
- hidden: bfloat16 [32768, 768], P(('row', 'col')), may hold values from -6 to 6
- projection: bfloat16 [768, 512], replicated, may hold values from -0.21875 to 0.21875
- alpha: bfloat16 [32768], P(('row', 'col')), may hold values from -6 to 6
- probe_pairs: bfloat16 [32768, 32], P(('row', 'col')), may hold values from -6 to 6
- amplitude: float32 [1], replicated, may hold values from 0.5 to 2
- length_sq: float32 [1], replicated, may hold values from 512 to 1024
Outputs:
- grad_hidden: bfloat16 [32768, 768], P(('row', 'col'))
- grad_proj: float32 [768, 512], P('row')
All inputs are finite; a program needn't handle non-finite values.
Results may differ from a plain program's by a relative error of at most 0.023.
Values may be sent and summed in bfloat16 or wider, within the bound.
No kernel may reach another device: no remote copies, remote signals or barrier semaphores. Data moves between devices by JAX's collectives and lax.ppermute only.
A program may use at most 64 MiB of HBM per device.

v0:
```python
import math

import jax
import jax.numpy as jnp
from jax import lax
from jax.sharding import PartitionSpec as P


def side_by_side(arrays, axis, dim, along):
    widths = [a.shape[along] for a in arrays]
    both = jnp.concatenate(arrays, axis=along)
    out = lax.all_gather(both, axis, axis=dim, tiled=True)
    return tuple(jnp.split(out, [sum(widths[:k]) for k in range(1, len(widths))], axis=along))


def in_blocks(x, dim, size):
    before, after = (x.shape[:dim], x.shape[dim + 1 :])
    return jnp.moveaxis(x.reshape(*before, size, -1, *after), dim, 0)


def sent_and_summed(x, axis, dim):
    blocks = in_blocks(x, dim, lax.axis_size(axis))
    arrived = lax.all_to_all(blocks, axis, split_axis=0, concat_axis=0, tiled=True)
    return arrived.astype(jnp.float32).sum(axis=0)


def sent_to_all(x, axis):
    size = lax.axis_size(axis)
    return lax.all_to_all(jnp.broadcast_to(x[None], (size, *x.shape)), axis, 0, 0, tiled=True)


def of_everyone(x, axis):
    everything = sent_to_all(x, axis)
    return jnp.sum(everything.astype(jnp.float32), axis=0)


def right_of(factors, probes):
    scale = 1.0 / (4 * probes)
    return jnp.concatenate(
        [
            factors[:, :1] * 0.5,
            factors[:, 1 + probes :] * -scale,
            factors[:, 1 : 1 + probes] * -scale,
        ],
        axis=1,
    )


def squares(feats):
    feat_f = feats.astype(jnp.float32)
    return jnp.sum(feat_f * feat_f, axis=1)


def per_device(hidden, projection, alpha, probe_pairs, amplitude, length_sq):
    feats = jnp.dot(hidden, projection, preferred_element_type=jnp.float32).astype(jnp.bfloat16)
    factors = jnp.concatenate([alpha[:, None], probe_pairs], axis=1)
    probes = probe_pairs.shape[1] // 2
    amp = amplitude[0]
    lsq = length_sq[0]
    width = feats.shape[1]

    def make_fold(rows_feat, rows_fac):
        rows_sq = squares(rows_feat)

        def fold(carry, pieces, start):
            cols_feat, cols_fac = pieces
            count = cols_feat.shape[0]
            size = math.gcd(count, 256)
            steps_feat = cols_feat.reshape(count // size, size, width)
            steps_fac = cols_fac.reshape(count // size, size, cols_fac.shape[1])

            def inner_step(state, blocks):
                block_feat, block_fac = blocks
                moved, rowsum = state
                block_sq = squares(block_feat)
                inner = jnp.dot(rows_feat, block_feat.T, preferred_element_type=jnp.float32)
                dist = rows_sq[:, None] + block_sq[None, :] - 2.0 * inner
                kern = amp * jnp.exp(-0.5 * dist / lsq)
                gmat = jnp.dot(
                    rows_fac, right_of(block_fac, probes).T, preferred_element_type=jnp.float32
                )
                weight = gmat * kern
                rowsum = rowsum + jnp.sum(weight, axis=1)
                moved = moved + jnp.dot(
                    weight.astype(jnp.bfloat16), block_feat, preferred_element_type=jnp.float32
                )
                return ((moved, rowsum), None)

            result, unused = lax.scan(inner_step, carry, (steps_feat, steps_fac))
            return result

        start_carry = (
            jnp.zeros((rows_feat.shape[0], width), jnp.float32),
            jnp.zeros((rows_feat.shape[0],), jnp.float32),
        )
        return (fold, start_carry)

    rows_feat, rows_fac = side_by_side((feats, factors), "col", 0, 1)
    fold, start_carry = make_fold(rows_feat, rows_fac)
    moved, rowsum = fold(
        start_carry,
        (
            lax.all_gather(feats, "row", axis=0, tiled=True),
            lax.all_gather(factors, "row", axis=0, tiled=True),
        ),
        jnp.int32(0),
    )
    moved_own, rowsum_own = (
        lax.psum_scatter(moved, "col", scatter_dimension=0, tiled=True),
        lax.psum_scatter(rowsum, "col", scatter_dimension=0, tiled=True),
    )
    grad_feat = (2.0 / lsq * (moved_own - rowsum_own[:, None] * feats.astype(jnp.float32))).astype(
        jnp.bfloat16
    )
    grad_hidden = jnp.dot(grad_feat, projection.T, preferred_element_type=jnp.float32).astype(
        jnp.bfloat16
    )
    partial_proj = lax.dot_general(
        hidden, grad_feat, (((0,), (0,)), ((), ())), preferred_element_type=jnp.float32
    )
    share = sent_and_summed(partial_proj.astype(jnp.bfloat16), "row", 0)
    grad_proj = of_everyone(share.astype(jnp.bfloat16), "col").astype(jnp.float32)
    return (grad_hidden, grad_proj)


def solution(mesh):
    placed = (P(("row", "col"), None), P(), P(("row", "col")), P(("row", "col"), None), P(), P())
    return jax.shard_map(
        per_device,
        mesh=mesh,
        in_specs=placed,
        out_specs=(P(("row", "col"), None), P("row", None)),
        check_vma=False,
    )
```

profile of v0, /device:TPU:32, one launch (start us, length us, event | category | flops | bytes accessed | tf_op | source)
XLA Modules:
  0.0 353.6 jit_solution(16949946160411979620)
XLA Ops:
  12.4 41.6 %all_gather.9 = bf16[4096,33]{0,1:T(8,128)(2,1)S(1)} all-gather(bf16[128,33]{0,1:T(8,128)(2,1)S(1)} %pad_maximum_fusion.1), channel_id=1, replica_groups=mesh['row'=32,'col'=8] {'row'}, dimensions={0}, use_global_device_ids=true | all-gather | bytes 278784 | tf_op jit(solution)/shard_map/all_gather | solution.py:104
  59.1 86.4 %all-gather.5.cloned.1.call-done = bf16[4096,512]{1,0:T(8,128)(2,1)} async-done(((bf16[128,512]{1,0:T(8,128)(2,1)}), bf16[4096,512]{1,0:T(8,128)(2,1)}) %all-gather.5.cloned.1.call-update) | async-done | bytes 4194320 | tf_op jit(solution)/shard_map/all_gather | solution.py:103
  145.5 100.2 %while.13 = (s32[]{:T(128)}, f32[1024,512]{1,0:T(8,128)S(1)}, f32[1024]{0:T(1024)S(1)}, bf16[16,256,33]{1,2,0:T(8,128)(2,1)S(1)}, bf16[1024,33]{1,0:T(8,128)(2,1...) while((s32[]{:T(128)}, f32[1024,512]{1,0:T(8,128)S(1)}, ...), condition=%wide.region_4.5_spmd.clone, body=%wide.region_1.4_spmd.clone.sunk | while | flops 558033408 | bytes 9350808 | solution.py:89
  146.7 3.1 fusion.43
  152.9 3.1 fusion.43
  159.2 3.1 fusion.43
  165.4 3.1 fusion.43
  171.7 3.1 fusion.43
  178.0 3.1 fusion.43
  184.2 3.1 fusion.43
  190.5 3.1 fusion.43
  196.8 3.1 fusion.43
  203.0 3.1 fusion.43
  209.3 3.1 fusion.43
  215.6 3.1 fusion.43
  221.8 3.1 fusion.43
  228.1 3.1 fusion.43
  234.4 3.1 fusion.43
  240.6 3.1 fusion.43
  249.1 20.5 %all-reduce = f32[1024]{0:T(1024)S(1)} all-reduce(f32[1024]{0:T(1024)S(1)} %get-tuple-element.56), channel_id=3, replica_groups=mesh['row'=32,'col'=8] {'col'}, use_global_device_ids=true, to_apply=%region_6.7.clone | all-reduce | flops 1024 | bytes 8192
  269.6 29.3 %reduce-scatter.2.cloned.1.call-done = f32[128,512]{1,0:T(8,128)} async-done(((f32[1024,512]{1,0:T(8,128)}), f32[128,512]{1,0:T(8,128)}) %reduce-scatter.2.cloned.1.call-update) | async-done | bytes 262160 | tf_op jit(solution)/shard_map/reduce_scatter | solution.py:109
  300.7 33.8 %all_to_all.10 = bf16[32,24,512]{2,1,0:T(8,128)(2,1)S(1)} all-to-all(bf16[32,24,512]{2,1,0:T(8,128)(2,1)S(1)} %bitcast.64), channel_id=1, replica_groups=mesh['row'=32,'col'=8] {'row'}, dimensions={0} | all-to-all | bytes 1572864 | tf_op jit(solution)/shard_map/all_to_all | solution.py:23
  335.3 4.4 %all-to-all-start.1 = ((bf16[8,24,512]{2,1,0:T(8,128)(2,1)}), bf16[8,24,512]{2,1,0:T(8,128)(2,1)S(1)}, u32[]{:S(2)}, u32[]{:S(2)}) async-start(bf16[8,24,512]{2,1,0:T(8,128)(2,1)} %broadcast_in_dim.21), calls=%async_computation.2 | async-start | bytes 393216 | tf_op jit(solution)/shard_map/all_to_all | solution.py:29
  340.8 5.6 %all-to-all-done.1 = bf16[8,24,512]{2,1,0:T(8,128)(2,1)S(1)} async-done(((bf16[8,24,512]{2,1,0:T(8,128)(2,1)}), bf16[8,24,512]{2,1,0:T(8,128)(2,1)S(1)}, u32[]{:S(2)}, u32[]{:S(2)}) %all-to-all-start.1) | async-done | bytes 196640 | tf_op jit(solution)/shard_map/all_to_all | solution.py:29
  (156 shorter events, 65.2 us)
Async XLA Ops:
  7.2 1.7 copy-start
  7.2 49.2 %all-gather.3.cloned.1.call-start = ((), (), s32[]{:S(2)}) async-start(), calls=%async_computation.3 | async-start | bytes 1474560 | tf_op jit(solution)/shard_map/all_gather | solution.py:12
  10.1 0.8 copy-start.3
  10.9 134.6 %all-gather.5.cloned.1.call-start = ((), (), s32[]{:S(2)}) async-start(), calls=%async_computation.4 | async-start | bytes 4325376 | tf_op jit(solution)/shard_map/all_gather | solution.py:103
  11.6 287.3 %reduce-scatter.2.cloned.1.call-start = ((), (), s32[]{:S(2)}) async-start(), calls=%async_computation.5 | async-start | bytes 2359296 | tf_op jit(solution)/shard_map/reduce_scatter | solution.py:109
  56.4 2.4 copy-start.2
  56.4 89.1 %slice-start = ((bf16[1024,545]{1,0:T(8,128)(2,1)}), bf16[1024,33]{1,0:T(8,128)(2,1)S(1)}, s32[]{:S(2)}) async-start(bf16[1024,545]{1,0:T(8,128)(2,1)} %all-gather.3.cloned.1.call-done), calls=%async_computation.6 | async-start | bytes 524288 | tf_op jit(solution)/shard_map/split | solution.py:13
  245.8 1.3 copy-start.1
  245.8 2.0 copy-start.6
  245.8 53.1 %copy-start.4 = (bf16[128,512]{1,0:T(8,128)(2,1)S(1)}, bf16[128,512]{1,0:T(8,128)(2,1)}, u32[]{:S(2)}) copy-start(bf16[128,512]{1,0:T(8,128)(2,1)} %copy-done.3) | copy-start | bytes 393220
  245.8 54.2 %copy-start.5 = (bf16[128,768]{1,0:T(8,128)(2,1)S(1)}, bf16[128,768]{1,0:T(8,128)(2,1)}, u32[]{:S(2)}) copy-start(bf16[128,768]{1,0:T(8,128)(2,1)} %param.8) | copy-start | bytes 589828
  335.3 11.1 %all-to-all-start.1 = ((bf16[8,24,512]{2,1,0:T(8,128)(2,1)}), bf16[8,24,512]{2,1,0:T(8,128)(2,1)S(1)}, u32[]{:S(2)}, u32[]{:S(2)}) async-start(bf16[8,24,512]{2,1,0:T(8,128)(2,1)} %broadcast_in_dim.21), calls=%async_computation.2 | async-start | bytes 393216 | tf_op jit(solution)/shard_map/all_to_all | solution.py:29
Sparse Core Ops, SparseCore 0:
  11.0 45.3 all-gather.2
  59.2 86.2 all-gather.4
  247.2 51.6 reduce-scatter.1
where the time goes:
time: 356 us; the launch traced here: 354 us
  waiting for transfers between devices  124 us (35%)
  blocking collectives  95.9 us (27%)
  matrix products  83.9 us (24%)
  other arithmetic  21.2 us (6%)
  between operations  15.2 us (4%)
  local copies, waits for them, and re-layouts  7.39 us (2%)
  starting transfers between devices  4.54 us (1%)
    all_gather x1, waiting for transfers between devices, per_device(): lax.all_gather(feats, 'row', axis=0, tiled=True)  86.4 us
    dot_general x16, matrix products, inner_step(): inner = jnp.dot(rows_feat, block_feat.T, preferred_element_type=jnp.float32)  50.4 us
    all_gather x1, blocking collectives, per_device(): lax.all_gather(factors, 'row', axis=0, tiled=True)  41.6 us
    all_to_all x1, blocking collectives, sent_and_summed(): lax.all_to_all(blocks, axis, split_axis=0, concat_axis=0, tiled=True)  33.8 us
    reduce_scatter x1, waiting for transfers between devices, per_device(): lax.psum_scatter(moved, 'col', scatter_dimension=0, tiled=True)  29.3 us
    dot_general x16, matrix products, inner_step(): jnp.dot(weight.astype(jnp.bfloat16), block_feat, preferred_element_type=j...  25.4 us
    unnamed x1, blocking collectives  20.5 us
    reduce_sum x17, other arithmetic, squares(): return jnp.sum(feat_f * feat_f, axis=1)  17.6 us
  transfers between devices with their start and end apart: 4, of which 4 were waited for; matrix products, arithmetic and copies ran while one was open for 1% of the time, Pallas kernels for 0%

commit v1 on v0

v1 whole, which is shorter than its diff:
```python
import functools

import jax
import jax.numpy as jnp
from jax import lax
from jax.experimental import pallas as pl
from jax.experimental.pallas import tpu as pltpu
from jax.sharding import Mesh, PartitionSpec as P

LOG2E = 1.4426950408889634
PTS = 128
FEAT = 512
MSG = 560
ROW_CHUNK = 256
COL_CHUNK = 1024
ALL = ("yh", "z", "c", "x", "yl")
VMEM = pl.BlockSpec(memory_space=pltpu.VMEM)
SMEM = pl.BlockSpec(memory_space=pltpu.SMEM)


def pair_kernel(n, amp_ref, lsq_ref, rows_ref, *refs):
    cols_refs = refs[:n]
    out_ref, rf, la, ai, cf, cfac, acc, rs = refs[n:]
    nb = rows_ref.shape[0]
    rows = nb * PTS
    chunk = COL_CHUNK
    c1 = LOG2E / lsq_ref[0]
    half = 0.5 * c1
    lane = lax.broadcasted_iota(jnp.int32, (PTS, 128), 1)
    for b in range(nb):
        here = slice(b * PTS, (b + 1) * PTS)
        for k in range(4):
            rf[here, k * 128 : (k + 1) * 128] = rows_ref[b, k * 128 : (k + 1) * 128, :]
        fac = rows_ref[b, FEAT:MSG, :].astype(jnp.float32)
        sq = fac[33:34] + fac[34:35] + fac[35:36]
        swapped = jnp.concatenate(
            [
                fac[0:1] * 0.5,
                fac[17:33] * (-1 / 64),
                fac[1:17] * (-1 / 64),
                sq * half,
                jnp.zeros((94, 128), jnp.float32),
            ],
            axis=0,
        ).T
        ai[here, :] = jnp.broadcast_to(swapped[:, 33:34], (PTS, 128))
        la[here, :] = jnp.where(lane < 33, swapped, 0.0).astype(jnp.bfloat16)
    at = 0
    for ref in cols_refs:
        for b in range(ref.shape[0] // MSG):
            for k in range(4):
                cf[at : at + PTS, k * 128 : (k + 1) * 128] = ref[
                    b * MSG + k * 128 : b * MSG + (k + 1) * 128, :
                ]
            j, o = divmod(at, chunk)
            cfac[j, 0:48, o : o + PTS] = ref[b * MSG + FEAT : (b + 1) * MSG, :]
            at += PTS
    acc[...] = jnp.zeros_like(acc)
    rs[...] = jnp.zeros_like(rs)
    cfac[:, 48:, :] = jnp.zeros((at // chunk, 80, chunk), jnp.bfloat16)
    log_amp = jnp.log2(jnp.full((1, chunk), amp_ref[0], jnp.float32))

    def step(j, carry):
        colf = cf[pl.ds(pl.multiple_of(j * chunk, chunk), chunk), :]
        fac = cfac[j]
        f3 = fac[32:40].astype(jnp.float32)
        bj = (f3[1:2] + f3[2:3] + f3[3:4]) * half - log_amp
        for r in range(rows // ROW_CHUNK):
            here = slice(r * ROW_CHUNK, (r + 1) * ROW_CHUNK)
            inner = lax.dot_general(
                rf[here, :], colf, (((1,), (1,)), ((), ())), preferred_element_type=jnp.float32
            )
            gmat = jnp.dot(la[here, :], fac, preferred_element_type=jnp.float32)
            a = jnp.concatenate([ai[here, :]] * (chunk // 128), axis=1)
            w = gmat * jnp.exp2(inner * c1 - a - bj)
            total = w[:, 0:128]
            for q in range(1, chunk // 128):
                total = total + w[:, q * 128 : (q + 1) * 128]
            rs[here, :] += total
            acc[here, :] += jnp.dot(
                w.astype(jnp.bfloat16), colf, preferred_element_type=jnp.float32
            )
        return carry

    lax.fori_loop(0, at // chunk, step, 0)
    scale = 2.0 / lsq_ref[0]
    for r in range(nb):
        here = slice(r * PTS, (r + 1) * PTS)
        rowsum = jnp.sum(rs[here, :], axis=1, keepdims=True)
        out_ref[r] = (scale * (acc[here, :] - rowsum * rf[here, :].astype(jnp.float32))).astype(
            jnp.bfloat16
        )


def pair(rows, cols, amp, lsq):
    nb = rows.shape[0]
    r = nb * PTS
    c = sum(x.shape[0] for x in cols) // MSG * PTS
    return pl.pallas_call(
        functools.partial(pair_kernel, len(cols)),
        out_shape=jax.ShapeDtypeStruct((nb, PTS, FEAT), jnp.bfloat16),
        in_specs=[SMEM, SMEM, VMEM] + [VMEM] * len(cols),
        out_specs=VMEM,
        scratch_shapes=[
            pltpu.VMEM((r, FEAT), jnp.bfloat16),
            pltpu.VMEM((r, 128), jnp.bfloat16),
            pltpu.VMEM((r, 128), jnp.float32),
            pltpu.VMEM((c, FEAT), jnp.bfloat16),
            pltpu.VMEM((c // COL_CHUNK, 128, COL_CHUNK), jnp.bfloat16),
            pltpu.VMEM((r, FEAT), jnp.float32),
            pltpu.VMEM((r, 128), jnp.float32),
        ],
        cost_estimate=pl.CostEstimate(
            flops=2 * r * c * 1280, bytes_accessed=4 * r * FEAT, transcendentals=r * c
        ),
        compiler_params=pltpu.CompilerParams(vmem_limit_bytes=48 * 1024 * 1024),
        name="pair",
    )(amp, lsq, rows, *cols)


def message_kernel(hidden_ref, proj_ref, alpha_ref, probes_ref, out_ref):
    feats = jnp.dot(hidden_ref[...], proj_ref[...], preferred_element_type=jnp.float32).astype(
        jnp.bfloat16
    )
    feat_f = feats.astype(jnp.float32)
    for k in range(4):
        out_ref[k * 128 : (k + 1) * 128, :] = feats[:, k * 128 : (k + 1) * 128]
    sq = jnp.sum(feat_f * feat_f, axis=1, keepdims=True)
    hi = sq.astype(jnp.bfloat16).astype(jnp.float32)
    mid = (sq - hi).astype(jnp.bfloat16).astype(jnp.float32)
    low = sq - hi - mid
    probes = probes_ref[...].astype(jnp.float32)
    wide = jnp.concatenate([probes, hi, mid, low, jnp.zeros((PTS, 93), jnp.float32)], axis=1).T
    fac = jnp.concatenate([alpha_ref[...].astype(jnp.float32), wide[0:47]], axis=0)
    out_ref[FEAT:MSG, :] = fac.astype(jnp.bfloat16)


def message(hidden, projection, alpha, probe_pairs):
    return pl.pallas_call(
        message_kernel,
        out_shape=jax.ShapeDtypeStruct((MSG, 128), jnp.bfloat16),
        in_specs=[VMEM] * 4,
        out_specs=VMEM,
        name="message",
    )(hidden, projection, alpha.reshape(1, PTS), probe_pairs)


def sent_to_all(x, axes, size):
    return lax.all_to_all(jnp.broadcast_to(x[None], (size, *x.shape)), axes, 0, 0, tiled=True)


def shifted(x, axis, by):
    n = lax.axis_size(axis)
    return lax.ppermute(x, axis, [(i, (i + by) % n) for i in range(n)])


def per_device(hidden, projection, alpha, probe_pairs, amplitude, length_sq):
    msg = message(hidden, projection, alpha, probe_pairs)
    rows = sent_to_all(msg, ("x", "yl"), 8)
    both = jnp.concatenate([msg, shifted(msg, "yh", 1)], axis=0)
    held = [both]
    up, down = both, both
    for k in range(4):
        up = shifted(up, "z", 1)
        held.append(up)
        if k < 3:
            down = shifted(down, "z", -1)
            held.append(down)
    cols = held + [shifted(x, "c", 1) for x in held]
    part = pair(rows, cols, amplitude, length_sq)
    arrived = lax.all_to_all(part, ("x", "yl"), 0, 0, tiled=True)
    grad_feat = arrived.astype(jnp.float32).sum(axis=0).astype(jnp.bfloat16)
    grad_hidden = jnp.dot(grad_feat, projection.T, preferred_element_type=jnp.float32).astype(
        jnp.bfloat16
    )
    partial = lax.dot_general(
        hidden, grad_feat, (((0,), (0,)), ((), ())), preferred_element_type=jnp.float32
    ).astype(jnp.bfloat16)
    blocks = partial.reshape(2, 8, 2, 24, FEAT).transpose(2, 1, 0, 3, 4)
    got = lax.all_to_all(blocks, "c", 0, 0, tiled=True)
    core_sum = got.astype(jnp.float32).sum(axis=0).astype(jnp.bfloat16)
    got = lax.all_to_all(core_sum, "z", 0, 0, tiled=True)
    z_sum = got.astype(jnp.float32).sum(axis=0).astype(jnp.bfloat16)
    spread = jnp.broadcast_to(z_sum[:, None], (2, 8, 24, FEAT)).reshape(16, 24, FEAT)
    got = lax.all_to_all(spread, ("yh", "x", "yl"), 0, 0, tiled=True)
    grad_proj = got.astype(jnp.float32).sum(axis=0)
    return grad_hidden, grad_proj


def solution(mesh):
    fine = Mesh(mesh.devices.reshape(2, 8, 2, 4, 2), ALL)
    placed = (P(ALL, None), P(), P(ALL), P(ALL, None), P(), P())
    return jax.shard_map(
        per_device,
        mesh=fine,
        in_specs=placed,
        out_specs=(P(ALL, None), P(("yh", "z", "c"), None)),
        check_vma=False,
    )
```

time: 356 us -> 131 us (0.37)
  waiting for transfers between devices: 124 us -> 29.1 us
  matrix products: 83.9 us -> 1.44 us
  blocking collectives: 95.9 us -> 47.9 us
  starting transfers between devices: 4.54 us -> 24.8 us
  other arithmetic: 21.2 us -> 1.96 us
  Pallas kernels: 0 us -> 17.9 us
  between operations: 15.2 us -> 2.08 us
    all_gather x2 -> x0, waiting for transfers between devices: 88.6 us -> none  [the longest x1 86.4 us: per_device(): lax.all_gather(feats, 'row', axis=0, tiled=True)]
    dot_general x49 -> x0, matrix products: 82.5 us -> none  [the longest x16 50.4 us: inner_step(): inner = jnp.dot(rows_feat, block_feat.T, preferred_element_type=jnp.float32)]
    all_gather x1 -> x0, blocking collectives: 41.6 us -> none  [per_device(): lax.all_gather(factors, 'row', axis=0, tiled=True)]
    reduce_scatter x1 -> x0, waiting for transfers between devices: 29.3 us -> none  [per_device(): lax.psum_scatter(moved, 'col', scatter_dimension=0, tiled=True)]
    ppermute x0 -> x16, waiting for transfers between devices: none -> 21.1 us  [shifted(): return lax.ppermute(x, axis, [(i, (i + by) % n) for i in range(n)])]
    unnamed x1 -> x0, blocking collectives: 20.5 us -> none
    pallas_call x0 -> x2, Pallas kernels: none -> 17.9 us  [the longest x1 15.6 us: pair(): pl.pallas_call(functools.partial(pair_kernel, len(cols)), out_shape=jax.S...]
    reduce_sum x19 -> x4, other arithmetic: 18.4 us -> 1.04 us  [the longest x1 0.68 us: per_device(): grad_proj = got.astype(jnp.float32).sum(axis=0)]
  transfers between devices with their start and end apart: 4 -> 18, of which waited for: 4 -> 8; matrix products, arithmetic and copies ran while one was open for 1% -> 2% of each run, Pallas kernels for 0% -> 0%
where the time goes in v1:
time: 131 us; the launch traced here: 130 us
  blocking collectives  47.9 us (37%)
  waiting for transfers between devices  29.1 us (22%)
  starting transfers between devices  24.8 us (19%)
  Pallas kernels  17.9 us (14%)
  local copies, waits for them, and re-layouts  4.64 us (4%)
  between operations  2.08 us (2%)
  other arithmetic  1.96 us (1%)
  matrix products  1.44 us (1%)
    all_to_all x1, blocking collectives, per_device(): got = lax.all_to_all(core_sum, 'z', 0, 0, tiled=True)  22.3 us
    all_to_all x1, blocking collectives, per_device(): arrived = lax.all_to_all(part, ('x', 'yl'), 0, 0, tiled=True)  21.2 us
    ppermute x16, waiting for transfers between devices, shifted(): return lax.ppermute(x, axis, [(i, (i + by) % n) for i in range(n)])  21.1 us
    pallas_call x1, Pallas kernels, pair(): pl.pallas_call(functools.partial(pair_kernel, len(cols)), out_shape=jax.S...  15.6 us
    ppermute x16, starting transfers between devices, shifted(): return lax.ppermute(x, axis, [(i, (i + by) % n) for i in range(n)])  14.3 us
    all_to_all x1, waiting for transfers between devices, per_device(): got = lax.all_to_all(spread, ('yh', 'x', 'yl'), 0, 0, tiled=True)  8.06 us
    all_to_all x1, starting transfers between devices, sent_to_all(): lax.all_to_all(jnp.broadcast_to(x[None], (size, *x.shape)), axes, 0, 0, t...  5.31 us
    all_to_all x1, starting transfers between devices, per_device(): got = lax.all_to_all(spread, ('yh', 'x', 'yl'), 0, 0, tiled=True)  5.19 us
  transfers between devices with their start and end apart: 18, of which 8 were waited for; matrix products, arithmetic and copies ran while one was open for 2% of the time, Pallas kernels for 0%

profile of v1, /device:TPU:32, one launch (start us, length us, event | category | flops | bytes accessed | tf_op | source)
XLA Modules:
  0.0 129.8 jit_solution(15554632461214972757)
XLA Ops:
  0.6 1.4 %copy.20.probes_ref = bf16[128,32]{1,0:T(8,128)(2,1)} copy(bf16[128,32]{0,1:T(8,128)(2,1)} %param.9) | data formatting | bytes 16384 | tf_op args[3]
  2.0 2.3 %message.1 = bf16[560,128]{1,0:T(8,128)(2,1)} custom-call(bf16[128,768]{1,0:T(8,128)(2,1)} %hidden_ref.1, bf16[768,512]{1,0:T(8,128)(2,1)} %proj_ref.1, bf16[1,128]{1,0:T(2,128)(2,1)} %bitcast.12, bf16[128,32]{1,0:T(8,128)(2,1)} %copy.20.probes_ref), custom_call_target="tpu_custom_call" | custom-call | tf_op jit(solution)/shard_map/message/pallas_call | solution.py:139
  4.3 3.2 %collective-permute-start = (bf16[560,128]{1,0:T(8,128)(2,1)}, bf16[560,128]{1,0:T(8,128)(2,1)S(1)}, u32[]{:S(2)}, u32[]{:S(2)}) collective-permute-start(bf16[560,128]{1,0:T(8,128)(2,1)} %message.1), channel_id=1, source_target_pairs={{0,128},{128,0},{1,129},{129,1},{2,130},{130,2},{3,131},{131,3},{4... | collective-permute-start | bytes 430088 | tf_op jit(solution)/shard_map/ppermute | solution.py:154
  7.5 4.0 %collective-permute-done = bf16[560,128]{1,0:T(8,128)(2,1)S(1)} collective-permute-done((bf16[560,128]{1,0:T(8,128)(2,1)}, bf16[560,128]{1,0:T(8,128)(2,1)S(1)}, u32[]{:S(2)}, u32[]{:S(2)}) %collective-permute-start) | collective-permute-done | bytes 143392 | tf_op jit(solution)/shard_map/ppermute | solution.py:154
  11.5 0.9 pad_maximum_fusion.refs_0_
  12.5 2.0 %collective-permute-start.1 = (bf16[1120,128]{1,0:T(8,128)(2,1)S(1)}, bf16[1120,128]{1,0:T(8,128)(2,1)S(1)}, u32[]{:S(2)}, u32[]{:S(2)}) collective-permute-start(bf16[1120,128]{1,0:T(8,128)(2,1)S(1)} %pad_maximum_fusion.refs_0_), channel_id=1, source_target_pairs={{0,16},{16,32},{32,48},{48,64},{64,80},{80,96},{96,112},{112,0},{1... | collective-permute-start | bytes 860168 | tf_op jit(solution)/shard_map/ppermute | solution.py:154
  14.6 5.7 %collective-permute-done.1.refs_1_ = bf16[1120,128]{1,0:T(8,128)(2,1)S(1)} collective-permute-done((bf16[1120,128]{1,0:T(8,128)(2,1)S(1)}, bf16[1120,128]{1,0:T(8,128)(2,1)S(1)}, u32[]{:S(2)}, u32[]{:S(2)}) %collective-permute-start.1) | collective-permute-done | bytes 286752 | tf_op jit(solution)/shard_map/ppermute | solution.py:154
  20.2 1.9 %collective-permute-start.3 = (bf16[1120,128]{1,0:T(8,128)(2,1)S(1)}, bf16[1120,128]{1,0:T(8,128)(2,1)S(1)}, u32[]{:S(2)}, u32[]{:S(2)}) collective-permute-start(bf16[1120,128]{1,0:T(8,128)(2,1)S(1)} %collective-permute-done.1.refs_1_), channel_id=1, source_target_pairs={{0,16},{16,32},{32,48},{48,64},{64,80},{80,96},{96,112},{112,0},{1... | collective-permute-start | bytes 860168 | tf_op jit(solution)/shard_map/ppermute | solution.py:154
  22.2 2.1 %broadcast_in_dim.4 = bf16[8,560,128]{2,1,0:T(8,128)(2,1)} broadcast(bf16[560,128]{1,0:T(8,128)(2,1)} %message.1), dimensions={1,2} | broadcast | bytes 1290240 | tf_op jit(solution)/shard_map/broadcast_in_dim | solution.py:149
  24.2 5.3 %all-to-all-start = ((bf16[8,560,128]{2,1,0:T(8,128)(2,1)}), bf16[8,560,128]{2,1,0:T(8,128)(2,1)}, u32[]{:S(2)}, u32[]{:S(2)}) async-start(bf16[8,560,128]{2,1,0:T(8,128)(2,1)} %broadcast_in_dim.4), calls=%async_computation | async-start | bytes 2293760 | tf_op jit(solution)/shard_map/all_to_all | solution.py:149
  29.5 2.4 %collective-permute-start.4 = (bf16[1120,128]{1,0:T(8,128)(2,1)S(1)}, bf16[1120,128]{1,0:T(8,128)(2,1)S(1)}, u32[]{:S(2)}, u32[]{:S(2)}) collective-permute-start(bf16[1120,128]{1,0:T(8,128)(2,1)S(1)} %collective-permute-done.2.refs_2_), channel_id=1, source_target_pairs={{0,112},{16,0},{32,16},{48,32},{64,48},{80,64},{96,80},{112,96},{1... | collective-permute-start | bytes 860168 | tf_op jit(solution)/shard_map/ppermute | solution.py:154
  32.8 4.0 %collective-permute-done.4.refs_4_ = bf16[1120,128]{1,0:T(8,128)(2,1)S(1)} collective-permute-done((bf16[1120,128]{1,0:T(8,128)(2,1)S(1)}, bf16[1120,128]{1,0:T(8,128)(2,1)S(1)}, u32[]{:S(2)}, u32[]{:S(2)}) %collective-permute-start.4) | collective-permute-done | bytes 286752 | tf_op jit(solution)/shard_map/ppermute | solution.py:154
  36.8 2.5 %collective-permute-start.6 = (bf16[1120,128]{1,0:T(8,128)(2,1)S(1)}, bf16[1120,128]{1,0:T(8,128)(2,1)S(1)}, u32[]{:S(2)}, u32[]{:S(2)}) collective-permute-start(bf16[1120,128]{1,0:T(8,128)(2,1)S(1)} %collective-permute-done.4.refs_4_), channel_id=1, source_target_pairs={{0,112},{16,0},{32,16},{48,32},{64,48},{80,64},{96,80},{112,96},{1... | collective-permute-start | bytes 860168 | tf_op jit(solution)/shard_map/ppermute | solution.py:154
  39.8 0.7 collective-permute-start.7
  41.1 4.0 %collective-permute-done.6.refs_6_ = bf16[1120,128]{1,0:T(8,128)(2,1)S(1)} collective-permute-done((bf16[1120,128]{1,0:T(8,128)(2,1)S(1)}, bf16[1120,128]{1,0:T(8,128)(2,1)S(1)}, u32[]{:S(2)}, u32[]{:S(2)}) %collective-permute-start.6) | collective-permute-done | bytes 286752 | tf_op jit(solution)/shard_map/ppermute | solution.py:154
  45.1 2.5 %collective-permute-done.7.refs_7_ = bf16[1120,128]{1,0:T(8,128)(2,1)S(1)} collective-permute-done((bf16[1120,128]{1,0:T(8,128)(2,1)S(1)}, bf16[1120,128]{1,0:T(8,128)(2,1)S(1)}, u32[]{:S(2)}, u32[]{:S(2)}) %collective-permute-start.7) | collective-permute-done | bytes 286752 | tf_op jit(solution)/shard_map/ppermute | solution.py:154
  49.3 15.6 %pair.1 = bf16[8,128,512]{2,1,0:T(8,128)(2,1)S(1)} custom-call(f32[1]{0:T(128)S(6)} %copy.26.amp_ref, f32[1]{0:T(128)S(6)} %copy.27.lsq_ref, bf16[8,560,128]{2,1,0:T(8,128)(2,1)} %all-to-all-done.rows_ref, bf16[1120,128]{1,0:T(8,128)(2,1)S(1)} %pad_maximum_fusion.refs_0_, bf16[1120,128]{1,0:T(8,128)(2,1)S(1)} %collective-permute-done.1.refs_1_, ...), custom_call_target="tpu_custom_call" | custom-call | flops 10737418240 | bytes 2097152 | tf_op jit(solution)/shard_map/pair/pallas_call | solution.py:99
  65.0 21.2 %all_to_all.25 = bf16[8,128,512]{2,1,0:T(8,128)(2,1)S(1)} all-to-all(bf16[8,128,512]{2,1,0:T(8,128)(2,1)S(1)} %pair.1), channel_id=1, replica_groups=mesh['yh'=2,'z'=8,'c'=2,'x'=4,'yl'=2] {'x','yl'}, dimensions={0} | all-to-all | bytes 2097152 | tf_op jit(solution)/shard_map/all_to_all | solution.py:171
  87.1 4.4 %all_to_all.26 = bf16[2,8,2,24,512]{4,3,1,2,0:T(8,128)(2,1)S(1)} all-to-all(bf16[2,8,2,24,512]{4,3,1,2,0:T(8,128)(2,1)S(1)} %copy.22), channel_id=1, replica_groups=mesh['yh'=2,'z'=8,'c'=2,'x'=4,'yl'=2] {'c'}, dimensions={0} | all-to-all | bytes 1572864 | tf_op jit(solution)/shard_map/all_to_all | solution.py:180
  91.7 22.3 %all_to_all.27 = bf16[8,2,24,512]{3,2,1,0:T(8,128)(2,1)S(1)} all-to-all(bf16[8,2,24,512]{3,2,1,0:T(8,128)(2,1)S(1)} %copy.24), channel_id=1, replica_groups=mesh['yh'=2,'z'=8,'c'=2,'x'=4,'yl'=2] {'z'}, dimensions={0} | all-to-all | bytes 786432 | tf_op jit(solution)/shard_map/all_to_all | solution.py:182
  114.1 0.8 broadcast_in_dim.5
  114.8 5.2 %all-to-all-start.4 = ((bf16[16,24,512]{2,1,0:T(8,128)(2,1)}), bf16[16,24,512]{2,1,0:T(8,128)(2,1)S(1)}, u32[]{:S(2)}, u32[]{:S(2)}) async-start(bf16[16,24,512]{2,1,0:T(8,128)(2,1)} %bitcast.4), calls=%async_computation.4 | async-start | bytes 786432 | tf_op jit(solution)/shard_map/all_to_all | solution.py:185
  120.0 1.1 convolution_convert_fusion.1
  121.1 8.1 %all-to-all-done.4 = bf16[16,24,512]{2,1,0:T(8,128)(2,1)S(1)} async-done(((bf16[16,24,512]{2,1,0:T(8,128)(2,1)}), bf16[16,24,512]{2,1,0:T(8,128)(2,1)S(1)}, u32[]{:S(2)}, u32[]{:S(2)}) %all-to-all-start.4) | async-done | bytes 393248 | tf_op jit(solution)/shard_map/all_to_all | solution.py:185
  (34 shorter events, 4.2 us)
Async XLA Ops:
  4.3 7.2 %collective-permute-start = (bf16[560,128]{1,0:T(8,128)(2,1)}, bf16[560,128]{1,0:T(8,128)(2,1)S(1)}, u32[]{:S(2)}, u32[]{:S(2)}) collective-permute-start(bf16[560,128]{1,0:T(8,128)(2,1)} %message.1), channel_id=1, source_target_pairs={{0,128},{128,0},{1,129},{129,1},{2,130},{130,2},{3,131},{131,3},{4... | collective-permute-start | bytes 430088 | tf_op jit(solution)/shard_map/ppermute | solution.py:154
  12.5 7.8 %collective-permute-start.1 = (bf16[1120,128]{1,0:T(8,128)(2,1)S(1)}, bf16[1120,128]{1,0:T(8,128)(2,1)S(1)}, u32[]{:S(2)}, u32[]{:S(2)}) collective-permute-start(bf16[1120,128]{1,0:T(8,128)(2,1)S(1)} %pad_maximum_fusion.refs_0_), channel_id=1, source_target_pairs={{0,16},{16,32},{32,48},{48,64},{64,80},{80,96},{96,112},{112,0},{1... | collective-permute-start | bytes 860168 | tf_op jit(solution)/shard_map/ppermute | solution.py:154
  14.4 15.1 %collective-permute-start.2 = (bf16[1120,128]{1,0:T(8,128)(2,1)S(1)}, bf16[1120,128]{1,0:T(8,128)(2,1)S(1)}, u32[]{:S(2)}, u32[]{:S(2)}) collective-permute-start(bf16[1120,128]{1,0:T(8,128)(2,1)S(1)} %pad_maximum_fusion.refs_0_), channel_id=1, source_target_pairs={{0,112},{16,0},{32,16},{48,32},{64,48},{80,64},{96,80},{112,96},{1... | collective-permute-start | bytes 860168 | tf_op jit(solution)/shard_map/ppermute | solution.py:154
  20.2 11.7 %collective-permute-start.3 = (bf16[1120,128]{1,0:T(8,128)(2,1)S(1)}, bf16[1120,128]{1,0:T(8,128)(2,1)S(1)}, u32[]{:S(2)}, u32[]{:S(2)}) collective-permute-start(bf16[1120,128]{1,0:T(8,128)(2,1)S(1)} %collective-permute-done.1.refs_1_), channel_id=1, source_target_pairs={{0,16},{16,32},{32,48},{48,64},{64,80},{80,96},{96,112},{112,0},{1... | collective-permute-start | bytes 860168 | tf_op jit(solution)/shard_map/ppermute | solution.py:154
  24.2 24.7 %all-to-all-start = ((bf16[8,560,128]{2,1,0:T(8,128)(2,1)}), bf16[8,560,128]{2,1,0:T(8,128)(2,1)}, u32[]{:S(2)}, u32[]{:S(2)}) async-start(bf16[8,560,128]{2,1,0:T(8,128)(2,1)} %broadcast_in_dim.4), calls=%async_computation | async-start | bytes 2293760 | tf_op jit(solution)/shard_map/all_to_all | solution.py:149
  29.5 7.3 %collective-permute-start.4 = (bf16[1120,128]{1,0:T(8,128)(2,1)S(1)}, bf16[1120,128]{1,0:T(8,128)(2,1)S(1)}, u32[]{:S(2)}, u32[]{:S(2)}) collective-permute-start(bf16[1120,128]{1,0:T(8,128)(2,1)S(1)} %collective-permute-done.2.refs_2_), channel_id=1, source_target_pairs={{0,112},{16,0},{32,16},{48,32},{64,48},{80,64},{96,80},{112,96},{1... | collective-permute-start | bytes 860168 | tf_op jit(solution)/shard_map/ppermute | solution.py:154
  31.9 7.8 %collective-permute-start.5 = (bf16[1120,128]{1,0:T(8,128)(2,1)S(1)}, bf16[1120,128]{1,0:T(8,128)(2,1)S(1)}, u32[]{:S(2)}, u32[]{:S(2)}) collective-permute-start(bf16[1120,128]{1,0:T(8,128)(2,1)S(1)} %collective-permute-done.3.refs_3_), channel_id=1, source_target_pairs={{0,16},{16,32},{32,48},{48,64},{64,80},{80,96},{96,112},{112,0},{1... | collective-permute-start | bytes 860168 | tf_op jit(solution)/shard_map/ppermute | solution.py:154
  32.3 8.2 %collective-permute-start.8 = (bf16[1120,128]{1,0:T(8,128)(2,1)S(1)}, bf16[1120,128]{1,0:T(8,128)(2,1)S(1)}, u32[]{:S(2)}, u32[]{:S(2)}) collective-permute-start(bf16[1120,128]{1,0:T(8,128)(2,1)S(1)} %pad_maximum_fusion.refs_0_), channel_id=1, source_target_pairs={{0,8},{8,0},{1,9},{9,1},{2,10},{10,2},{3,11},{11,3},{4,12},{12,4},... | collective-permute-start | bytes 860168 | tf_op jit(solution)/shard_map/ppermute | solution.py:154
  32.3 8.2 %collective-permute-start.9 = (bf16[1120,128]{1,0:T(8,128)(2,1)S(1)}, bf16[1120,128]{1,0:T(8,128)(2,1)S(1)}, u32[]{:S(2)}, u32[]{:S(2)}) collective-permute-start(bf16[1120,128]{1,0:T(8,128)(2,1)S(1)} %collective-permute-done.1.refs_1_), channel_id=1, source_target_pairs={{0,8},{8,0},{1,9},{9,1},{2,10},{10,2},{3,11},{11,3},{4,12},{12,4},... | collective-permute-start | bytes 860168 | tf_op jit(solution)/shard_map/ppermute | solution.py:154
  32.8 8.2 %collective-permute-start.10 = (bf16[1120,128]{1,0:T(8,128)(2,1)S(1)}, bf16[1120,128]{1,0:T(8,128)(2,1)S(1)}, u32[]{:S(2)}, u32[]{:S(2)}) collective-permute-start(bf16[1120,128]{1,0:T(8,128)(2,1)S(1)} %collective-permute-done.2.refs_2_), channel_id=1, source_target_pairs={{0,8},{8,0},{1,9},{9,1},{2,10},{10,2},{3,11},{11,3},{4,12},{12,4},... | collective-permute-start | bytes 860168 | tf_op jit(solution)/shard_map/ppermute | solution.py:154
  36.8 8.3 %collective-permute-start.6 = (bf16[1120,128]{1,0:T(8,128)(2,1)S(1)}, bf16[1120,128]{1,0:T(8,128)(2,1)S(1)}, u32[]{:S(2)}, u32[]{:S(2)}) collective-permute-start(bf16[1120,128]{1,0:T(8,128)(2,1)S(1)} %collective-permute-done.4.refs_4_), channel_id=1, source_target_pairs={{0,112},{16,0},{32,16},{48,32},{64,48},{80,64},{96,80},{112,96},{1... | collective-permute-start | bytes 860168 | tf_op jit(solution)/shard_map/ppermute | solution.py:154
  39.8 7.8 %collective-permute-start.7 = (bf16[1120,128]{1,0:T(8,128)(2,1)S(1)}, bf16[1120,128]{1,0:T(8,128)(2,1)S(1)}, u32[]{:S(2)}, u32[]{:S(2)}) collective-permute-start(bf16[1120,128]{1,0:T(8,128)(2,1)S(1)} %collective-permute-done.5.refs_5_), channel_id=1, source_target_pairs={{0,16},{16,32},{32,48},{48,64},{64,80},{80,96},{96,112},{112,0},{1... | collective-permute-start | bytes 860168 | tf_op jit(solution)/shard_map/ppermute | solution.py:154
  40.5 8.4 %collective-permute-start.11 = (bf16[1120,128]{1,0:T(8,128)(2,1)S(1)}, bf16[1120,128]{1,0:T(8,128)(2,1)S(1)}, u32[]{:S(2)}, u32[]{:S(2)}) collective-permute-start(bf16[1120,128]{1,0:T(8,128)(2,1)S(1)} %collective-permute-done.3.refs_3_), channel_id=1, source_target_pairs={{0,8},{8,0},{1,9},{9,1},{2,10},{10,2},{3,11},{11,3},{4,12},{12,4},... | collective-permute-start | bytes 860168 | tf_op jit(solution)/shard_map/ppermute | solution.py:154
  40.5 8.4 %collective-permute-start.12 = (bf16[1120,128]{1,0:T(8,128)(2,1)S(1)}, bf16[1120,128]{1,0:T(8,128)(2,1)}, u32[]{:S(2)}, u32[]{:S(2)}) collective-permute-start(bf16[1120,128]{1,0:T(8,128)(2,1)S(1)} %collective-permute-done.4.refs_4_), channel_id=1, source_target_pairs={{0,8},{8,0},{1,9},{9,1},{2,10},{10,2},{3,11},{11,3},{4,12},{12,4},... | collective-permute-start | bytes 860168 | tf_op jit(solution)/shard_map/ppermute | solution.py:154
  41.0 7.9 %collective-permute-start.13 = (bf16[1120,128]{1,0:T(8,128)(2,1)S(1)}, bf16[1120,128]{1,0:T(8,128)(2,1)}, u32[]{:S(2)}, u32[]{:S(2)}) collective-permute-start(bf16[1120,128]{1,0:T(8,128)(2,1)S(1)} %collective-permute-done.5.refs_5_), channel_id=1, source_target_pairs={{0,8},{8,0},{1,9},{9,1},{2,10},{10,2},{3,11},{11,3},{4,12},{12,4},... | collective-permute-start | bytes 860168 | tf_op jit(solution)/shard_map/ppermute | solution.py:154
  45.1 3.9 %collective-permute-start.14 = (bf16[1120,128]{1,0:T(8,128)(2,1)S(1)}, bf16[1120,128]{1,0:T(8,128)(2,1)}, u32[]{:S(2)}, u32[]{:S(2)}) collective-permute-start(bf16[1120,128]{1,0:T(8,128)(2,1)S(1)} %collective-permute-done.6.refs_6_), channel_id=1, source_target_pairs={{0,8},{8,0},{1,9},{9,1},{2,10},{10,2},{3,11},{11,3},{4,12},{12,4},... | collective-permute-start | bytes 860168 | tf_op jit(solution)/shard_map/ppermute | solution.py:154
  47.6 1.7 %collective-permute-start.15 = (bf16[1120,128]{1,0:T(8,128)(2,1)S(1)}, bf16[1120,128]{1,0:T(8,128)(2,1)}, u32[]{:S(2)}, u32[]{:S(2)}) collective-permute-start(bf16[1120,128]{1,0:T(8,128)(2,1)S(1)} %collective-permute-done.7.refs_7_), channel_id=1, source_target_pairs={{0,8},{8,0},{1,9},{9,1},{2,10},{10,2},{3,11},{11,3},{4,12},{12,4},... | collective-permute-start | bytes 860168 | tf_op jit(solution)/shard_map/ppermute | solution.py:154
  65.0 21.4 %copy-start.1 = (bf16[128,768]{1,0:T(8,128)(2,1)S(1)}, bf16[128,768]{1,0:T(8,128)(2,1)}, u32[]{:S(2)}) copy-start(bf16[128,768]{1,0:T(8,128)(2,1)} %hidden_ref.1) | copy-start | bytes 589828
  91.7 28.3 %copy-start = (bf16[768,512]{1,0:T(8,128)(2,1)S(1)}, bf16[768,512]{1,0:T(8,128)(2,1)}, u32[]{:S(2)}) copy-start(bf16[768,512]{1,0:T(8,128)(2,1)} %proj_ref.1) | copy-start | bytes 2359300
  114.8 14.3 %all-to-all-start.4 = ((bf16[16,24,512]{2,1,0:T(8,128)(2,1)}), bf16[16,24,512]{2,1,0:T(8,128)(2,1)S(1)}, u32[]{:S(2)}, u32[]{:S(2)}) async-start(bf16[16,24,512]{2,1,0:T(8,128)(2,1)} %bitcast.4), calls=%async_computation.4 | async-start | bytes 786432 | tf_op jit(solution)/shard_map/all_to_all | solution.py:185

commit v2 on v1

v2 whole, which is shorter than its diff:
```python
import functools

import jax
import jax.numpy as jnp
from jax import lax
from jax.experimental import pallas as pl
from jax.experimental.pallas import tpu as pltpu
from jax.sharding import Mesh, PartitionSpec as P


LOG2E = 1.4426950408889634
PTS = 128
FEAT = 512
MSG = 560
ROW_CHUNK = 512
ALL = ("yh", "z", "c", "x", "yl")
VMEM = pl.BlockSpec(memory_space=pltpu.VMEM)
SMEM = pl.BlockSpec(memory_space=pltpu.SMEM)


def prepare_kernel(lsq_ref, near_ref, far_ref, rf, la, ai):
    half = 0.5 * LOG2E / lsq_ref[0]
    lane = lax.broadcasted_iota(jnp.int32, (PTS, 128), 1)
    for side, ref in enumerate((near_ref, far_ref)):
        for b in range(ref.shape[0]):
            at = (side * ref.shape[0] + b) * PTS
            here = slice(at, at + PTS)
            for k in range(4):
                rf[here, k * 128 : (k + 1) * 128] = ref[b, k * 128 : (k + 1) * 128, :]
            fac = ref[b, FEAT:MSG, :].astype(jnp.float32)
            sq = fac[33:34] + fac[34:35] + fac[35:36]
            swapped = jnp.concatenate(
                [
                    fac[0:1] * 0.5,
                    fac[17:33] * (-1 / 64),
                    fac[1:17] * (-1 / 64),
                    sq * half,
                    jnp.zeros((94, 128), jnp.float32),
                ],
                axis=0,
            ).T
            ai[here, :] = jnp.broadcast_to(swapped[:, 33:34], (PTS, 128))
            la[here, :] = jnp.where(lane < 33, swapped, 0.0).astype(jnp.bfloat16)


def prepare(near, far, lsq):
    r = (near.shape[0] + far.shape[0]) * PTS
    return pl.pallas_call(
        prepare_kernel,
        out_shape=(
            jax.ShapeDtypeStruct((r, FEAT), jnp.bfloat16),
            jax.ShapeDtypeStruct((r, 128), jnp.bfloat16),
            jax.ShapeDtypeStruct((r, 128), jnp.float32),
        ),
        in_specs=[SMEM, VMEM, VMEM],
        out_specs=(VMEM, VMEM, VMEM),
        cost_estimate=pl.CostEstimate(flops=r * FEAT * 100, bytes_accessed=r * FEAT, transcendentals=0),
        compiler_params=pltpu.CompilerParams(vmem_limit_bytes=16 * 1024 * 1024),
        name="prepare",
    )(lsq, near, far)


def chunk_kernel(n, first, last, amp_ref, lsq_ref, rf, la, ai, *refs):
    if not first:
        acc_in, rs_in = refs[:2]
        refs = refs[2:]
    cols_refs = refs[:n]
    refs = refs[n:]
    if last:
        out_ref, cf, cfac, acc, rs = refs
    else:
        acc, rs, cf, cfac = refs
    rows, width = rf.shape[0], cf.shape[0]
    c1 = LOG2E / lsq_ref[0]
    half = 0.5 * c1
    at = 0
    for ref in cols_refs:
        for k in range(4):
            cf[at : at + PTS, k * 128 : (k + 1) * 128] = ref[k * 128 : (k + 1) * 128, :]
        cfac[0:48, at : at + PTS] = ref[FEAT:MSG, :]
        at += PTS
    cfac[48:, :] = jnp.zeros((80, width), jnp.bfloat16)
    f3 = cfac[32:40, :].astype(jnp.float32)
    bj = (f3[1:2] + f3[2:3] + f3[3:4]) * half - jnp.log2(
        jnp.full((1, width), amp_ref[0], jnp.float32)
    )
    for r in range(rows // ROW_CHUNK):
        here = slice(r * ROW_CHUNK, (r + 1) * ROW_CHUNK)
        inner = lax.dot_general(
            rf[here, :], cf[...], (((1,), (1,)), ((), ())), preferred_element_type=jnp.float32
        )
        gmat = jnp.dot(la[here, :], cfac[...], preferred_element_type=jnp.float32)
        a = jnp.concatenate([ai[here, :]] * (width // 128), axis=1)
        w = gmat * jnp.exp2(inner * c1 - a - bj)
        total = w[:, 0:128]
        for q in range(1, width // 128):
            total = total + w[:, q * 128 : (q + 1) * 128]
        moved = jnp.dot(w.astype(jnp.bfloat16), cf[...], preferred_element_type=jnp.float32)
        if not first:
            total = rs_in[here, :] + total
            moved = acc_in[here, :] + moved
        if last:
            rowsum = jnp.sum(total, axis=1, keepdims=True)
            diff = (2.0 / lsq_ref[0]) * (moved - rowsum * rf[here, :].astype(jnp.float32))
            for b in range(ROW_CHUNK // PTS):
                side, block = divmod(r * (ROW_CHUNK // PTS) + b, out_ref.shape[1])
                out_ref[side, block] = diff[b * PTS : (b + 1) * PTS, :].astype(jnp.bfloat16)
        else:
            rs[here, :] = total
            acc[here, :] = moved


def chunk(sums, prepared, cols, amp, lsq, last):
    rf, la, ai = prepared
    r = rf.shape[0]
    c = len(cols) * PTS
    first = sums is None
    sums_shape = (
        jax.ShapeDtypeStruct((r, FEAT), jnp.float32),
        jax.ShapeDtypeStruct((r, 128), jnp.float32),
    )
    scratch = [pltpu.VMEM((c, FEAT), jnp.bfloat16), pltpu.VMEM((128, c), jnp.bfloat16)]
    if last:
        out_shape = jax.ShapeDtypeStruct((2, r // PTS // 2, PTS, FEAT), jnp.bfloat16)
        out_specs = VMEM
        scratch += [pltpu.VMEM((8, 128), jnp.float32), pltpu.VMEM((8, 128), jnp.float32)]
    else:
        out_shape, out_specs = sums_shape, (VMEM, VMEM)
    operands = (amp, lsq, rf, la, ai) + (() if first else tuple(sums)) + tuple(cols)
    return pl.pallas_call(
        functools.partial(chunk_kernel, len(cols), first, last),
        out_shape=out_shape,
        in_specs=[SMEM, SMEM] + [VMEM] * (len(operands) - 2),
        out_specs=out_specs,
        scratch_shapes=scratch,
        cost_estimate=pl.CostEstimate(
            flops=2 * r * c * 1280, bytes_accessed=4 * r * FEAT, transcendentals=r * c
        ),
        compiler_params=pltpu.CompilerParams(vmem_limit_bytes=16 * 1024 * 1024),
        name="chunk",
    )(*operands)


def message_kernel(hidden_ref, proj_ref, alpha_ref, probes_ref, out_ref):
    feats = jnp.dot(hidden_ref[...], proj_ref[...], preferred_element_type=jnp.float32).astype(
        jnp.bfloat16
    )
    feat_f = feats.astype(jnp.float32)
    for k in range(4):
        out_ref[k * 128 : (k + 1) * 128, :] = feats[:, k * 128 : (k + 1) * 128]
    sq = jnp.sum(feat_f * feat_f, axis=1, keepdims=True)
    hi = sq.astype(jnp.bfloat16).astype(jnp.float32)
    mid = (sq - hi).astype(jnp.bfloat16).astype(jnp.float32)
    low = sq - hi - mid
    probes = probes_ref[...].astype(jnp.float32)
    wide = jnp.concatenate([probes, hi, mid, low, jnp.zeros((PTS, 93), jnp.float32)], axis=1).T
    fac = jnp.concatenate([alpha_ref[...].astype(jnp.float32), wide[0:47]], axis=0)
    out_ref[FEAT:MSG, :] = fac.astype(jnp.bfloat16)


def message(hidden, projection, alpha, probe_pairs):
    return pl.pallas_call(
        message_kernel,
        out_shape=jax.ShapeDtypeStruct((MSG, 128), jnp.bfloat16),
        in_specs=[VMEM] * 4,
        out_specs=VMEM,
        name="message",
    )(hidden, projection, alpha.reshape(1, PTS), probe_pairs)


def sent_to_all(x, axes, size):
    return lax.all_to_all(jnp.broadcast_to(x[None], (size, *x.shape)), axes, 0, 0, tiled=True)


def shifted(x, axis, by):
    n = lax.axis_size(axis)
    return lax.ppermute(x, axis, [(i, (i + by) % n) for i in range(n)])


def steps(hidden, projection, alpha, probe_pairs, amplitude, length_sq):
    msg = message(hidden, projection, alpha, probe_pairs)
    rows = sent_to_all(msg, ("x", "yl"), 8)
    prepared = prepare(rows, shifted(rows, "c", 1), length_sq)
    across = shifted(msg, "yh", 1)
    order = [msg, across]
    ups, downs = [msg, across], [msg, across]
    for k in range(1, 5):
        for chain in range(2):
            ups[chain] = shifted(ups[chain], "z", 1)
            order.append(ups[chain])
            if k < 4:
                downs[chain] = shifted(downs[chain], "z", -1)
                order.append(downs[chain])
    sums = None
    for k in range(4):
        sums = chunk(sums, prepared, order[4 * k : 4 * k + 4], amplitude, length_sq, k == 3)
    part = sums[0] + shifted(sums[1], "c", 1)
    arrived = lax.all_to_all(part, ("x", "yl"), 0, 0, tiled=True)
    grad_feat = arrived.astype(jnp.float32).sum(axis=0).astype(jnp.bfloat16)
    grad_hidden = jnp.dot(grad_feat, projection.T, preferred_element_type=jnp.float32).astype(
        jnp.bfloat16
    )
    partial = lax.dot_general(
        hidden, grad_feat, (((0,), (0,)), ((), ())), preferred_element_type=jnp.float32
    ).astype(jnp.bfloat16)
    blocks = partial.reshape(2, 8, 2, 24, FEAT).transpose(2, 1, 0, 3, 4)
    got = lax.all_to_all(blocks, "c", 0, 0, tiled=True)
    core_sum = got.astype(jnp.float32).sum(axis=0).astype(jnp.bfloat16)
    got = lax.all_to_all(core_sum, "z", 0, 0, tiled=True)
    z_sum = got.astype(jnp.float32).sum(axis=0).astype(jnp.bfloat16)
    spread = jnp.broadcast_to(z_sum[:, None], (2, 8, 24, FEAT)).reshape(16, 24, FEAT)
    got = lax.all_to_all(spread, ("yh", "x", "yl"), 0, 0, tiled=True)
    grad_proj = got.astype(jnp.float32).sum(axis=0)
    return grad_hidden, grad_proj


def solution(mesh):
    fine = Mesh(mesh.devices.reshape(2, 8, 2, 4, 2), ALL)
    placed = (P(ALL, None), P(), P(ALL), P(ALL, None), P(), P())
    return jax.shard_map(
        steps,
        mesh=fine,
        in_specs=placed,
        out_specs=(P(ALL, None), P(("yh", "z", "c"), None)),
        check_vma=False,
    )
```

time: 131 us -> 135 us (1.031)
  blocking collectives: 47.9 us -> 64.2 us
  waiting for transfers between devices: 29.1 us -> 15.5 us
  starting transfers between devices: 24.8 us -> 31 us
  Pallas kernels: 17.9 us -> 15.4 us
    all_to_all x3 -> x4, blocking collectives: 47.9 us -> 64.2 us  [the longest x1 21.9 us: sent_to_all(): lax.all_to_all(jnp.broadcast_to(x[None], (size, *x.shape)), axes, 0, 0, t...]
    ppermute x16 -> x17, waiting for transfers between devices: 21.1 us -> 7.48 us  [shifted(): return lax.ppermute(x, axis, [(i, (i + by) % n) for i in range(n)])]
    ppermute x16 -> x17, starting transfers between devices: 14.3 us -> 25.8 us  [shifted(): return lax.ppermute(x, axis, [(i, (i + by) % n) for i in range(n)])]
    all_to_all x2 -> x1, starting transfers between devices: 10.5 us -> 5.19 us  [steps(): got = lax.all_to_all(spread, ('yh', 'x', 'yl'), 0, 0, tiled=True)]
    pallas_call x1 -> x5, Pallas kernels: 15.6 us -> 13.2 us  [the longest x4 12.2 us: chunk(): pl.pallas_call(functools.partial(chunk_kernel, len(cols), first, last), o...]
    all_to_all x2 -> x1, waiting for transfers between devices: 8.06 us -> 8.05 us  [steps(): got = lax.all_to_all(spread, ('yh', 'x', 'yl'), 0, 0, tiled=True)]
  transfers between devices with their start and end apart: 18 -> 18, of which waited for: 8 -> 6; matrix products, arithmetic and copies ran while one was open for 2% -> 1% of each run, Pallas kernels for 0% -> 7%
where the time goes in v2:
time: 135 us
  blocking collectives  64.2 us (48%)
  starting transfers between devices  31 us (23%)
  waiting for transfers between devices  15.5 us (11%)
  Pallas kernels  15.4 us (11%)
  local copies, waits for them, and re-layouts  3.8 us (3%)
  between operations  2.12 us (2%)
  matrix products  1.45 us (1%)
    ppermute x17, starting transfers between devices, shifted(): return lax.ppermute(x, axis, [(i, (i + by) % n) for i in range(n)])  25.8 us
    all_to_all x1, blocking collectives, sent_to_all(): lax.all_to_all(jnp.broadcast_to(x[None], (size, *x.shape)), axes, 0, 0, t...  21.9 us
    all_to_all x1, blocking collectives, steps(): got = lax.all_to_all(core_sum, 'z', 0, 0, tiled=True)  19.5 us
    all_to_all x1, blocking collectives, steps(): arrived = lax.all_to_all(part, ('x', 'yl'), 0, 0, tiled=True)  18.5 us
    pallas_call x4, Pallas kernels, chunk(): pl.pallas_call(functools.partial(chunk_kernel, len(cols), first, last), o...  12.2 us
    all_to_all x1, waiting for transfers between devices, steps(): got = lax.all_to_all(spread, ('yh', 'x', 'yl'), 0, 0, tiled=True)  8.05 us
    ppermute x17, waiting for transfers between devices, shifted(): return lax.ppermute(x, axis, [(i, (i + by) % n) for i in range(n)])  7.48 us
    all_to_all x1, starting transfers between devices, steps(): got = lax.all_to_all(spread, ('yh', 'x', 'yl'), 0, 0, tiled=True)  5.19 us
  transfers between devices with their start and end apart: 18, of which 6 were waited for; matrix products, arithmetic and copies ran while one was open for 1% of the time, Pallas kernels for 7%

profile of v2, /device:TPU:32, one launch (start us, length us, event | category | flops | bytes accessed | tf_op | source)
XLA Modules:
  0.0 134.7 jit_solution(4576384910798391403)
XLA Ops:
  0.6 1.4 %copy.20.probes_ref = bf16[128,32]{1,0:T(8,128)(2,1)} copy(bf16[128,32]{0,1:T(8,128)(2,1)} %param.9) | data formatting | bytes 16384 | tf_op args[3]
  2.0 2.3 %message.1.refs_0_ = bf16[560,128]{1,0:T(8,128)(2,1)} custom-call(bf16[128,768]{1,0:T(8,128)(2,1)} %hidden_ref.1, bf16[768,512]{1,0:T(8,128)(2,1)} %proj_ref.1, bf16[1,128]{1,0:T(2,128)(2,1)} %bitcast.18, bf16[128,32]{1,0:T(8,128)(2,1)} %copy.20.probes_ref), custom_call_target="tpu_custom_call" | custom-call | tf_op jit(solution)/shard_map/message/pallas_call | solution.py:162
  5.4 21.9 %all_to_all.25.near_ref = bf16[8,560,128]{2,1,0:T(8,128)(2,1)S(1)} all-to-all(bf16[8,560,128]{2,1,0:T(8,128)(2,1)S(1)} %broadcast_in_dim.4), channel_id=1, replica_groups=mesh['yh'=2,'z'=8,'c'=2,'x'=4,'yl'=2] {'x','yl'}, dimensions={0} | all-to-all | bytes 2293760 | tf_op jit(solution)/shard_map/all_to_all | solution.py:172
  27.3 2.9 %collective-permute-start.1 = (bf16[560,128]{1,0:T(8,128)(2,1)S(1)}, bf16[560,128]{1,0:T(8,128)(2,1)S(1)}, u32[]{:S(2)}, u32[]{:S(2)}) collective-permute-start(bf16[560,128]{1,0:T(8,128)(2,1)S(1)} %copy-done), channel_id=1, source_target_pairs={{0,128},{128,0},{1,129},{129,1},{2,130},{130,2},{3,131},{131,3},{4... | collective-permute-start | bytes 430088 | tf_op jit(solution)/shard_map/ppermute | solution.py:177
  30.2 1.9 %collective-permute-start.2 = (bf16[560,128]{1,0:T(8,128)(2,1)S(1)}, bf16[560,128]{1,0:T(8,128)(2,1)S(1)}, u32[]{:S(2)}, u32[]{:S(2)}) collective-permute-start(bf16[560,128]{1,0:T(8,128)(2,1)S(1)} %copy-done), channel_id=1, source_target_pairs={{0,16},{16,32},{32,48},{48,64},{64,80},{80,96},{96,112},{112,0},{1... | collective-permute-start | bytes 430088 | tf_op jit(solution)/shard_map/ppermute | solution.py:177
  32.1 2.8 %collective-permute-done.1.refs_1_ = bf16[560,128]{1,0:T(8,128)(2,1)S(1)} collective-permute-done((bf16[560,128]{1,0:T(8,128)(2,1)S(1)}, bf16[560,128]{1,0:T(8,128)(2,1)S(1)}, u32[]{:S(2)}, u32[]{:S(2)}) %collective-permute-start.1) | collective-permute-done | bytes 143392 | tf_op jit(solution)/shard_map/ppermute | solution.py:177
  35.0 1.9 %collective-permute-start.4 = (bf16[560,128]{1,0:T(8,128)(2,1)S(1)}, bf16[560,128]{1,0:T(8,128)(2,1)S(1)}, u32[]{:S(2)}, u32[]{:S(2)}) collective-permute-start(bf16[560,128]{1,0:T(8,128)(2,1)S(1)} %collective-permute-done.1.refs_1_), channel_id=1, source_target_pairs={{0,16},{16,32},{32,48},{48,64},{64,80},{80,96},{96,112},{112,0},{1... | collective-permute-start | bytes 430088 | tf_op jit(solution)/shard_map/ppermute | solution.py:177
  37.0 4.0 %collective-permute-start.5 = (bf16[560,128]{1,0:T(8,128)(2,1)S(1)}, bf16[560,128]{1,0:T(8,128)(2,1)S(1)}, u32[]{:S(2)}, u32[]{:S(2)}) collective-permute-start(bf16[560,128]{1,0:T(8,128)(2,1)S(1)} %collective-permute-done.1.refs_1_), channel_id=1, source_target_pairs={{0,112},{16,0},{32,16},{48,32},{64,48},{80,64},{96,80},{112,96},{1... | collective-permute-start | bytes 430088 | tf_op jit(solution)/shard_map/ppermute | solution.py:177
  42.2 1.3 collective-permute-done.3.refs_3_
  43.5 1.6 %collective-permute-start.7 = (bf16[560,128]{1,0:T(8,128)(2,1)S(1)}, bf16[560,128]{1,0:T(8,128)(2,1)S(1)}, u32[]{:S(2)}, u32[]{:S(2)}) collective-permute-start(bf16[560,128]{1,0:T(8,128)(2,1)S(1)} %collective-permute-done.3.refs_3_), channel_id=1, source_target_pairs={{0,112},{16,0},{32,16},{48,32},{64,48},{80,64},{96,80},{112,96},{1... | collective-permute-start | bytes 430088 | tf_op jit(solution)/shard_map/ppermute | solution.py:177
  45.5 3.3 %collective-permute-start.9 = (bf16[560,128]{1,0:T(8,128)(2,1)S(1)}, bf16[560,128]{1,0:T(8,128)(2,1)S(1)}, u32[]{:S(2)}, u32[]{:S(2)}) collective-permute-start(bf16[560,128]{1,0:T(8,128)(2,1)S(1)} %collective-permute-done.5.refs_3_), channel_id=1, source_target_pairs={{0,112},{16,0},{32,16},{48,32},{64,48},{80,64},{96,80},{112,96},{1... | collective-permute-start | bytes 430088 | tf_op jit(solution)/shard_map/ppermute | solution.py:177
  49.1 2.7 %collective-permute-start.12 = (bf16[560,128]{1,0:T(8,128)(2,1)S(1)}, bf16[560,128]{1,0:T(8,128)(2,1)S(1)}, u32[]{:S(2)}, u32[]{:S(2)}) collective-permute-start(bf16[560,128]{1,0:T(8,128)(2,1)S(1)} %collective-permute-done.8.refs_2_), channel_id=1, source_target_pairs={{0,16},{16,32},{32,48},{48,64},{64,80},{80,96},{96,112},{112,0},{1... | collective-permute-start | bytes 430088 | tf_op jit(solution)/shard_map/ppermute | solution.py:177
  53.4 3.2 %collective-permute-start.13 = (bf16[560,128]{1,0:T(8,128)(2,1)S(1)}, bf16[560,128]{1,0:T(8,128)(2,1)S(1)}, u32[]{:S(2)}, u32[]{:S(2)}) collective-permute-start(bf16[560,128]{1,0:T(8,128)(2,1)S(1)} %collective-permute-done.9.refs_3_), channel_id=1, source_target_pairs={{0,112},{16,0},{32,16},{48,32},{64,48},{80,64},{96,80},{112,96},{1... | collective-permute-start | bytes 430088 | tf_op jit(solution)/shard_map/ppermute | solution.py:177
  56.7 2.5 %collective-permute-start.15 = (bf16[560,128]{1,0:T(8,128)(2,1)S(1)}, bf16[560,128]{1,0:T(8,128)(2,1)S(1)}, u32[]{:S(2)}, u32[]{:S(2)}) collective-permute-start(bf16[560,128]{1,0:T(8,128)(2,1)S(1)} %collective-permute-done.12.refs_2_), channel_id=1, source_target_pairs={{0,16},{16,32},{32,48},{48,64},{64,80},{80,96},{96,112},{112,0},{1... | collective-permute-start | bytes 430088 | tf_op jit(solution)/shard_map/ppermute | solution.py:177
  60.1 3.0 %chunk.4 = (f32[2048,512]{1,0:T(8,128)S(1)}, f32[2048,128]{1,0:T(8,128)S(1)}) custom-call(f32[1]{0:T(128)S(6)} %copy.26.amp_ref, f32[1]{0:T(128)S(6)} %copy.27.lsq_ref, bf16[2048,512]{1,0:T(8,128)(2,1)S(1)} %get-tuple-element.11.rf, bf16[2048,128]{1,0:T(8,128)(2,1)S(1)} %get-tuple-element.12.la, f32[2048,128]{1,0:T(8,128)S(1)} %get-tuple-element.13.ai, ...), custom_call_target="tpu_custom_call" | custom-call | flops 2684354560 | bytes 4194304 | tf_op jit(solution)/shard_map/chunk/pallas_call | solution.py:130
  63.1 3.0 %chunk.5 = (f32[2048,512]{1,0:T(8,128)S(1)}, f32[2048,128]{1,0:T(8,128)S(1)}) custom-call(f32[1]{0:T(128)S(6)} %copy.26.amp_ref, f32[1]{0:T(128)S(6)} %copy.27.lsq_ref, bf16[2048,512]{1,0:T(8,128)(2,1)S(1)} %get-tuple-element.11.rf, bf16[2048,128]{1,0:T(8,128)(2,1)S(1)} %get-tuple-element.12.la, f32[2048,128]{1,0:T(8,128)S(1)} %get-tuple-element.13.ai, ...), custom_call_target="tpu_custom_call" | custom-call | flops 2684354560 | bytes 4194304 | tf_op jit(solution)/shard_map/chunk/pallas_call | solution.py:130
  66.2 3.0 %chunk.6 = (f32[2048,512]{1,0:T(8,128)S(1)}, f32[2048,128]{1,0:T(8,128)S(1)}) custom-call(f32[1]{0:T(128)S(6)} %copy.26.amp_ref, f32[1]{0:T(128)S(6)} %copy.27.lsq_ref, bf16[2048,512]{1,0:T(8,128)(2,1)S(1)} %get-tuple-element.11.rf, bf16[2048,128]{1,0:T(8,128)(2,1)S(1)} %get-tuple-element.12.la, f32[2048,128]{1,0:T(8,128)S(1)} %get-tuple-element.13.ai, ...), custom_call_target="tpu_custom_call" | custom-call | flops 2684354560 | bytes 4194304 | tf_op jit(solution)/shard_map/chunk/pallas_call | solution.py:130
  69.2 3.2 %chunk.7 = bf16[2,8,128,512]{3,2,1,0:T(8,128)(2,1)S(1)} custom-call(f32[1]{0:T(128)S(6)} %copy.26.amp_ref, f32[1]{0:T(128)S(6)} %copy.27.lsq_ref, bf16[2048,512]{1,0:T(8,128)(2,1)S(1)} %get-tuple-element.11.rf, bf16[2048,128]{1,0:T(8,128)(2,1)S(1)} %get-tuple-element.12.la, f32[2048,128]{1,0:T(8,128)S(1)} %get-tuple-element.13.ai, ...), custom_call_target="tpu_custom_call" | custom-call | flops 2684354560 | bytes 4194304 | tf_op jit(solution)/shard_map/chunk/pallas_call | solution.py:130
  72.6 2.6 %collective-permute-done.16 = bf16[8,128,512]{2,1,0:T(8,128)(2,1)S(1)} collective-permute-done((bf16[8,128,512]{2,1,0:T(8,128)(2,1)S(1)}, bf16[8,128,512]{2,1,0:T(8,128)(2,1)S(1)}, u32[]{:S(2)}, u32[]{:S(2)}) %collective-permute-start.16) | collective-permute-done | bytes 1048608 | tf_op jit(solution)/shard_map/ppermute | solution.py:177
  75.4 18.5 %all_to_all.26 = bf16[8,128,512]{2,1,0:T(8,128)(2,1)S(1)} all-to-all(bf16[8,128,512]{2,1,0:T(8,128)(2,1)S(1)} %fusion.1), channel_id=1, replica_groups=mesh['yh'=2,'z'=8,'c'=2,'x'=4,'yl'=2] {'x','yl'}, dimensions={0} | all-to-all | bytes 2097152 | tf_op jit(solution)/shard_map/all_to_all | solution.py:198
  94.8 4.4 %all_to_all.27 = bf16[2,8,2,24,512]{4,3,1,2,0:T(8,128)(2,1)S(1)} all-to-all(bf16[2,8,2,24,512]{4,3,1,2,0:T(8,128)(2,1)S(1)} %copy.22), channel_id=1, replica_groups=mesh['yh'=2,'z'=8,'c'=2,'x'=4,'yl'=2] {'c'}, dimensions={0} | all-to-all | bytes 1572864 | tf_op jit(solution)/shard_map/all_to_all | solution.py:207
  99.3 19.5 %all_to_all.28 = bf16[8,2,24,512]{3,2,1,0:T(8,128)(2,1)S(1)} all-to-all(bf16[8,2,24,512]{3,2,1,0:T(8,128)(2,1)S(1)} %copy.24), channel_id=1, replica_groups=mesh['yh'=2,'z'=8,'c'=2,'x'=4,'yl'=2] {'z'}, dimensions={0} | all-to-all | bytes 786432 | tf_op jit(solution)/shard_map/all_to_all | solution.py:209
  119.7 5.2 %all-to-all-start.4 = ((bf16[16,24,512]{2,1,0:T(8,128)(2,1)}), bf16[16,24,512]{2,1,0:T(8,128)(2,1)S(1)}, u32[]{:S(2)}, u32[]{:S(2)}) async-start(bf16[16,24,512]{2,1,0:T(8,128)(2,1)} %bitcast.6), calls=%async_computation.4 | async-start | bytes 786432 | tf_op jit(solution)/shard_map/all_to_all | solution.py:212
  126.0 8.1 %all-to-all-done.4 = bf16[16,24,512]{2,1,0:T(8,128)(2,1)S(1)} async-done(((bf16[16,24,512]{2,1,0:T(8,128)(2,1)}), bf16[16,24,512]{2,1,0:T(8,128)(2,1)S(1)}, u32[]{:S(2)}, u32[]{:S(2)}) %all-to-all-start.4) | async-done | bytes 393248 | tf_op jit(solution)/shard_map/all_to_all | solution.py:212
  (42 shorter events, 8.4 us)
Async XLA Ops:
  4.3 23.0 %copy-start = (bf16[560,128]{1,0:T(8,128)(2,1)S(1)}, bf16[560,128]{1,0:T(8,128)(2,1)}, u32[]{:S(2)}) copy-start(bf16[560,128]{1,0:T(8,128)(2,1)} %message.1.refs_0_) | copy-start | bytes 430084
  27.3 31.8 %collective-permute-start = (bf16[8,560,128]{2,1,0:T(8,128)(2,1)S(1)}, bf16[8,560,128]{2,1,0:T(8,128)(2,1)S(1)}, u32[]{:S(2)}, u32[]{:S(2)}) collective-permute-start(bf16[8,560,128]{2,1,0:T(8,128)(2,1)S(1)} %all_to_all.25.near_ref), channel_id=1, source_target_pairs={{0,8},{8,0},{1,9},{9,1},{2,10},{10,2},{3,11},{11,3},{4,12},{12,4},... | collective-permute-start | bytes 3440648 | tf_op jit(solution)/shard_map/ppermute | solution.py:177
  27.3 7.7 %collective-permute-start.1 = (bf16[560,128]{1,0:T(8,128)(2,1)S(1)}, bf16[560,128]{1,0:T(8,128)(2,1)S(1)}, u32[]{:S(2)}, u32[]{:S(2)}) collective-permute-start(bf16[560,128]{1,0:T(8,128)(2,1)S(1)} %copy-done), channel_id=1, source_target_pairs={{0,128},{128,0},{1,129},{129,1},{2,130},{130,2},{3,131},{131,3},{4... | collective-permute-start | bytes 430088 | tf_op jit(solution)/shard_map/ppermute | solution.py:177
  30.2 10.7 %collective-permute-start.2 = (bf16[560,128]{1,0:T(8,128)(2,1)S(1)}, bf16[560,128]{1,0:T(8,128)(2,1)S(1)}, u32[]{:S(2)}, u32[]{:S(2)}) collective-permute-start(bf16[560,128]{1,0:T(8,128)(2,1)S(1)} %copy-done), channel_id=1, source_target_pairs={{0,16},{16,32},{32,48},{48,64},{64,80},{80,96},{96,112},{112,0},{1... | collective-permute-start | bytes 430088 | tf_op jit(solution)/shard_map/ppermute | solution.py:177
  35.0 6.0 %collective-permute-start.4 = (bf16[560,128]{1,0:T(8,128)(2,1)S(1)}, bf16[560,128]{1,0:T(8,128)(2,1)S(1)}, u32[]{:S(2)}, u32[]{:S(2)}) collective-permute-start(bf16[560,128]{1,0:T(8,128)(2,1)S(1)} %collective-permute-done.1.refs_1_), channel_id=1, source_target_pairs={{0,16},{16,32},{32,48},{48,64},{64,80},{80,96},{96,112},{112,0},{1... | collective-permute-start | bytes 430088 | tf_op jit(solution)/shard_map/ppermute | solution.py:177
  36.9 6.6 %collective-permute-start.3 = (bf16[560,128]{1,0:T(8,128)(2,1)S(1)}, bf16[560,128]{1,0:T(8,128)(2,1)S(1)}, u32[]{:S(2)}, u32[]{:S(2)}) collective-permute-start(bf16[560,128]{1,0:T(8,128)(2,1)S(1)} %copy-done), channel_id=1, source_target_pairs={{0,112},{16,0},{32,16},{48,32},{64,48},{80,64},{96,80},{112,96},{1... | collective-permute-start | bytes 430088 | tf_op jit(solution)/shard_map/ppermute | solution.py:177
  37.0 8.5 %collective-permute-start.5 = (bf16[560,128]{1,0:T(8,128)(2,1)S(1)}, bf16[560,128]{1,0:T(8,128)(2,1)S(1)}, u32[]{:S(2)}, u32[]{:S(2)}) collective-permute-start(bf16[560,128]{1,0:T(8,128)(2,1)S(1)} %collective-permute-done.1.refs_1_), channel_id=1, source_target_pairs={{0,112},{16,0},{32,16},{48,32},{64,48},{80,64},{96,80},{112,96},{1... | collective-permute-start | bytes 430088 | tf_op jit(solution)/shard_map/ppermute | solution.py:177
  41.0 7.8 %collective-permute-start.6 = (bf16[560,128]{1,0:T(8,128)(2,1)S(1)}, bf16[560,128]{1,0:T(8,128)(2,1)S(1)}, u32[]{:S(2)}, u32[]{:S(2)}) collective-permute-start(bf16[560,128]{1,0:T(8,128)(2,1)S(1)} %collective-permute-done.2.refs_2_), channel_id=1, source_target_pairs={{0,16},{16,32},{32,48},{48,64},{64,80},{80,96},{96,112},{112,0},{1... | collective-permute-start | bytes 430088 | tf_op jit(solution)/shard_map/ppermute | solution.py:177
  41.0 8.1 %collective-permute-start.8 = (bf16[560,128]{1,0:T(8,128)(2,1)S(1)}, bf16[560,128]{1,0:T(8,128)(2,1)S(1)}, u32[]{:S(2)}, u32[]{:S(2)}) collective-permute-start(bf16[560,128]{1,0:T(8,128)(2,1)S(1)} %collective-permute-done.4.refs_2_), channel_id=1, source_target_pairs={{0,16},{16,32},{32,48},{48,64},{64,80},{80,96},{96,112},{112,0},{1... | collective-permute-start | bytes 430088 | tf_op jit(solution)/shard_map/ppermute | solution.py:177
  43.5 9.5 %collective-permute-start.7 = (bf16[560,128]{1,0:T(8,128)(2,1)S(1)}, bf16[560,128]{1,0:T(8,128)(2,1)S(1)}, u32[]{:S(2)}, u32[]{:S(2)}) collective-permute-start(bf16[560,128]{1,0:T(8,128)(2,1)S(1)} %collective-permute-done.3.refs_3_), channel_id=1, source_target_pairs={{0,112},{16,0},{32,16},{48,32},{64,48},{80,64},{96,80},{112,96},{1... | collective-permute-start | bytes 430088 | tf_op jit(solution)/shard_map/ppermute | solution.py:177
  45.5 7.9 %collective-permute-start.9 = (bf16[560,128]{1,0:T(8,128)(2,1)S(1)}, bf16[560,128]{1,0:T(8,128)(2,1)S(1)}, u32[]{:S(2)}, u32[]{:S(2)}) collective-permute-start(bf16[560,128]{1,0:T(8,128)(2,1)S(1)} %collective-permute-done.5.refs_3_), channel_id=1, source_target_pairs={{0,112},{16,0},{32,16},{48,32},{64,48},{80,64},{96,80},{112,96},{1... | collective-permute-start | bytes 430088 | tf_op jit(solution)/shard_map/ppermute | solution.py:177
  48.8 7.8 %collective-permute-start.10 = (bf16[560,128]{1,0:T(8,128)(2,1)S(1)}, bf16[560,128]{1,0:T(8,128)(2,1)S(1)}, u32[]{:S(2)}, u32[]{:S(2)}) collective-permute-start(bf16[560,128]{1,0:T(8,128)(2,1)S(1)} %collective-permute-done.6.refs_4_), channel_id=1, source_target_pairs={{0,16},{16,32},{32,48},{48,64},{64,80},{80,96},{96,112},{112,0},{1... | collective-permute-start | bytes 430088 | tf_op jit(solution)/shard_map/ppermute | solution.py:177
  49.1 7.6 %collective-permute-start.12 = (bf16[560,128]{1,0:T(8,128)(2,1)S(1)}, bf16[560,128]{1,0:T(8,128)(2,1)S(1)}, u32[]{:S(2)}, u32[]{:S(2)}) collective-permute-start(bf16[560,128]{1,0:T(8,128)(2,1)S(1)} %collective-permute-done.8.refs_2_), channel_id=1, source_target_pairs={{0,16},{16,32},{32,48},{48,64},{64,80},{80,96},{96,112},{112,0},{1... | collective-permute-start | bytes 430088 | tf_op jit(solution)/shard_map/ppermute | solution.py:177
  53.1 13.1 %collective-permute-start.11 = (bf16[560,128]{1,0:T(8,128)(2,1)S(1)}, bf16[560,128]{1,0:T(8,128)(2,1)S(1)}, u32[]{:S(2)}, u32[]{:S(2)}) collective-permute-start(bf16[560,128]{1,0:T(8,128)(2,1)S(1)} %collective-permute-done.7.refs_5_), channel_id=1, source_target_pairs={{0,112},{16,0},{32,16},{48,32},{64,48},{80,64},{96,80},{112,96},{1... | collective-permute-start | bytes 430088 | tf_op jit(solution)/shard_map/ppermute | solution.py:177
  53.4 15.8 %collective-permute-start.13 = (bf16[560,128]{1,0:T(8,128)(2,1)S(1)}, bf16[560,128]{1,0:T(8,128)(2,1)S(1)}, u32[]{:S(2)}, u32[]{:S(2)}) collective-permute-start(bf16[560,128]{1,0:T(8,128)(2,1)S(1)} %collective-permute-done.9.refs_3_), channel_id=1, source_target_pairs={{0,112},{16,0},{32,16},{48,32},{64,48},{80,64},{96,80},{112,96},{1... | collective-permute-start | bytes 430088 | tf_op jit(solution)/shard_map/ppermute | solution.py:177
  56.7 12.5 %collective-permute-start.14 = (bf16[560,128]{1,0:T(8,128)(2,1)S(1)}, bf16[560,128]{1,0:T(8,128)(2,1)S(1)}, u32[]{:S(2)}, u32[]{:S(2)}) collective-permute-start(bf16[560,128]{1,0:T(8,128)(2,1)S(1)} %collective-permute-done.10.refs_4_), channel_id=1, source_target_pairs={{0,16},{16,32},{32,48},{48,64},{64,80},{80,96},{96,112},{112,0},{1... | collective-permute-start | bytes 430088 | tf_op jit(solution)/shard_map/ppermute | solution.py:177
  56.7 12.5 %collective-permute-start.15 = (bf16[560,128]{1,0:T(8,128)(2,1)S(1)}, bf16[560,128]{1,0:T(8,128)(2,1)S(1)}, u32[]{:S(2)}, u32[]{:S(2)}) collective-permute-start(bf16[560,128]{1,0:T(8,128)(2,1)S(1)} %collective-permute-done.12.refs_2_), channel_id=1, source_target_pairs={{0,16},{16,32},{32,48},{48,64},{64,80},{80,96},{96,112},{112,0},{1... | collective-permute-start | bytes 430088 | tf_op jit(solution)/shard_map/ppermute | solution.py:177
  72.5 2.7 %collective-permute-start.16 = (bf16[8,128,512]{2,1,0:T(8,128)(2,1)S(1)}, bf16[8,128,512]{2,1,0:T(8,128)(2,1)S(1)}, u32[]{:S(2)}, u32[]{:S(2)}) collective-permute-start(bf16[8,128,512]{2,1,0:T(8,128)(2,1)S(1)} %slice_bitcast_fusion), channel_id=1, source_target_pairs={{0,8},{8,0},{1,9},{9,1},{2,10},{10,2},{3,11},{11,3},{4,12},{12,4},... | collective-permute-start | bytes 3145736 | tf_op jit(solution)/shard_map/ppermute | solution.py:177
  75.4 18.7 %copy-start.2 = (bf16[128,768]{1,0:T(8,128)(2,1)S(1)}, bf16[128,768]{1,0:T(8,128)(2,1)}, u32[]{:S(2)}) copy-start(bf16[128,768]{1,0:T(8,128)(2,1)} %hidden_ref.1) | copy-start | bytes 589828
  99.1 25.8 %copy-start.1 = (bf16[768,512]{1,0:T(8,128)(2,1)S(1)}, bf16[768,512]{1,0:T(8,128)(2,1)}, u32[]{:S(2)}) copy-start(bf16[768,512]{1,0:T(8,128)(2,1)} %proj_ref.1) | copy-start | bytes 2359300
  119.7 14.3 %all-to-all-start.4 = ((bf16[16,24,512]{2,1,0:T(8,128)(2,1)}), bf16[16,24,512]{2,1,0:T(8,128)(2,1)S(1)}, u32[]{:S(2)}, u32[]{:S(2)}) async-start(bf16[16,24,512]{2,1,0:T(8,128)(2,1)} %bitcast.6), calls=%async_computation.4 | async-start | bytes 786432 | tf_op jit(solution)/shard_map/all_to_all | solution.py:212

commit v3 on v2

--- a/solution.py
+++ b/solution.py
@@ -11,6 +11,8 @@
 LOG2E = 1.4426950408889634
 PTS = 128
 FEAT = 512
+HID = 768
+ROW_MSG = 816
 MSG = 560
 ROW_CHUNK = 512
 ALL = ("yh", "z", "c", "x", "yl")
@@ -18,46 +20,61 @@
 SMEM = pl.BlockSpec(memory_space=pltpu.SMEM)
 
 
-def prepare_kernel(lsq_ref, near_ref, far_ref, rf, la, ai):
+def prepare_kernel(n, lsq_ref, proj_ref, *refs):
+    bundles, (hr, rf, la, ai) = refs[: 2 * n], refs[2 * n :]
     half = 0.5 * LOG2E / lsq_ref[0]
     lane = lax.broadcasted_iota(jnp.int32, (PTS, 128), 1)
-    for side, ref in enumerate((near_ref, far_ref)):
-        for b in range(ref.shape[0]):
-            at = (side * ref.shape[0] + b) * PTS
-            here = slice(at, at + PTS)
-            for k in range(4):
-                rf[here, k * 128 : (k + 1) * 128] = ref[b, k * 128 : (k + 1) * 128, :]
-            fac = ref[b, FEAT:MSG, :].astype(jnp.float32)
-            sq = fac[33:34] + fac[34:35] + fac[35:36]
-            swapped = jnp.concatenate(
-                [
-                    fac[0:1] * 0.5,
-                    fac[17:33] * (-1 / 64),
-                    fac[1:17] * (-1 / 64),
-                    sq * half,
-                    jnp.zeros((94, 128), jnp.float32),
-                ],
-                axis=0,
-            ).T
-            ai[here, :] = jnp.broadcast_to(swapped[:, 33:34], (PTS, 128))
-            la[here, :] = jnp.where(lane < 33, swapped, 0.0).astype(jnp.bfloat16)
-
-
-def prepare(near, far, lsq):
-    r = (near.shape[0] + far.shape[0]) * PTS
+    for side in range(2):
+        for dx in range(n):
+            ref = bundles[side * n + dx]
+            for dy in range(2):
+                at = ((side * n + dx) * 2 + dy) * PTS
+                here = slice(at, at + PTS)
+                base = dy * ROW_MSG
+                for k in range(6):
+                    hr[here, k * 128 : (k + 1) * 128] = ref[
+                        base + k * 128 : base + (k + 1) * 128, :
+                    ]
+                fac = ref[base + HID : base + ROW_MSG, :].astype(jnp.float32)
+                sq = fac[33:34] + fac[34:35] + fac[35:36]
+                swapped = jnp.concatenate(
+                    [
+                        fac[0:1] * 0.5,
+                        fac[17:33] * (-1 / 64),
+                        fac[1:17] * (-1 / 64),
+                        sq * half,
+                        jnp.zeros((94, 128), jnp.float32),
+                    ],
+                    axis=0,
+                ).T
+                ai[here, :] = jnp.broadcast_to(swapped[:, 33:34], (PTS, 128))
+                la[here, :] = jnp.where(lane < 33, swapped, 0.0).astype(jnp.bfloat16)
+    for r in range(rf.shape[0] // ROW_CHUNK):
+        here = slice(r * ROW_CHUNK, (r + 1) * ROW_CHUNK)
+        rf[here, :] = jnp.dot(
+            hr[here, :], proj_ref[...], preferred_element_type=jnp.float32
+        ).astype(jnp.bfloat16)
+
+
+def prepare(near, far, projection, lsq):
+    n = len(near)
+    r = 4 * n * PTS
     return pl.pallas_call(
-        prepare_kernel,
+        functools.partial(prepare_kernel, n),
         out_shape=(
+            jax.ShapeDtypeStruct((r, HID), jnp.bfloat16),
             jax.ShapeDtypeStruct((r, FEAT), jnp.bfloat16),
             jax.ShapeDtypeStruct((r, 128), jnp.bfloat16),
             jax.ShapeDtypeStruct((r, 128), jnp.float32),
         ),
-        in_specs=[SMEM, VMEM, VMEM],
-        out_specs=(VMEM, VMEM, VMEM),
-        cost_estimate=pl.CostEstimate(flops=r * FEAT * 100, bytes_accessed=r * FEAT, transcendentals=0),
-        compiler_params=pltpu.CompilerParams(vmem_limit_bytes=16 * 1024 * 1024),
+        in_specs=[SMEM, VMEM] + [VMEM] * (2 * n),
+        out_specs=(VMEM,) * 4,
+        cost_estimate=pl.CostEstimate(
+            flops=2 * r * HID * FEAT, bytes_accessed=r * FEAT, transcendentals=0
+        ),
+        compiler_params=pltpu.CompilerParams(vmem_limit_bytes=10 * 1024 * 1024),
         name="prepare",
-    )(lsq, near, far)
+    )(lsq, projection, *near, *far)
 
 
 def chunk_kernel(n, first, last, amp_ref, lsq_ref, rf, la, ai, *refs):
@@ -75,10 +92,13 @@
     half = 0.5 * c1
     at = 0
     for ref in cols_refs:
-        for k in range(4):
-            cf[at : at + PTS, k * 128 : (k + 1) * 128] = ref[k * 128 : (k + 1) * 128, :]
-        cfac[0:48, at : at + PTS] = ref[FEAT:MSG, :]
-        at += PTS
+        for base in range(0, ref.shape[0], MSG):
+            for k in range(4):
+                cf[at : at + PTS, k * 128 : (k + 1) * 128] = ref[
+                    base + k * 128 : base + (k + 1) * 128, :
+                ]
+            cfac[0:48, at : at + PTS] = ref[base + FEAT : base + MSG, :]
+            at += PTS
     cfac[48:, :] = jnp.zeros((80, width), jnp.bfloat16)
     f3 = cfac[32:40, :].astype(jnp.float32)
     bj = (f3[1:2] + f3[2:3] + f3[3:4]) * half - jnp.log2(
@@ -113,7 +133,7 @@
 def chunk(sums, prepared, cols, amp, lsq, last):
     rf, la, ai = prepared
     r = rf.shape[0]
-    c = len(cols) * PTS
+    c = sum(x.shape[0] for x in cols) // MSG * PTS
     first = sums is None
     sums_shape = (
         jax.ShapeDtypeStruct((r, FEAT), jnp.float32),
@@ -136,12 +156,12 @@
         cost_estimate=pl.CostEstimate(
             flops=2 * r * c * 1280, bytes_accessed=4 * r * FEAT, transcendentals=r * c
         ),
-        compiler_params=pltpu.CompilerParams(vmem_limit_bytes=16 * 1024 * 1024),
+        compiler_params=pltpu.CompilerParams(vmem_limit_bytes=10 * 1024 * 1024),
         name="chunk",
     )(*operands)
 
 
-def message_kernel(hidden_ref, proj_ref, alpha_ref, probes_ref, out_ref):
+def message_kernel(hidden_ref, proj_ref, alpha_ref, probes_ref, out_ref, row_ref):
     feats = jnp.dot(hidden_ref[...], proj_ref[...], preferred_element_type=jnp.float32).astype(
         jnp.bfloat16
     )
@@ -156,20 +176,22 @@
     wide = jnp.concatenate([probes, hi, mid, low, jnp.zeros((PTS, 93), jnp.float32)], axis=1).T
     fac = jnp.concatenate([alpha_ref[...].astype(jnp.float32), wide[0:47]], axis=0)
     out_ref[FEAT:MSG, :] = fac.astype(jnp.bfloat16)
+    for k in range(6):
+        row_ref[k * 128 : (k + 1) * 128, :] = hidden_ref[:, k * 128 : (k + 1) * 128]
+    row_ref[HID:ROW_MSG, :] = fac.astype(jnp.bfloat16)
 
 
 def message(hidden, projection, alpha, probe_pairs):
     return pl.pallas_call(
         message_kernel,
-        out_shape=jax.ShapeDtypeStruct((MSG, 128), jnp.bfloat16),
+        out_shape=(
+            jax.ShapeDtypeStruct((MSG, 128), jnp.bfloat16),
+            jax.ShapeDtypeStruct((ROW_MSG, 128), jnp.bfloat16),
+        ),
         in_specs=[VMEM] * 4,
-        out_specs=VMEM,
+        out_specs=(VMEM, VMEM),
         name="message",
     )(hidden, projection, alpha.reshape(1, PTS), probe_pairs)
-
-
-def sent_to_all(x, axes, size):
-    return lax.all_to_all(jnp.broadcast_to(x[None], (size, *x.shape)), axes, 0, 0, tiled=True)
 
 
 def shifted(x, axis, by):
@@ -177,35 +199,48 @@
     return lax.ppermute(x, axis, [(i, (i + by) % n) for i in range(n)])
 
 
+def apart(x):
+    n = lax.axis_size("z")
+    hops = [(2 * i + c, 2 * ((i + (1, -1)[c]) % n) + c) for i in range(n) for c in range(2)]
+    return lax.ppermute(x, ("z", "c"), hops)
+
+
 def steps(hidden, projection, alpha, probe_pairs, amplitude, length_sq):
-    msg = message(hidden, projection, alpha, probe_pairs)
-    rows = sent_to_all(msg, ("x", "yl"), 8)
-    prepared = prepare(rows, shifted(rows, "c", 1), length_sq)
-    across = shifted(msg, "yh", 1)
-    order = [msg, across]
-    ups, downs = [msg, across], [msg, across]
+    msg, row_msg = message(hidden, projection, alpha, probe_pairs)
+    pair_rows = jnp.concatenate([row_msg, shifted(row_msg, "yl", 1)], axis=0)
+    near = [pair_rows] + [shifted(pair_rows, "x", k) for k in (1, 2, 3)]
+    far = [shifted(b, "c", 1) for b in near]
+    hidden_rows, *prepared = prepare(near, far, projection, length_sq)
+    own = jnp.concatenate([msg, shifted(msg, "yh", 1)], axis=0)
+    held = jnp.concatenate([own, shifted(own, "c", 1)], axis=0)
+    ring = []
     for k in range(1, 5):
-        for chain in range(2):
-            ups[chain] = shifted(ups[chain], "z", 1)
-            order.append(ups[chain])
-            if k < 4:
-                downs[chain] = shifted(downs[chain], "z", -1)
-                order.append(downs[chain])
+        held = apart(held if k < 4 else held[: 2 * MSG])
+        ring.append(held)
+    groups = [[own, ring[0]], ring[1:2], ring[2:3], ring[3:4]]
     sums = None
-    for k in range(4):
-        sums = chunk(sums, prepared, order[4 * k : 4 * k + 4], amplitude, length_sq, k == 3)
+    for k, group in enumerate(groups):
+        sums = chunk(sums, prepared, group, amplitude, length_sq, k == 3)
+    partial = lax.dot_general(
+        hidden_rows,
+        sums.reshape(hidden_rows.shape[0], FEAT),
+        (((0,), (0,)), ((), ())),
+        preferred_element_type=jnp.float32,
+    ).astype(jnp.bfloat16)
     part = sums[0] + shifted(sums[1], "c", 1)
-    arrived = lax.all_to_all(part, ("x", "yl"), 0, 0, tiled=True)
-    grad_feat = arrived.astype(jnp.float32).sum(axis=0).astype(jnp.bfloat16)
+    total = part[0:2].astype(jnp.float32)
+    for k in (1, 2, 3):
+        total = total + shifted(part[2 * k : 2 * k + 2], "x", -k).astype(jnp.float32)
+    aside = shifted(total[1].astype(jnp.bfloat16), "yl", 1)
+    grad_feat = (total[0] + aside.astype(jnp.float32)).astype(jnp.bfloat16)
     grad_hidden = jnp.dot(grad_feat, projection.T, preferred_element_type=jnp.float32).astype(
         jnp.bfloat16
     )
-    partial = lax.dot_general(
-        hidden, grad_feat, (((0,), (0,)), ((), ())), preferred_element_type=jnp.float32
-    ).astype(jnp.bfloat16)
     blocks = partial.reshape(2, 8, 2, 24, FEAT).transpose(2, 1, 0, 3, 4)
-    got = lax.all_to_all(blocks, "c", 0, 0, tiled=True)
-    core_sum = got.astype(jnp.float32).sum(axis=0).astype(jnp.bfloat16)
+    core = lax.axis_index("c")
+    mine = lax.dynamic_index_in_dim(blocks, core, 0, keepdims=False)
+    other = lax.dynamic_index_in_dim(blocks, 1 - core, 0, keepdims=False)
+    core_sum = mine + shifted(other, "c", 1)
     got = lax.all_to_all(core_sum, "z", 0, 0, tiled=True)
     z_sum = got.astype(jnp.float32).sum(axis=0).astype(jnp.bfloat16)
     spread = jnp.broadcast_to(z_sum[:, None], (2, 8, 24, FEAT)).reshape(16, 24, FEAT)

time: 135 us -> 117 us (0.87)
  blocking collectives: 64.2 us -> 0 us
  waiting for transfers between devices: 15.5 us -> 41.7 us
  starting transfers between devices: 31 us -> 37.8 us
  local copies, waits for them, and re-layouts: 3.8 us -> 8.14 us
  other arithmetic: 1.14 us -> 4.87 us
  matrix products: 1.45 us -> 4.76 us
    all_to_all x4 -> x0, blocking collectives: 64.2 us -> none  [the longest x1 21.9 us: sent_to_all(): lax.all_to_all(jnp.broadcast_to(x[None], (size, *x.shape)), axes, 0, 0, t...]
    ppermute x17 -> x16, waiting for transfers between devices: 7.48 us -> 29.9 us  [shifted(): return lax.ppermute(x, axis, [(i, (i + by) % n) for i in range(n)])]
    ppermute x0 -> x4, starting transfers between devices: none -> 7.25 us  [apart(): return lax.ppermute(x, ('z', 'c'), hops)]
    ppermute x17 -> x16, starting transfers between devices: 25.8 us -> 18.9 us  [shifted(): return lax.ppermute(x, axis, [(i, (i + by) % n) for i in range(n)])]
    all_to_all x0 -> x1, starting transfers between devices: none -> 5.09 us  [steps(): got = lax.all_to_all(core_sum, 'z', 0, 0, tiled=True)]
    unnamed x7 -> x10, local copies, waits for them, and re-layouts: 1.43 us -> 6.08 us
    dot_general x1, matrix products: 0.38 us -> 3.7 us  [steps(): lax.dot_general(hidden_rows, sums.reshape(hidden_rows.shape[0], FEAT), ((...]
    all_to_all x0 -> x1, waiting for transfers between devices: none -> 1.96 us  [steps(): got = lax.all_to_all(core_sum, 'z', 0, 0, tiled=True)]
  transfers between devices with their start and end apart: 18 -> 22, of which waited for: 6 -> 10; matrix products, arithmetic and copies ran while one was open for 1% -> 9% of each run, Pallas kernels for 7% -> 11%
where the time goes in v3:
time: 117 us; the launch traced here: 116 us
  waiting for transfers between devices  41.7 us (36%)
  starting transfers between devices  37.8 us (32%)
  Pallas kernels  16.7 us (14%)
  local copies, waits for them, and re-layouts  8.14 us (7%)
  other arithmetic  4.87 us (4%)
  matrix products  4.76 us (4%)
  between operations  2.16 us (2%)
    ppermute x16, waiting for transfers between devices, shifted(): return lax.ppermute(x, axis, [(i, (i + by) % n) for i in range(n)])  29.9 us
    ppermute x16, starting transfers between devices, shifted(): return lax.ppermute(x, axis, [(i, (i + by) % n) for i in range(n)])  18.9 us
    pallas_call x4, Pallas kernels, chunk(): pl.pallas_call(functools.partial(chunk_kernel, len(cols), first, last), o...  12.4 us
    all_to_all x1, waiting for transfers between devices, steps(): got = lax.all_to_all(spread, ('yh', 'x', 'yl'), 0, 0, tiled=True)  8.06 us
    ppermute x4, starting transfers between devices, apart(): return lax.ppermute(x, ('z', 'c'), hops)  7.25 us
    all_to_all x1, starting transfers between devices, steps(): got = lax.all_to_all(spread, ('yh', 'x', 'yl'), 0, 0, tiled=True)  6.59 us
    unnamed x10, local copies, waits for them, and re-layouts  6.08 us
    all_to_all x1, starting transfers between devices, steps(): got = lax.all_to_all(core_sum, 'z', 0, 0, tiled=True)  5.09 us
  transfers between devices with their start and end apart: 22, of which 10 were waited for; matrix products, arithmetic and copies ran while one was open for 9% of the time, Pallas kernels for 11%

profile of v3, /device:TPU:32, one launch (start us, length us, event | category | flops | bytes accessed | tf_op | source)
XLA Modules:
  0.0 116.1 jit_solution(8645851482808735748)
XLA Ops:
  2.1 2.4 %message.1 = (bf16[560,128]{1,0:T(8,128)(2,1)}, bf16[816,128]{1,0:T(8,128)(2,1)}) custom-call(bf16[128,768]{1,0:T(8,128)(2,1)} %hidden_ref.1, bf16[768,512]{1,0:T(8,128)(2,1)} %proj_ref.3, bf16[1,128]{1,0:T(2,128)(2,1)} %bitcast.36, bf16[128,32]{1,0:T(8,128)(2,1)} %copy.13.probes_ref), custom_call_target="tpu_custom_call" | custom-call | tf_op jit(solution)/shard_map/message/pallas_call | solution.py:185
  4.5 3.2 %collective-permute-start.8 = (bf16[560,128]{1,0:T(8,128)(2,1)}, bf16[560,128]{1,0:T(8,128)(2,1)S(1)}, u32[]{:S(2)}, u32[]{:S(2)}) collective-permute-start(bf16[560,128]{1,0:T(8,128)(2,1)} %get-tuple-element.18), channel_id=1, source_target_pairs={{0,128},{128,0},{1,129},{129,1},{2,130},{130,2},{3,131},{131,3},{4... | collective-permute-start | bytes 430088 | tf_op jit(solution)/shard_map/ppermute | solution.py:199
  8.6 3.1 %collective-permute-done.8 = bf16[560,128]{1,0:T(8,128)(2,1)S(1)} collective-permute-done((bf16[560,128]{1,0:T(8,128)(2,1)}, bf16[560,128]{1,0:T(8,128)(2,1)S(1)}, u32[]{:S(2)}, u32[]{:S(2)}) %collective-permute-start.8) | collective-permute-done | bytes 143392 | tf_op jit(solution)/shard_map/ppermute | solution.py:199
  14.3 2.0 %collective-permute-start.10 = (bf16[2240,128]{1,0:T(8,128)(2,1)S(1)}, bf16[2240,128]{1,0:T(8,128)(2,1)S(1)}, u32[]{:S(2)}, u32[]{:S(2)}) collective-permute-start(bf16[2240,128]{1,0:T(8,128)(2,1)S(1)} %pad_maximum_fusion), channel_id=1, source_target_pairs={{0,16},{8,120},{16,32},{24,8},{32,48},{40,24},{48,64},{56,40},{64,... | collective-permute-start | bytes 1720328 | tf_op jit(solution)/shard_map/ppermute | solution.py:205
  18.9 4.1 %collective-permute-done = bf16[816,128]{1,0:T(8,128)(2,1)S(1)} collective-permute-done((bf16[816,128]{1,0:T(8,128)(2,1)}, bf16[816,128]{1,0:T(8,128)(2,1)S(1)}, u32[]{:S(2)}, u32[]{:S(2)}) %collective-permute-start) | collective-permute-done | bytes 208928 | tf_op jit(solution)/shard_map/ppermute | solution.py:199
  23.9 2.7 %collective-permute-start.2 = (bf16[1632,128]{1,0:T(8,128)(2,1)S(1)}, bf16[1632,128]{1,0:T(8,128)(2,1)S(1)}, u32[]{:S(2)}, u32[]{:S(2)}) collective-permute-start(bf16[1632,128]{1,0:T(8,128)(2,1)S(1)} %constant_dynamic-update-slice_fusion.refs_0_), channel_id=1, source_target_pairs={{0,4},{2,6},{4,0},{6,2},{1,5},{3,7},{5,1},{7,3},{8,12},{10,14},{12... | collective-permute-start | bytes 1253384 | tf_op jit(solution)/shard_map/ppermute | solution.py:199
  28.1 1.9 %collective-permute-start.11 = (bf16[2240,128]{1,0:T(8,128)(2,1)S(1)}, bf16[2240,128]{1,0:T(8,128)(2,1)S(1)}, u32[]{:S(2)}, u32[]{:S(2)}) collective-permute-start(bf16[2240,128]{1,0:T(8,128)(2,1)S(1)} %collective-permute-done.10.refs_1_), channel_id=1, source_target_pairs={{0,16},{8,120},{16,32},{24,8},{32,48},{40,24},{48,64},{56,40},{64,... | collective-permute-start | bytes 1720328 | tf_op jit(solution)/shard_map/ppermute | solution.py:205
  30.0 13.3 %collective-permute-done.1.refs_1_ = bf16[1632,128]{1,0:T(8,128)(2,1)S(1)} collective-permute-done((bf16[1632,128]{1,0:T(8,128)(2,1)S(1)}, bf16[1632,128]{1,0:T(8,128)(2,1)S(1)}, u32[]{:S(2)}, u32[]{:S(2)}) %collective-permute-start.1) | collective-permute-done | bytes 417824 | tf_op jit(solution)/shard_map/ppermute | solution.py:199
  46.4 1.9 %prepare.1 = (bf16[2048,768]{1,0:T(8,128)(2,1)S(1)}, bf16[2048,512]{1,0:T(8,128)(2,1)S(1)}, bf16[2048,128]{1,0:T(8,128)(2,1)S(1)}, f32[2048,128]{1,0:T(8,128)S(1)}) custom-call(f32[1]{0:T(128)S(6)} %copy.26.lsq_ref, bf16[768,512]{1,0:T(8,128)(2,1)S(1)} %copy-done.1, bf16[1632,128]{1,0:T(8,128)(2,1)S(1)} %constant_dynamic-update-slice_fusion.refs_0_, ...), custom_call_target="tpu_custom_call" | custom-call | flops 1610612736 | bytes 1048576 | tf_op jit(solution)/shard_map/prepare/pallas_call | solution.py:62
  50.0 4.4 %chunk.4 = (f32[2048,512]{1,0:T(8,128)S(1)}, f32[2048,128]{1,0:T(8,128)S(1)}) custom-call(f32[1]{0:T(128)S(6)} %copy.25.amp_ref, f32[1]{0:T(128)S(6)} %copy.26.lsq_ref, bf16[2048,512]{1,0:T(8,128)(2,1)S(1)} %get-tuple-element.15.rf, bf16[2048,128]{1,0:T(8,128)(2,1)S(1)} %get-tuple-element.16.la, f32[2048,128]{1,0:T(8,128)S(1)} %get-tuple-element.17.ai, ...), custom_call_target="tpu_custom_call" | custom-call | flops 4026531840 | bytes 4194304 | tf_op jit(solution)/shard_map/chunk/pallas_call | solution.py:150
  54.4 2.2 %collective-permute-start.13 = (bf16[1120,128]{1,0:T(8,128)(2,1)S(1)}, bf16[1120,128]{1,0:T(8,128)(2,1)S(1)}, u32[]{:S(2)}, u32[]{:S(2)}) collective-permute-start(bf16[1120,128]{1,0:T(8,128)(2,1)S(1)} %slice.37), channel_id=1, source_target_pairs={{0,16},{8,120},{16,32},{24,8},{32,48},{40,24},{48,64},{56,40},{64,... | collective-permute-start | bytes 860168 | tf_op jit(solution)/shard_map/ppermute | solution.py:205
  56.6 3.0 %chunk.5 = (f32[2048,512]{1,0:T(8,128)S(1)}, f32[2048,128]{1,0:T(8,128)S(1)}) custom-call(f32[1]{0:T(128)S(6)} %copy.25.amp_ref, f32[1]{0:T(128)S(6)} %copy.26.lsq_ref, bf16[2048,512]{1,0:T(8,128)(2,1)S(1)} %get-tuple-element.15.rf, bf16[2048,128]{1,0:T(8,128)(2,1)S(1)} %get-tuple-element.16.la, f32[2048,128]{1,0:T(8,128)S(1)} %get-tuple-element.17.ai, ...), custom_call_target="tpu_custom_call" | custom-call | flops 2684354560 | bytes 4194304 | tf_op jit(solution)/shard_map/chunk/pallas_call | solution.py:150
  59.6 3.0 %chunk.6 = (f32[2048,512]{1,0:T(8,128)S(1)}, f32[2048,128]{1,0:T(8,128)S(1)}) custom-call(f32[1]{0:T(128)S(6)} %copy.25.amp_ref, f32[1]{0:T(128)S(6)} %copy.26.lsq_ref, bf16[2048,512]{1,0:T(8,128)(2,1)S(1)} %get-tuple-element.15.rf, bf16[2048,128]{1,0:T(8,128)(2,1)S(1)} %get-tuple-element.16.la, f32[2048,128]{1,0:T(8,128)S(1)} %get-tuple-element.17.ai, ...), custom_call_target="tpu_custom_call" | custom-call | flops 2684354560 | bytes 4194304 | tf_op jit(solution)/shard_map/chunk/pallas_call | solution.py:150
  62.6 1.8 %collective-permute-done.13.refs_2_ = bf16[1120,128]{1,0:T(8,128)(2,1)S(1)} collective-permute-done((bf16[1120,128]{1,0:T(8,128)(2,1)S(1)}, bf16[1120,128]{1,0:T(8,128)(2,1)S(1)}, u32[]{:S(2)}, u32[]{:S(2)}) %collective-permute-start.13) | collective-permute-done | bytes 286752 | tf_op jit(solution)/shard_map/ppermute | solution.py:205
  64.4 2.0 %chunk.7 = bf16[2,8,128,512]{3,2,1,0:T(8,128)(2,1)S(1)} custom-call(f32[1]{0:T(128)S(6)} %copy.25.amp_ref, f32[1]{0:T(128)S(6)} %copy.26.lsq_ref, bf16[2048,512]{1,0:T(8,128)(2,1)S(1)} %get-tuple-element.15.rf, bf16[2048,128]{1,0:T(8,128)(2,1)S(1)} %get-tuple-element.16.la, f32[2048,128]{1,0:T(8,128)S(1)} %get-tuple-element.17.ai, ...), custom_call_target="tpu_custom_call" | custom-call | flops 1342177280 | bytes 4194304 | tf_op jit(solution)/shard_map/chunk/pallas_call | solution.py:150
  67.5 2.7 %collective-permute-start.14 = (bf16[8,128,512]{2,1,0:T(8,128)(2,1)}, bf16[8,128,512]{2,1,0:T(8,128)(2,1)}, u32[]{:S(2)}, u32[]{:S(2)}) collective-permute-start(bf16[8,128,512]{2,1,0:T(8,128)(2,1)} %slice_bitcast_fusion), channel_id=1, source_target_pairs={{0,8},{8,0},{1,9},{9,1},{2,10},{10,2},{3,11},{11,3},{4,12},{12,4},... | collective-permute-start | bytes 3145736 | tf_op jit(solution)/shard_map/ppermute | solution.py:199
  70.2 3.7 %convolution_convert_fusion = bf16[768,512]{1,0:T(8,128)(2,1)S(1)} fusion(bf16[2048,768]{1,0:T(8,128)(2,1)} %copy-done, bf16[2048,512]{1,0:T(8,128)(2,1)S(1)} %bitcast.33), kind=kOutput, calls=%fused_computation | convolution fusion | flops 1611005952 | bytes 6029312 | tf_op jit(solution)/shard_map/dot_general | solution.py:224
  76.5 2.1 %collective-permute-start.15 = (bf16[2,128,512]{2,1,0:T(8,128)(2,1)S(1)}, bf16[2,128,512]{2,1,0:T(8,128)(2,1)S(1)}, u32[]{:S(2)}, u32[]{:S(2)}) collective-permute-start(bf16[2,128,512]{2,1,0:T(8,128)(2,1)S(1)} %get-tuple-element.26), channel_id=1, source_target_pairs={{0,6},{2,0},{4,2},{6,4},{1,7},{3,1},{5,3},{7,5},{8,14},{10,8},{12,... | collective-permute-start | bytes 786440 | tf_op jit(solution)/shard_map/ppermute | solution.py:199
  81.2 5.1 %all-to-all-start = ((bf16[8,2,24,512]{3,2,1,0:T(8,128)(2,1)}), bf16[8,2,24,512]{3,2,1,0:T(8,128)(2,1)S(1)}, u32[]{:S(2)}, u32[]{:S(2)}) async-start(bf16[8,2,24,512]{3,2,1,0:T(8,128)(2,1)} %fusion.1), calls=%async_computation | async-start | bytes 786432 | tf_op jit(solution)/shard_map/all_to_all | solution.py:244
  86.3 4.2 %collective-permute-done.15 = bf16[2,128,512]{2,1,0:T(8,128)(2,1)S(1)} collective-permute-done((bf16[2,128,512]{2,1,0:T(8,128)(2,1)S(1)}, bf16[2,128,512]{2,1,0:T(8,128)(2,1)S(1)}, u32[]{:S(2)}, u32[]{:S(2)}) %collective-permute-start.15) | collective-permute-done | bytes 262176 | tf_op jit(solution)/shard_map/ppermute | solution.py:199
  90.5 3.7 %collective-permute-done.17 = bf16[2,128,512]{2,1,0:T(8,128)(2,1)S(1)} collective-permute-done((bf16[2,128,512]{2,1,0:T(8,128)(2,1)S(1)}, bf16[2,128,512]{2,1,0:T(8,128)(2,1)S(1)}, u32[]{:S(2)}, u32[]{:S(2)}) %collective-permute-start.17) | collective-permute-done | bytes 262176 | tf_op jit(solution)/shard_map/ppermute | solution.py:199
  96.9 2.0 %all-to-all-done = bf16[8,2,24,512]{3,2,1,0:T(8,128)(2,1)S(1)} async-done(((bf16[8,2,24,512]{3,2,1,0:T(8,128)(2,1)}), bf16[8,2,24,512]{3,2,1,0:T(8,128)(2,1)S(1)}, u32[]{:S(2)}, u32[]{:S(2)}) %all-to-all-start) | async-done | bytes 393248 | tf_op jit(solution)/shard_map/all_to_all | solution.py:244
  99.7 6.6 %all-to-all-start.1 = ((bf16[16,24,512]{2,1,0:T(8,128)(2,1)}), bf16[16,24,512]{2,1,0:T(8,128)(2,1)S(1)}, u32[]{:S(2)}, u32[]{:S(2)}) async-start(bf16[16,24,512]{2,1,0:T(8,128)(2,1)} %bitcast.11), calls=%async_computation.1 | async-start | bytes 786432 | tf_op jit(solution)/shard_map/all_to_all | solution.py:247
  107.4 8.1 %all-to-all-done.1 = bf16[16,24,512]{2,1,0:T(8,128)(2,1)S(1)} async-done(((bf16[16,24,512]{2,1,0:T(8,128)(2,1)}), bf16[16,24,512]{2,1,0:T(8,128)(2,1)S(1)}, u32[]{:S(2)}, u32[]{:S(2)}) %all-to-all-start.1) | async-done | bytes 393248 | tf_op jit(solution)/shard_map/all_to_all | solution.py:247
  (52 shorter events, 25.0 us)
Async XLA Ops:
  0.6 45.8 %copy-start.1 = (bf16[768,512]{1,0:T(8,128)(2,1)S(1)}, bf16[768,512]{1,0:T(8,128)(2,1)}, u32[]{:S(2)}) copy-start(bf16[768,512]{1,0:T(8,128)(2,1)} %proj_ref.3) | copy-start | bytes 2359300
  4.5 7.2 %collective-permute-start.8 = (bf16[560,128]{1,0:T(8,128)(2,1)}, bf16[560,128]{1,0:T(8,128)(2,1)S(1)}, u32[]{:S(2)}, u32[]{:S(2)}) collective-permute-start(bf16[560,128]{1,0:T(8,128)(2,1)} %get-tuple-element.18), channel_id=1, source_target_pairs={{0,128},{128,0},{1,129},{129,1},{2,130},{130,2},{3,131},{131,3},{4... | collective-permute-start | bytes 430088 | tf_op jit(solution)/shard_map/ppermute | solution.py:199
  11.7 1.7 %collective-permute-start.9 = (bf16[1120,128]{1,0:T(8,128)(2,1)S(1)}, bf16[1120,128]{1,0:T(8,128)(2,1)S(1)}, u32[]{:S(2)}, u32[]{:S(2)}) collective-permute-start(bf16[1120,128]{1,0:T(8,128)(2,1)S(1)} %constant_dynamic-update-slice_fusion.2.refs_0_), channel_id=1, source_target_pairs={{0,8},{8,0},{1,9},{9,1},{2,10},{10,2},{3,11},{11,3},{4,12},{12,4},... | collective-permute-start | bytes 860168 | tf_op jit(solution)/shard_map/ppermute | solution.py:199
  14.3 13.8 %collective-permute-start.10 = (bf16[2240,128]{1,0:T(8,128)(2,1)S(1)}, bf16[2240,128]{1,0:T(8,128)(2,1)S(1)}, u32[]{:S(2)}, u32[]{:S(2)}) collective-permute-start(bf16[2240,128]{1,0:T(8,128)(2,1)S(1)} %pad_maximum_fusion), channel_id=1, source_target_pairs={{0,16},{8,120},{16,32},{24,8},{32,48},{40,24},{48,64},{56,40},{64,... | collective-permute-start | bytes 1720328 | tf_op jit(solution)/shard_map/ppermute | solution.py:205
  16.3 6.6 %collective-permute-start = (bf16[816,128]{1,0:T(8,128)(2,1)}, bf16[816,128]{1,0:T(8,128)(2,1)S(1)}, u32[]{:S(2)}, u32[]{:S(2)}) collective-permute-start(bf16[816,128]{1,0:T(8,128)(2,1)} %get-tuple-element.14), channel_id=1, source_target_pairs={{0,1},{1,0},{2,3},{3,2},{4,5},{5,4},{6,7},{7,6},{8,9},{9,8},{10,11... | collective-permute-start | bytes 626696 | tf_op jit(solution)/shard_map/ppermute | solution.py:199
  23.0 20.3 %collective-permute-start.1 = (bf16[1632,128]{1,0:T(8,128)(2,1)S(1)}, bf16[1632,128]{1,0:T(8,128)(2,1)S(1)}, u32[]{:S(2)}, u32[]{:S(2)}) collective-permute-start(bf16[1632,128]{1,0:T(8,128)(2,1)S(1)} %constant_dynamic-update-slice_fusion.refs_0_), channel_id=1, source_target_pairs={{0,2},{2,4},{4,6},{6,0},{1,3},{3,5},{5,7},{7,1},{8,10},{10,12},{12... | collective-permute-start | bytes 1253384 | tf_op jit(solution)/shard_map/ppermute | solution.py:199
  23.9 19.4 %collective-permute-start.2 = (bf16[1632,128]{1,0:T(8,128)(2,1)S(1)}, bf16[1632,128]{1,0:T(8,128)(2,1)S(1)}, u32[]{:S(2)}, u32[]{:S(2)}) collective-permute-start(bf16[1632,128]{1,0:T(8,128)(2,1)S(1)} %constant_dynamic-update-slice_fusion.refs_0_), channel_id=1, source_target_pairs={{0,4},{2,6},{4,0},{6,2},{1,5},{3,7},{5,1},{7,3},{8,12},{10,14},{12... | collective-permute-start | bytes 1253384 | tf_op jit(solution)/shard_map/ppermute | solution.py:199
  26.7 17.2 %collective-permute-start.3 = (bf16[1632,128]{1,0:T(8,128)(2,1)S(1)}, bf16[1632,128]{1,0:T(8,128)(2,1)S(1)}, u32[]{:S(2)}, u32[]{:S(2)}) collective-permute-start(bf16[1632,128]{1,0:T(8,128)(2,1)S(1)} %constant_dynamic-update-slice_fusion.refs_0_), channel_id=1, source_target_pairs={{0,6},{2,0},{4,2},{6,4},{1,7},{3,1},{5,3},{7,5},{8,14},{10,8},{12,... | collective-permute-start | bytes 1253384 | tf_op jit(solution)/shard_map/ppermute | solution.py:199
  28.1 15.8 %collective-permute-start.11 = (bf16[2240,128]{1,0:T(8,128)(2,1)S(1)}, bf16[2240,128]{1,0:T(8,128)(2,1)S(1)}, u32[]{:S(2)}, u32[]{:S(2)}) collective-permute-start(bf16[2240,128]{1,0:T(8,128)(2,1)S(1)} %collective-permute-done.10.refs_1_), channel_id=1, source_target_pairs={{0,16},{8,120},{16,32},{24,8},{32,48},{40,24},{48,64},{56,40},{64,... | collective-permute-start | bytes 1720328 | tf_op jit(solution)/shard_map/ppermute | solution.py:205
  30.0 16.3 %collective-permute-start.4 = (bf16[1632,128]{1,0:T(8,128)(2,1)S(1)}, bf16[1632,128]{1,0:T(8,128)(2,1)S(1)}, u32[]{:S(2)}, u32[]{:S(2)}) collective-permute-start(bf16[1632,128]{1,0:T(8,128)(2,1)S(1)} %constant_dynamic-update-slice_fusion.refs_0_), channel_id=1, source_target_pairs={{0,8},{8,0},{1,9},{9,1},{2,10},{10,2},{3,11},{11,3},{4,12},{12,4},... | collective-permute-start | bytes 1253384 | tf_op jit(solution)/shard_map/ppermute | solution.py:199
  43.3 3.1 %collective-permute-start.5 = (bf16[1632,128]{1,0:T(8,128)(2,1)S(1)}, bf16[1632,128]{1,0:T(8,128)(2,1)S(1)}, u32[]{:S(2)}, u32[]{:S(2)}) collective-permute-start(bf16[1632,128]{1,0:T(8,128)(2,1)S(1)} %collective-permute-done.1.refs_1_), channel_id=1, source_target_pairs={{0,8},{8,0},{1,9},{9,1},{2,10},{10,2},{3,11},{11,3},{4,12},{12,4},... | collective-permute-start | bytes 1253384 | tf_op jit(solution)/shard_map/ppermute | solution.py:199
  43.3 3.1 %collective-permute-start.6 = (bf16[1632,128]{1,0:T(8,128)(2,1)S(1)}, bf16[1632,128]{1,0:T(8,128)(2,1)S(1)}, u32[]{:S(2)}, u32[]{:S(2)}) collective-permute-start(bf16[1632,128]{1,0:T(8,128)(2,1)S(1)} %collective-permute-done.2.refs_2_), channel_id=1, source_target_pairs={{0,8},{8,0},{1,9},{9,1},{2,10},{10,2},{3,11},{11,3},{4,12},{12,4},... | collective-permute-start | bytes 1253384 | tf_op jit(solution)/shard_map/ppermute | solution.py:199
  43.9 2.5 %collective-permute-start.7 = (bf16[1632,128]{1,0:T(8,128)(2,1)S(1)}, bf16[1632,128]{1,0:T(8,128)(2,1)S(1)}, u32[]{:S(2)}, u32[]{:S(2)}) collective-permute-start(bf16[1632,128]{1,0:T(8,128)(2,1)S(1)} %collective-permute-done.3.refs_3_), channel_id=1, source_target_pairs={{0,8},{8,0},{1,9},{9,1},{2,10},{10,2},{3,11},{11,3},{4,12},{12,4},... | collective-permute-start | bytes 1253384 | tf_op jit(solution)/shard_map/ppermute | solution.py:199
  43.9 10.4 %collective-permute-start.12 = (bf16[2240,128]{1,0:T(8,128)(2,1)S(1)}, bf16[2240,128]{1,0:T(8,128)(2,1)S(1)}, u32[]{:S(2)}, u32[]{:S(2)}) collective-permute-start(bf16[2240,128]{1,0:T(8,128)(2,1)S(1)} %collective-permute-done.11.refs_2_), channel_id=1, source_target_pairs={{0,16},{8,120},{16,32},{24,8},{32,48},{40,24},{48,64},{56,40},{64,... | collective-permute-start | bytes 1720328 | tf_op jit(solution)/shard_map/ppermute | solution.py:205
  48.3 1.6 %copy-start = (bf16[2048,768]{1,0:T(8,128)(2,1)}, bf16[2048,768]{1,0:T(8,128)(2,1)S(1)}, u32[]{:S(2)}) copy-start(bf16[2048,768]{1,0:T(8,128)(2,1)S(1)} %get-tuple-element.25) | copy-start | bytes 9437188
  54.4 10.0 %collective-permute-start.13 = (bf16[1120,128]{1,0:T(8,128)(2,1)S(1)}, bf16[1120,128]{1,0:T(8,128)(2,1)S(1)}, u32[]{:S(2)}, u32[]{:S(2)}) collective-permute-start(bf16[1120,128]{1,0:T(8,128)(2,1)S(1)} %slice.37), channel_id=1, source_target_pairs={{0,16},{8,120},{16,32},{24,8},{32,48},{40,24},{48,64},{56,40},{64,... | collective-permute-start | bytes 860168 | tf_op jit(solution)/shard_map/ppermute | solution.py:205
  67.5 6.6 %collective-permute-start.14 = (bf16[8,128,512]{2,1,0:T(8,128)(2,1)}, bf16[8,128,512]{2,1,0:T(8,128)(2,1)}, u32[]{:S(2)}, u32[]{:S(2)}) collective-permute-start(bf16[8,128,512]{2,1,0:T(8,128)(2,1)} %slice_bitcast_fusion), channel_id=1, source_target_pairs={{0,8},{8,0},{1,9},{9,1},{2,10},{10,2},{3,11},{11,3},{4,12},{12,4},... | collective-permute-start | bytes 3145736 | tf_op jit(solution)/shard_map/ppermute | solution.py:199
  74.0 6.4 %collective-permute-start.19 = (bf16[8,2,24,512]{3,2,1,0:T(8,128)(2,1)S(1)}, bf16[8,2,24,512]{3,2,1,0:T(8,128)(2,1)S(1)}, u32[]{:S(2)}, u32[]{:S(2)}) collective-permute-start(bf16[8,2,24,512]{3,2,1,0:T(8,128)(2,1)S(1)} %bitcast.35), channel_id=1, source_target_pairs={{0,8},{8,0},{1,9},{9,1},{2,10},{10,2},{3,11},{11,3},{4,12},{12,4},... | collective-permute-start | bytes 1179656 | tf_op jit(solution)/shard_map/ppermute | solution.py:199
  76.5 13.9 %collective-permute-start.15 = (bf16[2,128,512]{2,1,0:T(8,128)(2,1)S(1)}, bf16[2,128,512]{2,1,0:T(8,128)(2,1)S(1)}, u32[]{:S(2)}, u32[]{:S(2)}) collective-permute-start(bf16[2,128,512]{2,1,0:T(8,128)(2,1)S(1)} %get-tuple-element.26), channel_id=1, source_target_pairs={{0,6},{2,0},{4,2},{6,4},{1,7},{3,1},{5,3},{7,5},{8,14},{10,8},{12,... | collective-permute-start | bytes 786440 | tf_op jit(solution)/shard_map/ppermute | solution.py:199
  78.6 11.9 %collective-permute-start.16 = (bf16[2,128,512]{2,1,0:T(8,128)(2,1)S(1)}, bf16[2,128,512]{2,1,0:T(8,128)(2,1)S(1)}, u32[]{:S(2)}, u32[]{:S(2)}) collective-permute-start(bf16[2,128,512]{2,1,0:T(8,128)(2,1)S(1)} %get-tuple-element.28), channel_id=1, source_target_pairs={{0,4},{2,6},{4,0},{6,2},{1,5},{3,7},{5,1},{7,3},{8,12},{10,14},{12... | collective-permute-start | bytes 786440 | tf_op jit(solution)/shard_map/ppermute | solution.py:199
  79.7 14.4 %collective-permute-start.17 = (bf16[2,128,512]{2,1,0:T(8,128)(2,1)S(1)}, bf16[2,128,512]{2,1,0:T(8,128)(2,1)S(1)}, u32[]{:S(2)}, u32[]{:S(2)}) collective-permute-start(bf16[2,128,512]{2,1,0:T(8,128)(2,1)S(1)} %get-tuple-element.27), channel_id=1, source_target_pairs={{0,2},{2,4},{4,6},{6,0},{1,3},{3,5},{5,7},{7,1},{8,10},{10,12},{12... | collective-permute-start | bytes 786440 | tf_op jit(solution)/shard_map/ppermute | solution.py:199
  81.2 17.7 %all-to-all-start = ((bf16[8,2,24,512]{3,2,1,0:T(8,128)(2,1)}), bf16[8,2,24,512]{3,2,1,0:T(8,128)(2,1)S(1)}, u32[]{:S(2)}, u32[]{:S(2)}) async-start(bf16[8,2,24,512]{3,2,1,0:T(8,128)(2,1)} %fusion.1), calls=%async_computation | async-start | bytes 786432 | tf_op jit(solution)/shard_map/all_to_all | solution.py:244
  95.3 11.1 %collective-permute-start.18 = (bf16[128,512]{1,0:T(8,128)(2,1)S(1)}, bf16[128,512]{1,0:T(8,128)(2,1)S(1)}, u32[]{:S(2)}, u32[]{:S(2)}) collective-permute-start(bf16[128,512]{1,0:T(8,128)(2,1)S(1)} %fusion.5), channel_id=1, source_target_pairs={{0,1},{1,0},{2,3},{3,2},{4,5},{5,4},{6,7},{7,6},{8,9},{9,8},{10,11... | collective-permute-start | bytes 393224 | tf_op jit(solution)/shard_map/ppermute | solution.py:199
  99.7 15.7 %all-to-all-start.1 = ((bf16[16,24,512]{2,1,0:T(8,128)(2,1)}), bf16[16,24,512]{2,1,0:T(8,128)(2,1)S(1)}, u32[]{:S(2)}, u32[]{:S(2)}) async-start(bf16[16,24,512]{2,1,0:T(8,128)(2,1)} %bitcast.11), calls=%async_computation.1 | async-start | bytes 786432 | tf_op jit(solution)/shard_map/all_to_all | solution.py:247
  (1 other events, 1.0 us)

commit v4 on v3

v4 whole, which is shorter than its diff:
```python
import functools

import jax
import jax.numpy as jnp
from jax import lax
from jax.experimental import pallas as pl
from jax.experimental.pallas import tpu as pltpu
from jax.sharding import Mesh, PartitionSpec as P


LOG2E = 1.4426950408889634
PTS = 128
FEAT = 512
HID = 768
ROW_MSG = 816
MSG = 560
ROW_CHUNK = 512
ALL = ("yh", "z", "c", "x", "yl")
VMEM = pl.BlockSpec(memory_space=pltpu.VMEM)
SMEM = pl.BlockSpec(memory_space=pltpu.SMEM)


def prepare_kernel(n, lsq_ref, proj_ref, *refs):
    bundles, (hr, rf, la, ai) = refs[:n], refs[n:]
    half = 0.5 * LOG2E / lsq_ref[0]
    lane = lax.broadcasted_iota(jnp.int32, (PTS, 128), 1)
    for dx in range(n):
        ref = bundles[dx]
        for dy in range(2):
            at = (dx * 2 + dy) * PTS
            here = slice(at, at + PTS)
            base = dy * ROW_MSG
            for k in range(6):
                hr[here, k * 128 : (k + 1) * 128] = ref[base + k * 128 : base + (k + 1) * 128, :]
            fac = ref[base + HID : base + ROW_MSG, :].astype(jnp.float32)
            sq = fac[33:34] + fac[34:35] + fac[35:36]
            swapped = jnp.concatenate(
                [
                    fac[0:1] * 0.5,
                    fac[17:33] * (-1 / 64),
                    fac[1:17] * (-1 / 64),
                    sq * half,
                    jnp.zeros((94, 128), jnp.float32),
                ],
                axis=0,
            ).T
            ai[here, :] = jnp.broadcast_to(swapped[:, 33:34], (PTS, 128))
            la[here, :] = jnp.where(lane < 33, swapped, 0.0).astype(jnp.bfloat16)
    for r in range(rf.shape[0] // ROW_CHUNK):
        here = slice(r * ROW_CHUNK, (r + 1) * ROW_CHUNK)
        rf[here, :] = jnp.dot(
            hr[here, :], proj_ref[...], preferred_element_type=jnp.float32
        ).astype(jnp.bfloat16)


def prepare(bundles, projection, lsq):
    n = len(bundles)
    r = 2 * n * PTS
    return pl.pallas_call(
        functools.partial(prepare_kernel, n),
        out_shape=(
            jax.ShapeDtypeStruct((r, HID), jnp.bfloat16),
            jax.ShapeDtypeStruct((r, FEAT), jnp.bfloat16),
            jax.ShapeDtypeStruct((r, 128), jnp.bfloat16),
            jax.ShapeDtypeStruct((r, 128), jnp.float32),
        ),
        in_specs=[SMEM, VMEM] + [VMEM] * n,
        out_specs=(VMEM,) * 4,
        cost_estimate=pl.CostEstimate(
            flops=2 * r * HID * FEAT, bytes_accessed=r * FEAT, transcendentals=0
        ),
        compiler_params=pltpu.CompilerParams(vmem_limit_bytes=10 * 1024 * 1024),
        name="prepare",
    )(lsq, projection, *bundles)


def chunk_kernel(n, first, last, amp_ref, lsq_ref, *refs):
    sides, refs = (refs[0:3], refs[3:6]), refs[6:]
    if not first:
        acc_in, rs_in = refs[:2]
        refs = refs[2:]
    cols_refs = refs[:n]
    refs = refs[n:]
    if last:
        near_ref, far_ref, cf, cfac = refs
    else:
        acc, rs, cf, cfac = refs
    rows, width = sides[0][0].shape[0], cf.shape[0]
    c1 = LOG2E / lsq_ref[0]
    half = 0.5 * c1
    at = 0
    for ref in cols_refs:
        for base in range(0, ref.shape[0], MSG):
            for k in range(4):
                cf[at : at + PTS, k * 128 : (k + 1) * 128] = ref[
                    base + k * 128 : base + (k + 1) * 128, :
                ]
            cfac[0:48, at : at + PTS] = ref[base + FEAT : base + MSG, :]
            at += PTS
    cfac[48:, :] = jnp.zeros((80, width), jnp.bfloat16)
    f3 = cfac[32:40, :].astype(jnp.float32)
    bj = (f3[1:2] + f3[2:3] + f3[3:4]) * half - jnp.log2(
        jnp.full((1, width), amp_ref[0], jnp.float32)
    )
    for r in range(2 * rows // ROW_CHUNK):
        here = slice(r * ROW_CHUNK, (r + 1) * ROW_CHUNK)
        side, inside = divmod(r * ROW_CHUNK, rows)
        local = slice(inside, inside + ROW_CHUNK)
        rf, la, ai = sides[side]
        inner = lax.dot_general(
            rf[local, :], cf[...], (((1,), (1,)), ((), ())), preferred_element_type=jnp.float32
        )
        gmat = jnp.dot(la[local, :], cfac[...], preferred_element_type=jnp.float32)
        a = jnp.concatenate([ai[local, :]] * (width // 128), axis=1)
        w = gmat * jnp.exp2(inner * c1 - a - bj)
        total = w[:, 0:128]
        for q in range(1, width // 128):
            total = total + w[:, q * 128 : (q + 1) * 128]
        moved = jnp.dot(w.astype(jnp.bfloat16), cf[...], preferred_element_type=jnp.float32)
        if not first:
            total = rs_in[here, :] + total
            moved = acc_in[here, :] + moved
        if last:
            rowsum = jnp.sum(total, axis=1, keepdims=True)
            diff = (2.0 / lsq_ref[0]) * (moved - rowsum * rf[local, :].astype(jnp.float32))
            (near_ref, far_ref)[side][local, :] = diff.astype(jnp.bfloat16)
        else:
            rs[here, :] = total
            acc[here, :] = moved


def chunk(sums, prepared, cols, amp, lsq, last):
    r = 2 * prepared[0].shape[0]
    c = sum(x.shape[0] for x in cols) // MSG * PTS
    first = sums is None
    sums_shape = (
        jax.ShapeDtypeStruct((r, FEAT), jnp.float32),
        jax.ShapeDtypeStruct((r, 128), jnp.float32),
    )
    scratch = [pltpu.VMEM((c, FEAT), jnp.bfloat16), pltpu.VMEM((128, c), jnp.bfloat16)]
    if last:
        out_shape, out_specs = (jax.ShapeDtypeStruct((r // 2, FEAT), jnp.bfloat16),) * 2, (VMEM, VMEM)
    else:
        out_shape, out_specs = sums_shape, (VMEM, VMEM)
    operands = (amp, lsq, *prepared) + (() if first else tuple(sums)) + tuple(cols)
    return pl.pallas_call(
        functools.partial(chunk_kernel, len(cols), first, last),
        out_shape=out_shape,
        in_specs=[SMEM, SMEM] + [VMEM] * (len(operands) - 2),
        out_specs=out_specs,
        scratch_shapes=scratch,
        cost_estimate=pl.CostEstimate(
            flops=2 * r * c * 1280, bytes_accessed=4 * r * FEAT, transcendentals=r * c
        ),
        compiler_params=pltpu.CompilerParams(vmem_limit_bytes=10 * 1024 * 1024),
        name="chunk",
    )(*operands)


def message_kernel(hidden_ref, proj_ref, alpha_ref, probes_ref, out_ref, row_ref):
    feats = jnp.dot(hidden_ref[...], proj_ref[...], preferred_element_type=jnp.float32).astype(
        jnp.bfloat16
    )
    feat_f = feats.astype(jnp.float32)
    for k in range(4):
        out_ref[k * 128 : (k + 1) * 128, :] = feats[:, k * 128 : (k + 1) * 128]
    sq = jnp.sum(feat_f * feat_f, axis=1, keepdims=True)
    hi = sq.astype(jnp.bfloat16).astype(jnp.float32)
    mid = (sq - hi).astype(jnp.bfloat16).astype(jnp.float32)
    low = sq - hi - mid
    wide = jnp.concatenate([hi, mid, low, jnp.zeros((PTS, 125), jnp.float32)], axis=1).T
    fac = jnp.concatenate(
        [alpha_ref[...].astype(jnp.float32), probes_ref[...].astype(jnp.float32), wide[0:15]],
        axis=0,
    )
    out_ref[FEAT:MSG, :] = fac.astype(jnp.bfloat16)
    for k in range(6):
        row_ref[k * 128 : (k + 1) * 128, :] = hidden_ref[:, k * 128 : (k + 1) * 128]
    row_ref[HID:ROW_MSG, :] = fac.astype(jnp.bfloat16)


def message(hidden, projection, alpha, probe_pairs):
    return pl.pallas_call(
        message_kernel,
        out_shape=(
            jax.ShapeDtypeStruct((MSG, 128), jnp.bfloat16),
            jax.ShapeDtypeStruct((ROW_MSG, 128), jnp.bfloat16),
        ),
        in_specs=[VMEM] * 4,
        out_specs=(VMEM, VMEM),
        name="message",
    )(hidden, projection, alpha.reshape(1, PTS), probe_pairs.T)


def halve_kernel(partial_ref, mine_ref, other_ref):
    first = lax.axis_index("c") == 0
    for yh in range(2):
        for z in range(8):
            at = (yh * 8 + z) * 48
            a, b = partial_ref[at : at + 24, :], partial_ref[at + 24 : at + 48, :]
            mine_ref[z, yh] = jnp.where(first, a, b)
            other_ref[z, yh] = jnp.where(first, b, a)


def halve(partial):
    half = jax.ShapeDtypeStruct((8, 2, 24, FEAT), jnp.bfloat16)
    return pl.pallas_call(
        halve_kernel,
        out_shape=(half, half),
        in_specs=[VMEM],
        out_specs=(VMEM, VMEM),
        compiler_params=pltpu.CompilerParams(vmem_limit_bytes=10 * 1024 * 1024),
        name="halve",
    )(partial)


def spread_kernel(got_ref, out_ref):
    for yh in range(2):
        total = got_ref[0, yh].astype(jnp.float32)
        for z in range(1, 8):
            total = total + got_ref[z, yh].astype(jnp.float32)
        for k in range(8):
            out_ref[yh * 8 + k] = total.astype(jnp.bfloat16)


def spread(got):
    return pl.pallas_call(
        spread_kernel,
        out_shape=jax.ShapeDtypeStruct((16, 24, FEAT), jnp.bfloat16),
        in_specs=[VMEM],
        out_specs=VMEM,
        compiler_params=pltpu.CompilerParams(vmem_limit_bytes=10 * 1024 * 1024),
        name="spread",
    )(got)


def shifted(x, axis, by):
    n = lax.axis_size(axis)
    return lax.ppermute(x, axis, [(i, (i + by) % n) for i in range(n)])


def apart(x):
    n = lax.axis_size("z")
    hops = [(2 * i + c, 2 * ((i + (1, -1)[c]) % n) + c) for i in range(n) for c in range(2)]
    return lax.ppermute(x, ("z", "c"), hops)


def steps(hidden, projection, alpha, probe_pairs, amplitude, length_sq):
    msg, row_msg = message(hidden, projection, alpha, probe_pairs)
    pair_rows = jnp.concatenate([row_msg, shifted(row_msg, "yl", 1)], axis=0)
    near = [pair_rows] + [shifted(pair_rows, "x", k) for k in (1, 2, 3)]
    far = [shifted(b, "c", 1) for b in near]
    hidden_near, *prepared = prepare(near, projection, length_sq)
    hidden_far, *more = prepare(far, projection, length_sq)
    prepared += more
    ring = [jnp.concatenate([msg, shifted(msg, "c", 1)], axis=0)]
    for k in range(1, 5):
        ring.append(apart(ring[-1] if k < 4 else ring[-1][:MSG]))
    crossed = [shifted(b, "yh", 1) for b in [msg] + ring[1:]]
    groups = [[msg, ring[1], crossed[0]], ring[2:4], crossed[1:3], [ring[4]] + crossed[3:5]]
    sums = None
    for k, group in enumerate(groups):
        sums = chunk(sums, prepared, group, amplitude, length_sq, k == 3)
    near_diff, far_diff = sums
    across_rows = (((0,), (0,)), ((), ()))
    partial = lax.dot_general(
        hidden_near, near_diff, across_rows, preferred_element_type=jnp.float32
    )
    partial += lax.dot_general(
        hidden_far, far_diff, across_rows, preferred_element_type=jnp.float32
    )
    partial = partial.astype(jnp.bfloat16)
    part = (near_diff + shifted(far_diff, "c", 1)).reshape(8, PTS, FEAT)
    owned = [shifted(part[2 * k : 2 * k + 2], "x", -k) for k in (1, 2, 3)]
    total = part[0:2].astype(jnp.float32)
    for piece in owned:
        total = total + piece.astype(jnp.float32)
    aside = shifted(total[1].astype(jnp.bfloat16), "yl", 1)
    grad_feat = (total[0] + aside.astype(jnp.float32)).astype(jnp.bfloat16)
    grad_hidden = jnp.dot(grad_feat, projection.T, preferred_element_type=jnp.float32).astype(
        jnp.bfloat16
    )
    mine, other = halve(partial)
    core_sum = mine + shifted(other, "c", 1)
    got = lax.all_to_all(core_sum, "z", 0, 0, tiled=True)
    got = lax.all_to_all(spread(got), ("yh", "x", "yl"), 0, 0, tiled=True)
    grad_proj = got.astype(jnp.float32).sum(axis=0)
    return grad_hidden, grad_proj


def solution(mesh):
    fine = Mesh(mesh.devices.reshape(2, 8, 2, 4, 2), ALL)
    placed = (P(ALL, None), P(), P(ALL), P(ALL, None), P(), P())
    return jax.shard_map(
        steps,
        mesh=fine,
        in_specs=placed,
        out_specs=(P(ALL, None), P(("yh", "z", "c"), None)),
        check_vma=False,
    )
```

time: 117 us -> 120 us (1.026)
  starting transfers between devices: 37.8 us -> 46.1 us
  local copies, waits for them, and re-layouts: 8.14 us -> 1.12 us
  waiting for transfers between devices: 41.7 us -> 45.6 us
  other arithmetic: 4.87 us -> 2.88 us
  matrix products: 4.76 us -> 3.08 us
    all_to_all x1, waiting for transfers between devices: 1.96 us -> 7.74 us  [steps(): got = lax.all_to_all(core_sum, 'z', 0, 0, tiled=True)]
    ppermute x16 -> x20, starting transfers between devices: 18.9 us -> 24 us  [shifted(): return lax.ppermute(x, axis, [(i, (i + by) % n) for i in range(n)])]
    unnamed x10 -> x5, local copies, waits for them, and re-layouts: 6.08 us -> 0.99 us
    ppermute x16 -> x20, waiting for transfers between devices: 29.9 us -> 26.4 us  [shifted(): return lax.ppermute(x, axis, [(i, (i + by) % n) for i in range(n)])]
    all_to_all x1, starting transfers between devices: 5.09 us -> 8.53 us  [steps(): got = lax.all_to_all(core_sum, 'z', 0, 0, tiled=True)]
    add x2, other arithmetic: 2.41 us -> 0.41 us  [the longest x1 0.28 us: steps(): part = (near_diff + shifted(far_diff, 'c', 1)).reshape(8, PTS, FEAT)]
    dot_general x1 -> x2, matrix products: 3.7 us -> 2.01 us  [the longest x1 1.01 us: steps(): lax.dot_general(hidden_near, near_diff, across_rows, preferred_element_ty...]
    ppermute x4, waiting for transfers between devices: 1.79 us -> 3.43 us  [apart(): return lax.ppermute(x, ('z', 'c'), hops)]
  transfers between devices with their start and end apart: 22 -> 26, of which waited for: 10 -> 10; matrix products, arithmetic and copies ran while one was open for 9% -> 5% of each run, Pallas kernels for 11% -> 10%
where the time goes in v4:
time: 120 us; the launch traced here: 119 us
  starting transfers between devices  46.1 us (38%)
  waiting for transfers between devices  45.6 us (38%)
  Pallas kernels  17.8 us (15%)
  matrix products  3.08 us (3%)
  other arithmetic  2.88 us (2%)
  between operations  2.14 us (2%)
    ppermute x20, waiting for transfers between devices, shifted(): return lax.ppermute(x, axis, [(i, (i + by) % n) for i in range(n)])  26.4 us
    ppermute x20, starting transfers between devices, shifted(): return lax.ppermute(x, axis, [(i, (i + by) % n) for i in range(n)])  24 us
    pallas_call x4, Pallas kernels, chunk(): pl.pallas_call(functools.partial(chunk_kernel, len(cols), first, last), o...  12.4 us
    all_to_all x1, starting transfers between devices, steps(): got = lax.all_to_all(core_sum, 'z', 0, 0, tiled=True)  8.53 us
    all_to_all x1, waiting for transfers between devices, steps(): got = lax.all_to_all(spread(got), ('yh', 'x', 'yl'), 0, 0, tiled=True)  8.06 us
    ppermute x4, starting transfers between devices, apart(): return lax.ppermute(x, ('z', 'c'), hops)  7.75 us
    all_to_all x1, waiting for transfers between devices, steps(): got = lax.all_to_all(core_sum, 'z', 0, 0, tiled=True)  7.74 us
    all_to_all x1, starting transfers between devices, steps(): got = lax.all_to_all(spread(got), ('yh', 'x', 'yl'), 0, 0, tiled=True)  5.82 us
  transfers between devices with their start and end apart: 26, of which 10 were waited for; matrix products, arithmetic and copies ran while one was open for 5% of the time, Pallas kernels for 10%

profile of v4, /device:TPU:32, one launch (start us, length us, event | category | flops | bytes accessed | tf_op | source)
XLA Modules:
  0.0 118.8 jit_solution(3504462941195783979)
XLA Ops:
  0.6 2.4 %message.1 = (bf16[560,128]{1,0:T(8,128)(2,1)}, bf16[816,128]{1,0:T(8,128)(2,1)}) custom-call(bf16[128,768]{1,0:T(8,128)(2,1)} %hidden_ref.1, bf16[768,512]{1,0:T(8,128)(2,1)} %proj_ref.5, bf16[1,128]{1,0:T(2,128)(2,1)} %bitcast.26, bf16[32,128]{1,0:T(8,128)(2,1)} %bitcast.25), custom_call_target="tpu_custom_call" | custom-call | tf_op jit(solution)/shard_map/message/pallas_call | solution.py:183
  6.5 2.0 %collective-permute-start.9 = (bf16[1120,128]{1,0:T(8,128)(2,1)S(1)}, bf16[1120,128]{1,0:T(8,128)(2,1)S(1)}, u32[]{:S(2)}, u32[]{:S(2)}) collective-permute-start(bf16[1120,128]{1,0:T(8,128)(2,1)S(1)} %pad_maximum_fusion), channel_id=1, source_target_pairs={{0,16},{8,120},{16,32},{24,8},{32,48},{40,24},{48,64},{56,40},{64,... | collective-permute-start | bytes 860168 | tf_op jit(solution)/shard_map/ppermute | solution.py:245
  8.5 2.3 %collective-permute-done = bf16[816,128]{1,0:T(8,128)(2,1)S(1)} collective-permute-done((bf16[816,128]{1,0:T(8,128)(2,1)}, bf16[816,128]{1,0:T(8,128)(2,1)S(1)}, u32[]{:S(2)}, u32[]{:S(2)}) %collective-permute-start) | collective-permute-done | bytes 208928 | tf_op jit(solution)/shard_map/ppermute | solution.py:239
  12.4 2.7 %collective-permute-start.2 = (bf16[1632,128]{1,0:T(8,128)(2,1)S(1)}, bf16[1632,128]{1,0:T(8,128)(2,1)S(1)}, u32[]{:S(2)}, u32[]{:S(2)}) collective-permute-start(bf16[1632,128]{1,0:T(8,128)(2,1)S(1)} %constant_dynamic-update-slice_fusion.refs_0_), channel_id=1, source_target_pairs={{0,4},{2,6},{4,0},{6,2},{1,5},{3,7},{5,1},{7,3},{8,12},{10,14},{12... | collective-permute-start | bytes 1253384 | tf_op jit(solution)/shard_map/ppermute | solution.py:239
  16.6 1.9 %collective-permute-start.11 = (bf16[1120,128]{1,0:T(8,128)(2,1)S(1)}, bf16[1120,128]{1,0:T(8,128)(2,1)S(1)}, u32[]{:S(2)}, u32[]{:S(2)}) collective-permute-start(bf16[1120,128]{1,0:T(8,128)(2,1)S(1)} %collective-permute-done.9.refs_7_), channel_id=1, source_target_pairs={{0,16},{8,120},{16,32},{24,8},{32,48},{40,24},{48,64},{56,40},{64,... | collective-permute-start | bytes 860168 | tf_op jit(solution)/shard_map/ppermute | solution.py:245
  18.5 5.2 %collective-permute-done.1.refs_1_ = bf16[1632,128]{1,0:T(8,128)(2,1)S(1)} collective-permute-done((bf16[1632,128]{1,0:T(8,128)(2,1)S(1)}, bf16[1632,128]{1,0:T(8,128)(2,1)S(1)}, u32[]{:S(2)}, u32[]{:S(2)}) %collective-permute-start.1) | collective-permute-done | bytes 417824 | tf_op jit(solution)/shard_map/ppermute | solution.py:239
  23.7 9.6 %collective-permute-done.2.refs_2_ = bf16[1632,128]{1,0:T(8,128)(2,1)S(1)} collective-permute-done((bf16[1632,128]{1,0:T(8,128)(2,1)S(1)}, bf16[1632,128]{1,0:T(8,128)(2,1)S(1)}, u32[]{:S(2)}, u32[]{:S(2)}) %collective-permute-start.2) | collective-permute-done | bytes 417824 | tf_op jit(solution)/shard_map/ppermute | solution.py:239
  33.8 1.9 %collective-permute-start.12 = (bf16[1120,128]{1,0:T(8,128)(2,1)S(1)}, bf16[1120,128]{1,0:T(8,128)(2,1)S(1)}, u32[]{:S(2)}, u32[]{:S(2)}) collective-permute-start(bf16[1120,128]{1,0:T(8,128)(2,1)S(1)} %collective-permute-done.11.refs_8_), channel_id=1, source_target_pairs={{0,16},{8,120},{16,32},{24,8},{32,48},{40,24},{48,64},{56,40},{64,... | collective-permute-start | bytes 860168 | tf_op jit(solution)/shard_map/ppermute | solution.py:245
  37.0 3.4 %collective-permute-done.12.refs_9_ = bf16[1120,128]{1,0:T(8,128)(2,1)S(1)} collective-permute-done((bf16[1120,128]{1,0:T(8,128)(2,1)S(1)}, bf16[1120,128]{1,0:T(8,128)(2,1)S(1)}, u32[]{:S(2)}, u32[]{:S(2)}) %collective-permute-start.12) | collective-permute-done | bytes 286752 | tf_op jit(solution)/shard_map/ppermute | solution.py:245
  40.4 3.2 %collective-permute-start.10 = (bf16[560,128]{1,0:T(8,128)(2,1)}, bf16[560,128]{1,0:T(8,128)(2,1)S(1)}, u32[]{:S(2)}, u32[]{:S(2)}) collective-permute-start(bf16[560,128]{1,0:T(8,128)(2,1)} %get-tuple-element.29.refs_6_), channel_id=1, source_target_pairs={{0,128},{128,0},{1,129},{129,1},{2,130},{130,2},{3,131},{131,3},{4... | collective-permute-start | bytes 430088 | tf_op jit(solution)/shard_map/ppermute | solution.py:239
  45.2 3.2 %collective-permute-start.14 = (bf16[1120,128]{1,0:T(8,128)(2,1)S(1)}, bf16[1120,128]{1,0:T(8,128)(2,1)S(1)}, u32[]{:S(2)}, u32[]{:S(2)}) collective-permute-start(bf16[1120,128]{1,0:T(8,128)(2,1)S(1)} %collective-permute-done.11.refs_8_), channel_id=1, source_target_pairs={{0,128},{128,0},{1,129},{129,1},{2,130},{130,2},{3,131},{131,3},{4... | collective-permute-start | bytes 860168 | tf_op jit(solution)/shard_map/ppermute | solution.py:239
  48.4 1.9 %collective-permute-start.15 = (bf16[560,128]{1,0:T(8,128)(2,1)S(1)}, bf16[560,128]{1,0:T(8,128)(2,1)S(1)}, u32[]{:S(2)}, u32[]{:S(2)}) collective-permute-start(bf16[560,128]{1,0:T(8,128)(2,1)S(1)} %slice.42), channel_id=1, source_target_pairs={{0,16},{8,120},{16,32},{24,8},{32,48},{40,24},{48,64},{56,40},{64,... | collective-permute-start | bytes 430088 | tf_op jit(solution)/shard_map/ppermute | solution.py:245
  51.8 3.0 %chunk.4 = (f32[2048,512]{1,0:T(8,128)S(1)}, f32[2048,128]{1,0:T(8,128)S(1)}) custom-call(f32[1]{0:T(128)S(6)} %copy.9.amp_ref, f32[1]{0:T(128)S(6)} %copy.10.lsq_ref, bf16[1024,512]{1,0:T(8,128)(2,1)S(1)} %get-tuple-element.23.refs_0_, bf16[1024,128]{1,0:T(8,128)(2,1)S(1)} %get-tuple-element.24.refs_1_, f32[1024,128]{1,0:T(8,128)S(1)} %get-tuple-element.25.refs_2_, ...), custom_call_target="tpu_custom_call" | custom-call | flops 2684354560 | bytes 4194304 | tf_op jit(solution)/shard_map/chunk/pallas_call | solution.py:146
  54.8 3.0 %chunk.5 = (f32[2048,512]{1,0:T(8,128)S(1)}, f32[2048,128]{1,0:T(8,128)S(1)}) custom-call(f32[1]{0:T(128)S(6)} %copy.9.amp_ref, f32[1]{0:T(128)S(6)} %copy.10.lsq_ref, bf16[1024,512]{1,0:T(8,128)(2,1)S(1)} %get-tuple-element.23.refs_0_, bf16[1024,128]{1,0:T(8,128)(2,1)S(1)} %get-tuple-element.24.refs_1_, f32[1024,128]{1,0:T(8,128)S(1)} %get-tuple-element.25.refs_2_, ...), custom_call_target="tpu_custom_call" | custom-call | flops 2684354560 | bytes 4194304 | tf_op jit(solution)/shard_map/chunk/pallas_call | solution.py:146
  57.8 3.3 %collective-permute-start.17 = (bf16[560,128]{1,0:T(8,128)(2,1)S(1)}, bf16[560,128]{1,0:T(8,128)(2,1)S(1)}, u32[]{:S(2)}, u32[]{:S(2)}) collective-permute-start(bf16[560,128]{1,0:T(8,128)(2,1)S(1)} %collective-permute-done.15.refs_8_), channel_id=1, source_target_pairs={{0,128},{128,0},{1,129},{129,1},{2,130},{130,2},{3,131},{131,3},{4... | collective-permute-start | bytes 430088 | tf_op jit(solution)/shard_map/ppermute | solution.py:239
  62.2 3.0 %chunk.6 = (f32[2048,512]{1,0:T(8,128)S(1)}, f32[2048,128]{1,0:T(8,128)S(1)}) custom-call(f32[1]{0:T(128)S(6)} %copy.9.amp_ref, f32[1]{0:T(128)S(6)} %copy.10.lsq_ref, bf16[1024,512]{1,0:T(8,128)(2,1)S(1)} %get-tuple-element.23.refs_0_, bf16[1024,128]{1,0:T(8,128)(2,1)S(1)} %get-tuple-element.24.refs_1_, f32[1024,128]{1,0:T(8,128)S(1)} %get-tuple-element.25.refs_2_, ...), custom_call_target="tpu_custom_call" | custom-call | flops 2684354560 | bytes 4194304 | tf_op jit(solution)/shard_map/chunk/pallas_call | solution.py:146
  65.3 4.3 %collective-permute-done.17.refs_10_ = bf16[560,128]{1,0:T(8,128)(2,1)S(1)} collective-permute-done((bf16[560,128]{1,0:T(8,128)(2,1)S(1)}, bf16[560,128]{1,0:T(8,128)(2,1)S(1)}, u32[]{:S(2)}, u32[]{:S(2)}) %collective-permute-start.17) | collective-permute-done | bytes 143392 | tf_op jit(solution)/shard_map/ppermute | solution.py:239
  69.6 3.3 %chunk.7 = (bf16[1024,512]{1,0:T(8,128)(2,1)S(1)}, bf16[1024,512]{1,0:T(8,128)(2,1)S(1)}) custom-call(f32[1]{0:T(128)S(6)} %copy.9.amp_ref, f32[1]{0:T(128)S(6)} %copy.10.lsq_ref, bf16[1024,512]{1,0:T(8,128)(2,1)S(1)} %get-tuple-element.23.refs_0_, bf16[1024,128]{1,0:T(8,128)(2,1)S(1)} %get-tuple-element.24.refs_1_, ...), custom_call_target="tpu_custom_call" | custom-call | flops 2684354560 | bytes 4194304 | tf_op jit(solution)/shard_map/chunk/pallas_call | solution.py:146
  76.3 2.3 %collective-permute-start.19 = (bf16[2,128,512]{2,1,0:T(8,128)(2,1)S(1)}, bf16[2,128,512]{2,1,0:T(8,128)(2,1)S(1)}, u32[]{:S(2)}, u32[]{:S(2)}) collective-permute-start(bf16[2,128,512]{2,1,0:T(8,128)(2,1)S(1)} %bitcast.24), channel_id=1, source_target_pairs={{0,6},{2,0},{4,2},{6,4},{1,7},{3,1},{5,3},{7,5},{8,14},{10,8},{12,... | collective-permute-start | bytes 786440 | tf_op jit(solution)/shard_map/ppermute | solution.py:239
  81.2 8.5 %all-to-all-start = ((bf16[8,2,24,512]{3,2,1,0:T(8,128)(2,1)}), bf16[8,2,24,512]{3,2,1,0:T(8,128)(2,1)S(1)}, u32[]{:S(2)}, u32[]{:S(2)}) async-start(bf16[8,2,24,512]{3,2,1,0:T(8,128)(2,1)} %add.27), calls=%async_computation | async-start | bytes 786432 | tf_op jit(solution)/shard_map/all_to_all | solution.py:285
  90.0 3.7 %collective-permute-done.21 = bf16[2,128,512]{2,1,0:T(8,128)(2,1)S(1)} collective-permute-done((bf16[2,128,512]{2,1,0:T(8,128)(2,1)S(1)}, bf16[2,128,512]{2,1,0:T(8,128)(2,1)S(1)}, u32[]{:S(2)}, u32[]{:S(2)}) %collective-permute-start.21) | collective-permute-done | bytes 262176 | tf_op jit(solution)/shard_map/ppermute | solution.py:239
  94.7 7.7 %all-to-all-done.got_ref = bf16[8,2,24,512]{3,2,1,0:T(8,128)(2,1)S(1)} async-done(((bf16[8,2,24,512]{3,2,1,0:T(8,128)(2,1)}), bf16[8,2,24,512]{3,2,1,0:T(8,128)(2,1)S(1)}, u32[]{:S(2)}, u32[]{:S(2)}) %all-to-all-start) | async-done | bytes 393248 | tf_op jit(solution)/shard_map/all_to_all | solution.py:285
  103.2 5.8 %all-to-all-start.1 = ((bf16[16,24,512]{2,1,0:T(8,128)(2,1)}), bf16[16,24,512]{2,1,0:T(8,128)(2,1)S(1)}, u32[]{:S(2)}, u32[]{:S(2)}) async-start(bf16[16,24,512]{2,1,0:T(8,128)(2,1)} %spread.1), calls=%async_computation.1 | async-start | bytes 786432 | tf_op jit(solution)/shard_map/all_to_all | solution.py:286
  110.1 8.1 %all-to-all-done.1 = bf16[16,24,512]{2,1,0:T(8,128)(2,1)S(1)} async-done(((bf16[16,24,512]{2,1,0:T(8,128)(2,1)}), bf16[16,24,512]{2,1,0:T(8,128)(2,1)S(1)}, u32[]{:S(2)}, u32[]{:S(2)}) %all-to-all-start.1) | async-done | bytes 393248 | tf_op jit(solution)/shard_map/all_to_all | solution.py:286
  (54 shorter events, 20.9 us)
Async XLA Ops:
  3.0 7.8 %collective-permute-start = (bf16[816,128]{1,0:T(8,128)(2,1)}, bf16[816,128]{1,0:T(8,128)(2,1)S(1)}, u32[]{:S(2)}, u32[]{:S(2)}) collective-permute-start(bf16[816,128]{1,0:T(8,128)(2,1)} %get-tuple-element.22), channel_id=1, source_target_pairs={{0,1},{1,0},{2,3},{3,2},{4,5},{5,4},{6,7},{7,6},{8,9},{9,8},{10,11... | collective-permute-start | bytes 626696 | tf_op jit(solution)/shard_map/ppermute | solution.py:239
  6.5 10.1 %collective-permute-start.9 = (bf16[1120,128]{1,0:T(8,128)(2,1)S(1)}, bf16[1120,128]{1,0:T(8,128)(2,1)S(1)}, u32[]{:S(2)}, u32[]{:S(2)}) collective-permute-start(bf16[1120,128]{1,0:T(8,128)(2,1)S(1)} %pad_maximum_fusion), channel_id=1, source_target_pairs={{0,16},{8,120},{16,32},{24,8},{32,48},{40,24},{48,64},{56,40},{64,... | collective-permute-start | bytes 860168 | tf_op jit(solution)/shard_map/ppermute | solution.py:245
  10.9 12.8 %collective-permute-start.1 = (bf16[1632,128]{1,0:T(8,128)(2,1)S(1)}, bf16[1632,128]{1,0:T(8,128)(2,1)S(1)}, u32[]{:S(2)}, u32[]{:S(2)}) collective-permute-start(bf16[1632,128]{1,0:T(8,128)(2,1)S(1)} %constant_dynamic-update-slice_fusion.refs_0_), channel_id=1, source_target_pairs={{0,2},{2,4},{4,6},{6,0},{1,3},{3,5},{5,7},{7,1},{8,10},{10,12},{12... | collective-permute-start | bytes 1253384 | tf_op jit(solution)/shard_map/ppermute | solution.py:239
  12.4 20.9 %collective-permute-start.2 = (bf16[1632,128]{1,0:T(8,128)(2,1)S(1)}, bf16[1632,128]{1,0:T(8,128)(2,1)S(1)}, u32[]{:S(2)}, u32[]{:S(2)}) collective-permute-start(bf16[1632,128]{1,0:T(8,128)(2,1)S(1)} %constant_dynamic-update-slice_fusion.refs_0_), channel_id=1, source_target_pairs={{0,4},{2,6},{4,0},{6,2},{1,5},{3,7},{5,1},{7,3},{8,12},{10,14},{12... | collective-permute-start | bytes 1253384 | tf_op jit(solution)/shard_map/ppermute | solution.py:239
  15.2 18.1 %collective-permute-start.3 = (bf16[1632,128]{1,0:T(8,128)(2,1)S(1)}, bf16[1632,128]{1,0:T(8,128)(2,1)S(1)}, u32[]{:S(2)}, u32[]{:S(2)}) collective-permute-start(bf16[1632,128]{1,0:T(8,128)(2,1)S(1)} %constant_dynamic-update-slice_fusion.refs_0_), channel_id=1, source_target_pairs={{0,6},{2,0},{4,2},{6,4},{1,7},{3,1},{5,3},{7,5},{8,14},{10,8},{12,... | collective-permute-start | bytes 1253384 | tf_op jit(solution)/shard_map/ppermute | solution.py:239
  16.6 17.2 %collective-permute-start.11 = (bf16[1120,128]{1,0:T(8,128)(2,1)S(1)}, bf16[1120,128]{1,0:T(8,128)(2,1)S(1)}, u32[]{:S(2)}, u32[]{:S(2)}) collective-permute-start(bf16[1120,128]{1,0:T(8,128)(2,1)S(1)} %collective-permute-done.9.refs_7_), channel_id=1, source_target_pairs={{0,16},{8,120},{16,32},{24,8},{32,48},{40,24},{48,64},{56,40},{64,... | collective-permute-start | bytes 860168 | tf_op jit(solution)/shard_map/ppermute | solution.py:245
  18.5 26.2 %collective-permute-start.4 = (bf16[1632,128]{1,0:T(8,128)(2,1)S(1)}, bf16[1632,128]{1,0:T(8,128)(2,1)S(1)}, u32[]{:S(2)}, u32[]{:S(2)}) collective-permute-start(bf16[1632,128]{1,0:T(8,128)(2,1)S(1)} %constant_dynamic-update-slice_fusion.refs_0_), channel_id=1, source_target_pairs={{0,8},{8,0},{1,9},{9,1},{2,10},{10,2},{3,11},{11,3},{4,12},{12,4},... | collective-permute-start | bytes 1253384 | tf_op jit(solution)/shard_map/ppermute | solution.py:239
  23.7 21.5 %collective-permute-start.5 = (bf16[1632,128]{1,0:T(8,128)(2,1)S(1)}, bf16[1632,128]{1,0:T(8,128)(2,1)S(1)}, u32[]{:S(2)}, u32[]{:S(2)}) collective-permute-start(bf16[1632,128]{1,0:T(8,128)(2,1)S(1)} %collective-permute-done.1.refs_1_), channel_id=1, source_target_pairs={{0,8},{8,0},{1,9},{9,1},{2,10},{10,2},{3,11},{11,3},{4,12},{12,4},... | collective-permute-start | bytes 1253384 | tf_op jit(solution)/shard_map/ppermute | solution.py:239
  33.3 15.1 %collective-permute-start.6 = (bf16[1632,128]{1,0:T(8,128)(2,1)S(1)}, bf16[1632,128]{1,0:T(8,128)(2,1)S(1)}, u32[]{:S(2)}, u32[]{:S(2)}) collective-permute-start(bf16[1632,128]{1,0:T(8,128)(2,1)S(1)} %collective-permute-done.2.refs_2_), channel_id=1, source_target_pairs={{0,8},{8,0},{1,9},{9,1},{2,10},{10,2},{3,11},{11,3},{4,12},{12,4},... | collective-permute-start | bytes 1253384 | tf_op jit(solution)/shard_map/ppermute | solution.py:239
  33.3 17.0 %collective-permute-start.7 = (bf16[1632,128]{1,0:T(8,128)(2,1)S(1)}, bf16[1632,128]{1,0:T(8,128)(2,1)S(1)}, u32[]{:S(2)}, u32[]{:S(2)}) collective-permute-start(bf16[1632,128]{1,0:T(8,128)(2,1)S(1)} %collective-permute-done.3.refs_3_), channel_id=1, source_target_pairs={{0,8},{8,0},{1,9},{9,1},{2,10},{10,2},{3,11},{11,3},{4,12},{12,4},... | collective-permute-start | bytes 1253384 | tf_op jit(solution)/shard_map/ppermute | solution.py:239
  33.8 6.6 %collective-permute-start.12 = (bf16[1120,128]{1,0:T(8,128)(2,1)S(1)}, bf16[1120,128]{1,0:T(8,128)(2,1)S(1)}, u32[]{:S(2)}, u32[]{:S(2)}) collective-permute-start(bf16[1120,128]{1,0:T(8,128)(2,1)S(1)} %collective-permute-done.11.refs_8_), channel_id=1, source_target_pairs={{0,16},{8,120},{16,32},{24,8},{32,48},{40,24},{48,64},{56,40},{64,... | collective-permute-start | bytes 860168 | tf_op jit(solution)/shard_map/ppermute | solution.py:245
  40.4 11.3 %collective-permute-start.10 = (bf16[560,128]{1,0:T(8,128)(2,1)}, bf16[560,128]{1,0:T(8,128)(2,1)S(1)}, u32[]{:S(2)}, u32[]{:S(2)}) collective-permute-start(bf16[560,128]{1,0:T(8,128)(2,1)} %get-tuple-element.29.refs_6_), channel_id=1, source_target_pairs={{0,128},{128,0},{1,129},{129,1},{2,130},{130,2},{3,131},{131,3},{4... | collective-permute-start | bytes 430088 | tf_op jit(solution)/shard_map/ppermute | solution.py:239
  44.8 16.4 %collective-permute-start.13 = (bf16[1120,128]{1,0:T(8,128)(2,1)S(1)}, bf16[1120,128]{1,0:T(8,128)(2,1)S(1)}, u32[]{:S(2)}, u32[]{:S(2)}) collective-permute-start(bf16[1120,128]{1,0:T(8,128)(2,1)S(1)} %collective-permute-done.9.refs_7_), channel_id=1, source_target_pairs={{0,128},{128,0},{1,129},{129,1},{2,130},{130,2},{3,131},{131,3},{4... | collective-permute-start | bytes 860168 | tf_op jit(solution)/shard_map/ppermute | solution.py:239
  45.2 17.0 %collective-permute-start.14 = (bf16[1120,128]{1,0:T(8,128)(2,1)S(1)}, bf16[1120,128]{1,0:T(8,128)(2,1)S(1)}, u32[]{:S(2)}, u32[]{:S(2)}) collective-permute-start(bf16[1120,128]{1,0:T(8,128)(2,1)S(1)} %collective-permute-done.11.refs_8_), channel_id=1, source_target_pairs={{0,128},{128,0},{1,129},{129,1},{2,130},{130,2},{3,131},{131,3},{4... | collective-permute-start | bytes 860168 | tf_op jit(solution)/shard_map/ppermute | solution.py:239
  48.4 9.4 %collective-permute-start.15 = (bf16[560,128]{1,0:T(8,128)(2,1)S(1)}, bf16[560,128]{1,0:T(8,128)(2,1)S(1)}, u32[]{:S(2)}, u32[]{:S(2)}) collective-permute-start(bf16[560,128]{1,0:T(8,128)(2,1)S(1)} %slice.42), channel_id=1, source_target_pairs={{0,16},{8,120},{16,32},{24,8},{32,48},{40,24},{48,64},{56,40},{64,... | collective-permute-start | bytes 430088 | tf_op jit(solution)/shard_map/ppermute | solution.py:245
  50.3 19.3 %collective-permute-start.16 = (bf16[1120,128]{1,0:T(8,128)(2,1)S(1)}, bf16[1120,128]{1,0:T(8,128)(2,1)S(1)}, u32[]{:S(2)}, u32[]{:S(2)}) collective-permute-start(bf16[1120,128]{1,0:T(8,128)(2,1)S(1)} %collective-permute-done.12.refs_9_), channel_id=1, source_target_pairs={{0,128},{128,0},{1,129},{129,1},{2,130},{130,2},{3,131},{131,3},{4... | collective-permute-start | bytes 860168 | tf_op jit(solution)/shard_map/ppermute | solution.py:239
  57.8 11.7 %collective-permute-start.17 = (bf16[560,128]{1,0:T(8,128)(2,1)S(1)}, bf16[560,128]{1,0:T(8,128)(2,1)S(1)}, u32[]{:S(2)}, u32[]{:S(2)}) collective-permute-start(bf16[560,128]{1,0:T(8,128)(2,1)S(1)} %collective-permute-done.15.refs_8_), channel_id=1, source_target_pairs={{0,128},{128,0},{1,129},{129,1},{2,130},{130,2},{3,131},{131,3},{4... | collective-permute-start | bytes 430088 | tf_op jit(solution)/shard_map/ppermute | solution.py:239
  75.3 5.0 %collective-permute-start.23 = (bf16[8,2,24,512]{3,2,1,0:T(8,128)(2,1)S(1)}, bf16[8,2,24,512]{3,2,1,0:T(8,128)(2,1)S(1)}, u32[]{:S(2)}, u32[]{:S(2)}) collective-permute-start(bf16[8,2,24,512]{3,2,1,0:T(8,128)(2,1)S(1)} %get-tuple-element.41), channel_id=1, source_target_pairs={{0,8},{8,0},{1,9},{9,1},{2,10},{10,2},{3,11},{11,3},{4,12},{12,4},... | collective-permute-start | bytes 1179656 | tf_op jit(solution)/shard_map/ppermute | solution.py:239
  76.3 13.7 %collective-permute-start.19 = (bf16[2,128,512]{2,1,0:T(8,128)(2,1)S(1)}, bf16[2,128,512]{2,1,0:T(8,128)(2,1)S(1)}, u32[]{:S(2)}, u32[]{:S(2)}) collective-permute-start(bf16[2,128,512]{2,1,0:T(8,128)(2,1)S(1)} %bitcast.24), channel_id=1, source_target_pairs={{0,6},{2,0},{4,2},{6,4},{1,7},{3,1},{5,3},{7,5},{8,14},{10,8},{12,... | collective-permute-start | bytes 786440 | tf_op jit(solution)/shard_map/ppermute | solution.py:239
  78.5 11.5 %collective-permute-start.20 = (bf16[2,128,512]{2,1,0:T(8,128)(2,1)S(1)}, bf16[2,128,512]{2,1,0:T(8,128)(2,1)S(1)}, u32[]{:S(2)}, u32[]{:S(2)}) collective-permute-start(bf16[2,128,512]{2,1,0:T(8,128)(2,1)S(1)} %bitcast.23), channel_id=1, source_target_pairs={{0,4},{2,6},{4,0},{6,2},{1,5},{3,7},{5,1},{7,3},{8,12},{10,14},{12... | collective-permute-start | bytes 786440 | tf_op jit(solution)/shard_map/ppermute | solution.py:239
  79.7 14.0 %collective-permute-start.21 = (bf16[2,128,512]{2,1,0:T(8,128)(2,1)S(1)}, bf16[2,128,512]{2,1,0:T(8,128)(2,1)S(1)}, u32[]{:S(2)}, u32[]{:S(2)}) collective-permute-start(bf16[2,128,512]{2,1,0:T(8,128)(2,1)S(1)} %bitcast.22), channel_id=1, source_target_pairs={{0,2},{2,4},{4,6},{6,0},{1,3},{3,5},{5,7},{7,1},{8,10},{10,12},{12... | collective-permute-start | bytes 786440 | tf_op jit(solution)/shard_map/ppermute | solution.py:239
  81.2 21.2 %all-to-all-start = ((bf16[8,2,24,512]{3,2,1,0:T(8,128)(2,1)}), bf16[8,2,24,512]{3,2,1,0:T(8,128)(2,1)S(1)}, u32[]{:S(2)}, u32[]{:S(2)}) async-start(bf16[8,2,24,512]{3,2,1,0:T(8,128)(2,1)} %add.27), calls=%async_computation | async-start | bytes 786432 | tf_op jit(solution)/shard_map/all_to_all | solution.py:285
  93.8 15.2 %collective-permute-start.22 = (bf16[128,512]{1,0:T(8,128)(2,1)S(1)}, bf16[128,512]{1,0:T(8,128)(2,1)S(1)}, u32[]{:S(2)}, u32[]{:S(2)}) collective-permute-start(bf16[128,512]{1,0:T(8,128)(2,1)S(1)} %fusion.5), channel_id=1, source_target_pairs={{0,1},{1,0},{2,3},{3,2},{4,5},{5,4},{6,7},{7,6},{8,9},{9,8},{10,11... | collective-permute-start | bytes 393224 | tf_op jit(solution)/shard_map/ppermute | solution.py:239
  103.2 15.0 %all-to-all-start.1 = ((bf16[16,24,512]{2,1,0:T(8,128)(2,1)}), bf16[16,24,512]{2,1,0:T(8,128)(2,1)S(1)}, u32[]{:S(2)}, u32[]{:S(2)}) async-start(bf16[16,24,512]{2,1,0:T(8,128)(2,1)} %spread.1), calls=%async_computation.1 | async-start | bytes 786432 | tf_op jit(solution)/shard_map/all_to_all | solution.py:286
  (4 other events, 55.6 us)

commit v5 on v4

--- a/solution.py
+++ b/solution.py
@@ -192,18 +192,36 @@
     )(hidden, projection, alpha.reshape(1, PTS), probe_pairs.T)
 
 
+def merge_kernel(near_ref, far_ref, *out_refs):
+    for k, ref in enumerate(out_refs):
+        for y in range(2):
+            here = slice((2 * k + y) * PTS, (2 * k + y + 1) * PTS)
+            both = near_ref[here, :].astype(jnp.float32) + far_ref[here, :].astype(jnp.float32)
+            ref[y] = both.astype(jnp.bfloat16)
+
+
+def merge(near, far):
+    n = near.shape[0] // (2 * PTS)
+    return pl.pallas_call(
+        merge_kernel,
+        out_shape=(jax.ShapeDtypeStruct((2, PTS, FEAT), jnp.bfloat16),) * n,
+        in_specs=[VMEM, VMEM],
+        out_specs=(VMEM,) * n,
+        compiler_params=pltpu.CompilerParams(vmem_limit_bytes=10 * 1024 * 1024),
+        name="merge",
+    )(near, far)
+
+
 def halve_kernel(partial_ref, mine_ref, other_ref):
     first = lax.axis_index("c") == 0
-    for yh in range(2):
-        for z in range(8):
-            at = (yh * 8 + z) * 48
-            a, b = partial_ref[at : at + 24, :], partial_ref[at + 24 : at + 48, :]
-            mine_ref[z, yh] = jnp.where(first, a, b)
-            other_ref[z, yh] = jnp.where(first, b, a)
+    for k in range(mine_ref.shape[0]):
+        a, b = partial_ref[k * 48 : k * 48 + 24, :], partial_ref[k * 48 + 24 : k * 48 + 48, :]
+        mine_ref[k] = jnp.where(first, a, b)
+        other_ref[k] = jnp.where(first, b, a)
 
 
 def halve(partial):
-    half = jax.ShapeDtypeStruct((8, 2, 24, FEAT), jnp.bfloat16)
+    half = jax.ShapeDtypeStruct((16, 24, FEAT), jnp.bfloat16)
     return pl.pallas_call(
         halve_kernel,
         out_shape=(half, half),
@@ -215,18 +233,17 @@
 
 
 def spread_kernel(got_ref, out_ref):
-    for yh in range(2):
-        total = got_ref[0, yh].astype(jnp.float32)
-        for z in range(1, 8):
-            total = total + got_ref[z, yh].astype(jnp.float32)
-        for k in range(8):
-            out_ref[yh * 8 + k] = total.astype(jnp.bfloat16)
+    total = got_ref[0].astype(jnp.float32)
+    for z in range(1, got_ref.shape[0]):
+        total = total + got_ref[z].astype(jnp.float32)
+    for k in range(out_ref.shape[0]):
+        out_ref[k] = total.astype(jnp.bfloat16)
 
 
 def spread(got):
     return pl.pallas_call(
         spread_kernel,
-        out_shape=jax.ShapeDtypeStruct((16, 24, FEAT), jnp.bfloat16),
+        out_shape=jax.ShapeDtypeStruct((8, 24, FEAT), jnp.bfloat16),
         in_specs=[VMEM],
         out_specs=VMEM,
         compiler_params=pltpu.CompilerParams(vmem_limit_bytes=10 * 1024 * 1024),
@@ -270,9 +287,9 @@
         hidden_far, far_diff, across_rows, preferred_element_type=jnp.float32
     )
     partial = partial.astype(jnp.bfloat16)
-    part = (near_diff + shifted(far_diff, "c", 1)).reshape(8, PTS, FEAT)
-    owned = [shifted(part[2 * k : 2 * k + 2], "x", -k) for k in (1, 2, 3)]
-    total = part[0:2].astype(jnp.float32)
+    parts = merge(near_diff, shifted(far_diff, "c", 1))
+    owned = [shifted(parts[k], "x", -k) for k in (1, 2, 3)]
+    total = parts[0].astype(jnp.float32)
     for piece in owned:
         total = total + piece.astype(jnp.float32)
     aside = shifted(total[1].astype(jnp.bfloat16), "yl", 1)
@@ -282,8 +299,8 @@
     )
     mine, other = halve(partial)
     core_sum = mine + shifted(other, "c", 1)
-    got = lax.all_to_all(core_sum, "z", 0, 0, tiled=True)
-    got = lax.all_to_all(spread(got), ("yh", "x", "yl"), 0, 0, tiled=True)
+    got = lax.all_to_all(core_sum, ("yh", "z"), 0, 0, tiled=True)
+    got = lax.all_to_all(spread(got), ("x", "yl"), 0, 0, tiled=True)
     grad_proj = got.astype(jnp.float32).sum(axis=0)
     return grad_hidden, grad_proj
 

time: 120 us -> 119 us (level)
  waiting for transfers between devices: 45.6 us -> 40.7 us
  Pallas kernels: 17.8 us -> 20.2 us
  matrix products: 3.08 us -> 4.29 us
    ppermute x20, waiting for transfers between devices: 26.4 us -> 23.6 us  [shifted(): return lax.ppermute(x, axis, [(i, (i + by) % n) for i in range(n)])]
    all_to_all x2, waiting for transfers between devices: 15.8 us -> 13.7 us  [the longest x1 9.32 us: steps(): got = lax.all_to_all(core_sum, ('yh', 'z'), 0, 0, tiled=True)]
    pallas_call x4, Pallas kernels: 12.4 us -> 13.8 us  [chunk(): pl.pallas_call(functools.partial(chunk_kernel, len(cols), first, last), o...]
    dot_general x1, matrix products: 1 us -> 2.22 us  [steps(): lax.dot_general(hidden_far, far_diff, across_rows, preferred_element_type...]
  transfers between devices with their start and end apart: 26 -> 26, of which waited for: 10 -> 9; matrix products, arithmetic and copies ran while one was open for 5% -> 6% of each run, Pallas kernels for 10% -> 11%
where the time goes in v5:
time: 119 us; the launch traced here: 118 us
  starting transfers between devices  47.3 us (40%)
  waiting for transfers between devices  40.7 us (34%)
  Pallas kernels  20.2 us (17%)
  matrix products  4.29 us (4%)
  other arithmetic  2.56 us (2%)
  between operations  2.12 us (2%)
    ppermute x20, starting transfers between devices, shifted(): return lax.ppermute(x, axis, [(i, (i + by) % n) for i in range(n)])  25 us
    ppermute x20, waiting for transfers between devices, shifted(): return lax.ppermute(x, axis, [(i, (i + by) % n) for i in range(n)])  23.6 us
    pallas_call x4, Pallas kernels, chunk(): pl.pallas_call(functools.partial(chunk_kernel, len(cols), first, last), o...  13.8 us
    all_to_all x1, starting transfers between devices, steps(): got = lax.all_to_all(core_sum, ('yh', 'z'), 0, 0, tiled=True)  10.2 us
    all_to_all x1, waiting for transfers between devices, steps(): got = lax.all_to_all(core_sum, ('yh', 'z'), 0, 0, tiled=True)  9.32 us
    ppermute x4, starting transfers between devices, apart(): return lax.ppermute(x, ('z', 'c'), hops)  7.74 us
    all_to_all x1, starting transfers between devices, steps(): got = lax.all_to_all(spread(got), ('x', 'yl'), 0, 0, tiled=True)  4.4 us
    all_to_all x1, waiting for transfers between devices, steps(): got = lax.all_to_all(spread(got), ('x', 'yl'), 0, 0, tiled=True)  4.38 us
  transfers between devices with their start and end apart: 26, of which 9 were waited for; matrix products, arithmetic and copies ran while one was open for 6% of the time, Pallas kernels for 11%

profile of v5, /device:TPU:32, one launch (start us, length us, event | category | flops | bytes accessed | tf_op | source)
XLA Modules:
  0.0 118.1 jit_solution(17774768518494649744)
XLA Ops:
  0.6 2.4 %message.1 = (bf16[560,128]{1,0:T(8,128)(2,1)}, bf16[816,128]{1,0:T(8,128)(2,1)}) custom-call(bf16[128,768]{1,0:T(8,128)(2,1)} %hidden_ref.1, bf16[768,512]{1,0:T(8,128)(2,1)} %proj_ref.5, bf16[1,128]{1,0:T(2,128)(2,1)} %bitcast.17, bf16[32,128]{1,0:T(8,128)(2,1)} %bitcast.16), custom_call_target="tpu_custom_call" | custom-call | tf_op jit(solution)/shard_map/message/pallas_call | solution.py:183
  6.5 2.0 %collective-permute-start.9 = (bf16[1120,128]{1,0:T(8,128)(2,1)S(1)}, bf16[1120,128]{1,0:T(8,128)(2,1)S(1)}, u32[]{:S(2)}, u32[]{:S(2)}) collective-permute-start(bf16[1120,128]{1,0:T(8,128)(2,1)S(1)} %pad_maximum_fusion), channel_id=1, source_target_pairs={{0,16},{8,120},{16,32},{24,8},{32,48},{40,24},{48,64},{56,40},{64,... | collective-permute-start | bytes 860168 | tf_op jit(solution)/shard_map/ppermute | solution.py:262
  8.5 2.3 %collective-permute-done = bf16[816,128]{1,0:T(8,128)(2,1)S(1)} collective-permute-done((bf16[816,128]{1,0:T(8,128)(2,1)}, bf16[816,128]{1,0:T(8,128)(2,1)S(1)}, u32[]{:S(2)}, u32[]{:S(2)}) %collective-permute-start) | collective-permute-done | bytes 208928 | tf_op jit(solution)/shard_map/ppermute | solution.py:256
  12.4 2.7 %collective-permute-start.2 = (bf16[1632,128]{1,0:T(8,128)(2,1)S(1)}, bf16[1632,128]{1,0:T(8,128)(2,1)S(1)}, u32[]{:S(2)}, u32[]{:S(2)}) collective-permute-start(bf16[1632,128]{1,0:T(8,128)(2,1)S(1)} %constant_dynamic-update-slice_fusion.refs_0_), channel_id=1, source_target_pairs={{0,4},{2,6},{4,0},{6,2},{1,5},{3,7},{5,1},{7,3},{8,12},{10,14},{12... | collective-permute-start | bytes 1253384 | tf_op jit(solution)/shard_map/ppermute | solution.py:256
  16.6 1.9 %collective-permute-start.11 = (bf16[1120,128]{1,0:T(8,128)(2,1)S(1)}, bf16[1120,128]{1,0:T(8,128)(2,1)S(1)}, u32[]{:S(2)}, u32[]{:S(2)}) collective-permute-start(bf16[1120,128]{1,0:T(8,128)(2,1)S(1)} %collective-permute-done.9.refs_7_), channel_id=1, source_target_pairs={{0,16},{8,120},{16,32},{24,8},{32,48},{40,24},{48,64},{56,40},{64,... | collective-permute-start | bytes 860168 | tf_op jit(solution)/shard_map/ppermute | solution.py:262
  18.5 5.2 %collective-permute-done.1.refs_1_ = bf16[1632,128]{1,0:T(8,128)(2,1)S(1)} collective-permute-done((bf16[1632,128]{1,0:T(8,128)(2,1)S(1)}, bf16[1632,128]{1,0:T(8,128)(2,1)S(1)}, u32[]{:S(2)}, u32[]{:S(2)}) %collective-permute-start.1) | collective-permute-done | bytes 417824 | tf_op jit(solution)/shard_map/ppermute | solution.py:256
  23.7 9.6 %collective-permute-done.2.refs_2_ = bf16[1632,128]{1,0:T(8,128)(2,1)S(1)} collective-permute-done((bf16[1632,128]{1,0:T(8,128)(2,1)S(1)}, bf16[1632,128]{1,0:T(8,128)(2,1)S(1)}, u32[]{:S(2)}, u32[]{:S(2)}) %collective-permute-start.2) | collective-permute-done | bytes 417824 | tf_op jit(solution)/shard_map/ppermute | solution.py:256
  33.8 1.9 %collective-permute-start.12 = (bf16[1120,128]{1,0:T(8,128)(2,1)S(1)}, bf16[1120,128]{1,0:T(8,128)(2,1)S(1)}, u32[]{:S(2)}, u32[]{:S(2)}) collective-permute-start(bf16[1120,128]{1,0:T(8,128)(2,1)S(1)} %collective-permute-done.11.refs_8_), channel_id=1, source_target_pairs={{0,16},{8,120},{16,32},{24,8},{32,48},{40,24},{48,64},{56,40},{64,... | collective-permute-start | bytes 860168 | tf_op jit(solution)/shard_map/ppermute | solution.py:262
  37.0 3.4 %collective-permute-done.12.refs_9_ = bf16[1120,128]{1,0:T(8,128)(2,1)S(1)} collective-permute-done((bf16[1120,128]{1,0:T(8,128)(2,1)S(1)}, bf16[1120,128]{1,0:T(8,128)(2,1)S(1)}, u32[]{:S(2)}, u32[]{:S(2)}) %collective-permute-start.12) | collective-permute-done | bytes 286752 | tf_op jit(solution)/shard_map/ppermute | solution.py:262
  40.4 3.2 %collective-permute-start.10 = (bf16[560,128]{1,0:T(8,128)(2,1)}, bf16[560,128]{1,0:T(8,128)(2,1)S(1)}, u32[]{:S(2)}, u32[]{:S(2)}) collective-permute-start(bf16[560,128]{1,0:T(8,128)(2,1)} %get-tuple-element.33.refs_6_), channel_id=1, source_target_pairs={{0,128},{128,0},{1,129},{129,1},{2,130},{130,2},{3,131},{131,3},{4... | collective-permute-start | bytes 430088 | tf_op jit(solution)/shard_map/ppermute | solution.py:256
  45.2 3.2 %collective-permute-start.14 = (bf16[1120,128]{1,0:T(8,128)(2,1)S(1)}, bf16[1120,128]{1,0:T(8,128)(2,1)S(1)}, u32[]{:S(2)}, u32[]{:S(2)}) collective-permute-start(bf16[1120,128]{1,0:T(8,128)(2,1)S(1)} %collective-permute-done.11.refs_8_), channel_id=1, source_target_pairs={{0,128},{128,0},{1,129},{129,1},{2,130},{130,2},{3,131},{131,3},{4... | collective-permute-start | bytes 860168 | tf_op jit(solution)/shard_map/ppermute | solution.py:256
  51.8 3.1 %chunk.4 = (f32[2048,512]{1,0:T(8,128)S(1)}, f32[2048,128]{1,0:T(8,128)S(1)}) custom-call(f32[1]{0:T(128)S(6)} %copy.9.amp_ref, f32[1]{0:T(128)S(6)} %copy.10.lsq_ref, bf16[1024,512]{1,0:T(8,128)(2,1)S(1)} %get-tuple-element.27.refs_0_, bf16[1024,128]{1,0:T(8,128)(2,1)S(1)} %get-tuple-element.28.refs_1_, f32[1024,128]{1,0:T(8,128)S(1)} %get-tuple-element.29.refs_2_, ...), custom_call_target="tpu_custom_call" | custom-call | flops 2684354560 | bytes 4194304 | tf_op jit(solution)/shard_map/chunk/pallas_call | solution.py:146
  54.8 3.2 %chunk.5 = (f32[2048,512]{1,0:T(8,128)S(1)}, f32[2048,128]{1,0:T(8,128)S(1)}) custom-call(f32[1]{0:T(128)S(6)} %copy.9.amp_ref, f32[1]{0:T(128)S(6)} %copy.10.lsq_ref, bf16[1024,512]{1,0:T(8,128)(2,1)S(1)} %get-tuple-element.27.refs_0_, bf16[1024,128]{1,0:T(8,128)(2,1)S(1)} %get-tuple-element.28.refs_1_, f32[1024,128]{1,0:T(8,128)S(1)} %get-tuple-element.29.refs_2_, ...), custom_call_target="tpu_custom_call" | custom-call | flops 2684354560 | bytes 4194304 | tf_op jit(solution)/shard_map/chunk/pallas_call | solution.py:146
  58.0 3.3 %collective-permute-start.17 = (bf16[560,128]{1,0:T(8,128)(2,1)S(1)}, bf16[560,128]{1,0:T(8,128)(2,1)S(1)}, u32[]{:S(2)}, u32[]{:S(2)}) collective-permute-start(bf16[560,128]{1,0:T(8,128)(2,1)S(1)} %collective-permute-done.15.refs_8_), channel_id=1, source_target_pairs={{0,128},{128,0},{1,129},{129,1},{2,130},{130,2},{3,131},{131,3},{4... | collective-permute-start | bytes 430088 | tf_op jit(solution)/shard_map/ppermute | solution.py:256
  62.2 3.1 %chunk.6 = (f32[2048,512]{1,0:T(8,128)S(1)}, f32[2048,128]{1,0:T(8,128)S(1)}) custom-call(f32[1]{0:T(128)S(6)} %copy.9.amp_ref, f32[1]{0:T(128)S(6)} %copy.10.lsq_ref, bf16[1024,512]{1,0:T(8,128)(2,1)S(1)} %get-tuple-element.27.refs_0_, bf16[1024,128]{1,0:T(8,128)(2,1)S(1)} %get-tuple-element.28.refs_1_, f32[1024,128]{1,0:T(8,128)S(1)} %get-tuple-element.29.refs_2_, ...), custom_call_target="tpu_custom_call" | custom-call | flops 2684354560 | bytes 4194304 | tf_op jit(solution)/shard_map/chunk/pallas_call | solution.py:146
  65.4 4.2 %collective-permute-done.17.refs_10_ = bf16[560,128]{1,0:T(8,128)(2,1)S(1)} collective-permute-done((bf16[560,128]{1,0:T(8,128)(2,1)S(1)}, bf16[560,128]{1,0:T(8,128)(2,1)S(1)}, u32[]{:S(2)}, u32[]{:S(2)}) %collective-permute-start.17) | collective-permute-done | bytes 143392 | tf_op jit(solution)/shard_map/ppermute | solution.py:256
  69.6 4.4 %chunk.7 = (bf16[1024,512]{1,0:T(8,128)(2,1)S(1)}, bf16[1024,512]{1,0:T(8,128)(2,1)}) custom-call(f32[1]{0:T(128)S(6)} %copy.9.amp_ref, f32[1]{0:T(128)S(6)} %copy.10.lsq_ref, bf16[1024,512]{1,0:T(8,128)(2,1)S(1)} %get-tuple-element.27.refs_0_, bf16[1024,128]{1,0:T(8,128)(2,1)S(1)} %get-tuple-element.28.refs_1_, f32[1024,128]{1,0:T(8,128)S(1)} %get-tuple-element.29.refs_2_, ...), custom_call_target="tpu_custom_call" | custom-call | flops 2684354560 | bytes 4194304 | tf_op jit(solution)/shard_map/chunk/pallas_call | solution.py:146
  74.0 2.2 %fusion.4 = f32[768,512]{1,0:T(8,128)S(1)} fusion(bf16[1024,768]{1,0:T(8,128)(2,1)S(1)} %get-tuple-element.47, bf16[1024,512]{1,0:T(8,128)(2,1)} %get-tuple-element.41), kind=kOutput, calls=%fused_computation.12 | convolution fusion | flops 805306368 | bytes 4194304 | tf_op jit(solution)/shard_map/dot_general | solution.py:286
  80.1 10.2 %all-to-all-start = ((bf16[16,24,512]{2,1,0:T(8,128)(2,1)}), bf16[16,24,512]{2,1,0:T(8,128)(2,1)S(1)}, u32[]{:S(2)}, u32[]{:S(2)}) async-start(bf16[16,24,512]{2,1,0:T(8,128)(2,1)} %add.23), calls=%async_computation | async-start | bytes 786432 | tf_op jit(solution)/shard_map/all_to_all | solution.py:302
  91.3 2.2 %collective-permute-start.19 = (bf16[2,128,512]{2,1,0:T(8,128)(2,1)}, bf16[2,128,512]{2,1,0:T(8,128)(2,1)S(1)}, u32[]{:S(2)}, u32[]{:S(2)}) collective-permute-start(bf16[2,128,512]{2,1,0:T(8,128)(2,1)} %get-tuple-element.43), channel_id=1, source_target_pairs={{0,6},{2,0},{4,2},{6,4},{1,7},{3,1},{5,3},{7,5},{8,14},{10,8},{12,... | collective-permute-start | bytes 786440 | tf_op jit(solution)/shard_map/ppermute | solution.py:256
  95.3 9.3 %all-to-all-done.got_ref = bf16[16,24,512]{2,1,0:T(8,128)(2,1)S(1)} async-done(((bf16[16,24,512]{2,1,0:T(8,128)(2,1)}), bf16[16,24,512]{2,1,0:T(8,128)(2,1)S(1)}, u32[]{:S(2)}, u32[]{:S(2)}) %all-to-all-start) | async-done | bytes 393248 | tf_op jit(solution)/shard_map/all_to_all | solution.py:302
  105.4 4.4 %all-to-all-start.1 = ((bf16[8,24,512]{2,1,0:T(8,128)(2,1)}), bf16[8,24,512]{2,1,0:T(8,128)(2,1)S(1)}, u32[]{:S(2)}, u32[]{:S(2)}) async-start(bf16[8,24,512]{2,1,0:T(8,128)(2,1)} %spread.1), calls=%async_computation.1 | async-start | bytes 393216 | tf_op jit(solution)/shard_map/all_to_all | solution.py:303
  110.0 2.1 %collective-permute-start.22 = (bf16[128,512]{1,0:T(8,128)(2,1)S(1)}, bf16[128,512]{1,0:T(8,128)(2,1)S(1)}, u32[]{:S(2)}, u32[]{:S(2)}) collective-permute-start(bf16[128,512]{1,0:T(8,128)(2,1)S(1)} %fusion.3), channel_id=1, source_target_pairs={{0,1},{1,0},{2,3},{3,2},{4,5},{5,4},{6,7},{7,6},{8,9},{9,8},{10,11... | collective-permute-start | bytes 393224 | tf_op jit(solution)/shard_map/ppermute | solution.py:256
  112.1 4.4 %all-to-all-done.1 = bf16[8,24,512]{2,1,0:T(8,128)(2,1)S(1)} async-done(((bf16[8,24,512]{2,1,0:T(8,128)(2,1)}), bf16[8,24,512]{2,1,0:T(8,128)(2,1)S(1)}, u32[]{:S(2)}, u32[]{:S(2)}) %all-to-all-start.1) | async-done | bytes 196640 | tf_op jit(solution)/shard_map/all_to_all | solution.py:303
  (53 shorter events, 22.2 us)
Async XLA Ops:
  3.0 7.8 %collective-permute-start = (bf16[816,128]{1,0:T(8,128)(2,1)}, bf16[816,128]{1,0:T(8,128)(2,1)S(1)}, u32[]{:S(2)}, u32[]{:S(2)}) collective-permute-start(bf16[816,128]{1,0:T(8,128)(2,1)} %get-tuple-element.26), channel_id=1, source_target_pairs={{0,1},{1,0},{2,3},{3,2},{4,5},{5,4},{6,7},{7,6},{8,9},{9,8},{10,11... | collective-permute-start | bytes 626696 | tf_op jit(solution)/shard_map/ppermute | solution.py:256
  6.5 10.1 %collective-permute-start.9 = (bf16[1120,128]{1,0:T(8,128)(2,1)S(1)}, bf16[1120,128]{1,0:T(8,128)(2,1)S(1)}, u32[]{:S(2)}, u32[]{:S(2)}) collective-permute-start(bf16[1120,128]{1,0:T(8,128)(2,1)S(1)} %pad_maximum_fusion), channel_id=1, source_target_pairs={{0,16},{8,120},{16,32},{24,8},{32,48},{40,24},{48,64},{56,40},{64,... | collective-permute-start | bytes 860168 | tf_op jit(solution)/shard_map/ppermute | solution.py:262
  10.9 12.8 %collective-permute-start.1 = (bf16[1632,128]{1,0:T(8,128)(2,1)S(1)}, bf16[1632,128]{1,0:T(8,128)(2,1)S(1)}, u32[]{:S(2)}, u32[]{:S(2)}) collective-permute-start(bf16[1632,128]{1,0:T(8,128)(2,1)S(1)} %constant_dynamic-update-slice_fusion.refs_0_), channel_id=1, source_target_pairs={{0,2},{2,4},{4,6},{6,0},{1,3},{3,5},{5,7},{7,1},{8,10},{10,12},{12... | collective-permute-start | bytes 1253384 | tf_op jit(solution)/shard_map/ppermute | solution.py:256
  12.4 20.9 %collective-permute-start.2 = (bf16[1632,128]{1,0:T(8,128)(2,1)S(1)}, bf16[1632,128]{1,0:T(8,128)(2,1)S(1)}, u32[]{:S(2)}, u32[]{:S(2)}) collective-permute-start(bf16[1632,128]{1,0:T(8,128)(2,1)S(1)} %constant_dynamic-update-slice_fusion.refs_0_), channel_id=1, source_target_pairs={{0,4},{2,6},{4,0},{6,2},{1,5},{3,7},{5,1},{7,3},{8,12},{10,14},{12... | collective-permute-start | bytes 1253384 | tf_op jit(solution)/shard_map/ppermute | solution.py:256
  15.2 18.1 %collective-permute-start.3 = (bf16[1632,128]{1,0:T(8,128)(2,1)S(1)}, bf16[1632,128]{1,0:T(8,128)(2,1)S(1)}, u32[]{:S(2)}, u32[]{:S(2)}) collective-permute-start(bf16[1632,128]{1,0:T(8,128)(2,1)S(1)} %constant_dynamic-update-slice_fusion.refs_0_), channel_id=1, source_target_pairs={{0,6},{2,0},{4,2},{6,4},{1,7},{3,1},{5,3},{7,5},{8,14},{10,8},{12,... | collective-permute-start | bytes 1253384 | tf_op jit(solution)/shard_map/ppermute | solution.py:256
  16.6 17.2 %collective-permute-start.11 = (bf16[1120,128]{1,0:T(8,128)(2,1)S(1)}, bf16[1120,128]{1,0:T(8,128)(2,1)S(1)}, u32[]{:S(2)}, u32[]{:S(2)}) collective-permute-start(bf16[1120,128]{1,0:T(8,128)(2,1)S(1)} %collective-permute-done.9.refs_7_), channel_id=1, source_target_pairs={{0,16},{8,120},{16,32},{24,8},{32,48},{40,24},{48,64},{56,40},{64,... | collective-permute-start | bytes 860168 | tf_op jit(solution)/shard_map/ppermute | solution.py:262
  18.5 26.3 %collective-permute-start.4 = (bf16[1632,128]{1,0:T(8,128)(2,1)S(1)}, bf16[1632,128]{1,0:T(8,128)(2,1)S(1)}, u32[]{:S(2)}, u32[]{:S(2)}) collective-permute-start(bf16[1632,128]{1,0:T(8,128)(2,1)S(1)} %constant_dynamic-update-slice_fusion.refs_0_), channel_id=1, source_target_pairs={{0,8},{8,0},{1,9},{9,1},{2,10},{10,2},{3,11},{11,3},{4,12},{12,4},... | collective-permute-start | bytes 1253384 | tf_op jit(solution)/shard_map/ppermute | solution.py:256
  23.7 21.5 %collective-permute-start.5 = (bf16[1632,128]{1,0:T(8,128)(2,1)S(1)}, bf16[1632,128]{1,0:T(8,128)(2,1)S(1)}, u32[]{:S(2)}, u32[]{:S(2)}) collective-permute-start(bf16[1632,128]{1,0:T(8,128)(2,1)S(1)} %collective-permute-done.1.refs_1_), channel_id=1, source_target_pairs={{0,8},{8,0},{1,9},{9,1},{2,10},{10,2},{3,11},{11,3},{4,12},{12,4},... | collective-permute-start | bytes 1253384 | tf_op jit(solution)/shard_map/ppermute | solution.py:256
  33.3 15.1 %collective-permute-start.6 = (bf16[1632,128]{1,0:T(8,128)(2,1)S(1)}, bf16[1632,128]{1,0:T(8,128)(2,1)S(1)}, u32[]{:S(2)}, u32[]{:S(2)}) collective-permute-start(bf16[1632,128]{1,0:T(8,128)(2,1)S(1)} %collective-permute-done.2.refs_2_), channel_id=1, source_target_pairs={{0,8},{8,0},{1,9},{9,1},{2,10},{10,2},{3,11},{11,3},{4,12},{12,4},... | collective-permute-start | bytes 1253384 | tf_op jit(solution)/shard_map/ppermute | solution.py:256
  33.3 17.0 %collective-permute-start.7 = (bf16[1632,128]{1,0:T(8,128)(2,1)S(1)}, bf16[1632,128]{1,0:T(8,128)(2,1)S(1)}, u32[]{:S(2)}, u32[]{:S(2)}) collective-permute-start(bf16[1632,128]{1,0:T(8,128)(2,1)S(1)} %collective-permute-done.3.refs_3_), channel_id=1, source_target_pairs={{0,8},{8,0},{1,9},{9,1},{2,10},{10,2},{3,11},{11,3},{4,12},{12,4},... | collective-permute-start | bytes 1253384 | tf_op jit(solution)/shard_map/ppermute | solution.py:256
  33.8 6.6 %collective-permute-start.12 = (bf16[1120,128]{1,0:T(8,128)(2,1)S(1)}, bf16[1120,128]{1,0:T(8,128)(2,1)S(1)}, u32[]{:S(2)}, u32[]{:S(2)}) collective-permute-start(bf16[1120,128]{1,0:T(8,128)(2,1)S(1)} %collective-permute-done.11.refs_8_), channel_id=1, source_target_pairs={{0,16},{8,120},{16,32},{24,8},{32,48},{40,24},{48,64},{56,40},{64,... | collective-permute-start | bytes 860168 | tf_op jit(solution)/shard_map/ppermute | solution.py:262
  40.4 11.3 %collective-permute-start.10 = (bf16[560,128]{1,0:T(8,128)(2,1)}, bf16[560,128]{1,0:T(8,128)(2,1)S(1)}, u32[]{:S(2)}, u32[]{:S(2)}) collective-permute-start(bf16[560,128]{1,0:T(8,128)(2,1)} %get-tuple-element.33.refs_6_), channel_id=1, source_target_pairs={{0,128},{128,0},{1,129},{129,1},{2,130},{130,2},{3,131},{131,3},{4... | collective-permute-start | bytes 430088 | tf_op jit(solution)/shard_map/ppermute | solution.py:256
  44.8 16.5 %collective-permute-start.13 = (bf16[1120,128]{1,0:T(8,128)(2,1)S(1)}, bf16[1120,128]{1,0:T(8,128)(2,1)S(1)}, u32[]{:S(2)}, u32[]{:S(2)}) collective-permute-start(bf16[1120,128]{1,0:T(8,128)(2,1)S(1)} %collective-permute-done.9.refs_7_), channel_id=1, source_target_pairs={{0,128},{128,0},{1,129},{129,1},{2,130},{130,2},{3,131},{131,3},{4... | collective-permute-start | bytes 860168 | tf_op jit(solution)/shard_map/ppermute | solution.py:256
  45.2 17.0 %collective-permute-start.14 = (bf16[1120,128]{1,0:T(8,128)(2,1)S(1)}, bf16[1120,128]{1,0:T(8,128)(2,1)S(1)}, u32[]{:S(2)}, u32[]{:S(2)}) collective-permute-start(bf16[1120,128]{1,0:T(8,128)(2,1)S(1)} %collective-permute-done.11.refs_8_), channel_id=1, source_target_pairs={{0,128},{128,0},{1,129},{129,1},{2,130},{130,2},{3,131},{131,3},{4... | collective-permute-start | bytes 860168 | tf_op jit(solution)/shard_map/ppermute | solution.py:256
  48.4 9.6 %collective-permute-start.15 = (bf16[560,128]{1,0:T(8,128)(2,1)S(1)}, bf16[560,128]{1,0:T(8,128)(2,1)S(1)}, u32[]{:S(2)}, u32[]{:S(2)}) collective-permute-start(bf16[560,128]{1,0:T(8,128)(2,1)S(1)} %slice.13), channel_id=1, source_target_pairs={{0,16},{8,120},{16,32},{24,8},{32,48},{40,24},{48,64},{56,40},{64,... | collective-permute-start | bytes 430088 | tf_op jit(solution)/shard_map/ppermute | solution.py:262
  50.3 19.3 %collective-permute-start.16 = (bf16[1120,128]{1,0:T(8,128)(2,1)S(1)}, bf16[1120,128]{1,0:T(8,128)(2,1)S(1)}, u32[]{:S(2)}, u32[]{:S(2)}) collective-permute-start(bf16[1120,128]{1,0:T(8,128)(2,1)S(1)} %collective-permute-done.12.refs_9_), channel_id=1, source_target_pairs={{0,128},{128,0},{1,129},{129,1},{2,130},{130,2},{3,131},{131,3},{4... | collective-permute-start | bytes 860168 | tf_op jit(solution)/shard_map/ppermute | solution.py:256
  58.0 11.6 %collective-permute-start.17 = (bf16[560,128]{1,0:T(8,128)(2,1)S(1)}, bf16[560,128]{1,0:T(8,128)(2,1)S(1)}, u32[]{:S(2)}, u32[]{:S(2)}) collective-permute-start(bf16[560,128]{1,0:T(8,128)(2,1)S(1)} %collective-permute-done.15.refs_8_), channel_id=1, source_target_pairs={{0,128},{128,0},{1,129},{129,1},{2,130},{130,2},{3,131},{131,3},{4... | collective-permute-start | bytes 430088 | tf_op jit(solution)/shard_map/ppermute | solution.py:256
  74.0 16.3 %collective-permute-start.18 = (bf16[1024,512]{1,0:T(8,128)(2,1)}, bf16[1024,512]{1,0:T(8,128)(2,1)S(1)}, u32[]{:S(2)}, u32[]{:S(2)}) collective-permute-start(bf16[1024,512]{1,0:T(8,128)(2,1)} %get-tuple-element.41), channel_id=1, source_target_pairs={{0,8},{8,0},{1,9},{9,1},{2,10},{10,2},{3,11},{11,3},{4,12},{12,4},... | collective-permute-start | bytes 3145736 | tf_op jit(solution)/shard_map/ppermute | solution.py:256
  80.1 24.5 %all-to-all-start = ((bf16[16,24,512]{2,1,0:T(8,128)(2,1)}), bf16[16,24,512]{2,1,0:T(8,128)(2,1)S(1)}, u32[]{:S(2)}, u32[]{:S(2)}) async-start(bf16[16,24,512]{2,1,0:T(8,128)(2,1)} %add.23), calls=%async_computation | async-start | bytes 786432 | tf_op jit(solution)/shard_map/all_to_all | solution.py:302
  91.3 18.5 %collective-permute-start.19 = (bf16[2,128,512]{2,1,0:T(8,128)(2,1)}, bf16[2,128,512]{2,1,0:T(8,128)(2,1)S(1)}, u32[]{:S(2)}, u32[]{:S(2)}) collective-permute-start(bf16[2,128,512]{2,1,0:T(8,128)(2,1)} %get-tuple-element.43), channel_id=1, source_target_pairs={{0,6},{2,0},{4,2},{6,4},{1,7},{3,1},{5,3},{7,5},{8,14},{10,8},{12,... | collective-permute-start | bytes 786440 | tf_op jit(solution)/shard_map/ppermute | solution.py:256
  93.5 16.3 %collective-permute-start.20 = (bf16[2,128,512]{2,1,0:T(8,128)(2,1)}, bf16[2,128,512]{2,1,0:T(8,128)(2,1)S(1)}, u32[]{:S(2)}, u32[]{:S(2)}) collective-permute-start(bf16[2,128,512]{2,1,0:T(8,128)(2,1)} %get-tuple-element.44), channel_id=1, source_target_pairs={{0,4},{2,6},{4,0},{6,2},{1,5},{3,7},{5,1},{7,3},{8,12},{10,14},{12... | collective-permute-start | bytes 786440 | tf_op jit(solution)/shard_map/ppermute | solution.py:256
  94.6 15.2 %collective-permute-start.21 = (bf16[2,128,512]{2,1,0:T(8,128)(2,1)}, bf16[2,128,512]{2,1,0:T(8,128)(2,1)S(1)}, u32[]{:S(2)}, u32[]{:S(2)}) collective-permute-start(bf16[2,128,512]{2,1,0:T(8,128)(2,1)} %get-tuple-element.45), channel_id=1, source_target_pairs={{0,2},{2,4},{4,6},{6,0},{1,3},{3,5},{5,7},{7,1},{8,10},{10,12},{12... | collective-permute-start | bytes 786440 | tf_op jit(solution)/shard_map/ppermute | solution.py:256
  105.4 11.1 %all-to-all-start.1 = ((bf16[8,24,512]{2,1,0:T(8,128)(2,1)}), bf16[8,24,512]{2,1,0:T(8,128)(2,1)S(1)}, u32[]{:S(2)}, u32[]{:S(2)}) async-start(bf16[8,24,512]{2,1,0:T(8,128)(2,1)} %spread.1), calls=%async_computation.1 | async-start | bytes 393216 | tf_op jit(solution)/shard_map/all_to_all | solution.py:303
  110.0 7.1 %collective-permute-start.22 = (bf16[128,512]{1,0:T(8,128)(2,1)S(1)}, bf16[128,512]{1,0:T(8,128)(2,1)S(1)}, u32[]{:S(2)}, u32[]{:S(2)}) collective-permute-start(bf16[128,512]{1,0:T(8,128)(2,1)S(1)} %fusion.3), channel_id=1, source_target_pairs={{0,1},{1,0},{2,3},{3,2},{4,5},{5,4},{6,7},{7,6},{8,9},{9,8},{10,11... | collective-permute-start | bytes 393224 | tf_op jit(solution)/shard_map/ppermute | solution.py:256
  (4 other events, 54.6 us)
